TPU v7x, 128 devices: a whole 4x4x4 slice. The times are simulated.
128 devices in a mesh: row: 16 (over x, z), col: 8 (over y, core).
Axes of the slice: x: 4, y: 4, z: 4, core: 2. Of those that a mesh axis runs over, the one named last changes fastest.
Arguments:
- coeffs: bfloat16 [4096, 128, 128], P(('row', 'col')), as said below
- tiles: int32 [4096, 1], replicated, may hold values from 0 to 7; in each aligned block of 32 rows (0 to 31, 32 to 63, ...) at most 5 rows name the same one
- primal: bfloat16 [1024, 1024], replicated, as said below
- dual_inverse: bfloat16 [1024, 1024], replicated, as said below
Outputs:
- schur: float32 [4096, 4096], P('row', 'col')
Inputs may be any that keep to these rules, and one draw needn't show every extreme that they name: `tiles`: within each aligned block of 32 constraints (the constraints of one device) no tile is named more than 5 times, a bound that some block reaches. Each coeffs[i] is symmetric. `primal`: Symmetric. `dual_inverse`: Symmetric.
All inputs are finite; a program needn't handle non-finite values.
Results may differ from a plain program's by a relative error of at most 0.0022.
Values may be sent and summed in bfloat16 or wider, within the bound.
No kernel may reach another device: no remote copies, remote signals or barrier semaphores. Data moves between devices by JAX's collectives and lax.ppermute only.
A program may use at most 128 MiB of HBM per device.

v0:
```python
import functools

import jax
import jax.numpy as jnp
import numpy as np
from jax import lax
from jax.experimental import pallas as pl
from jax.experimental.pallas import tpu as pltpu
from jax.sharding import Mesh
from jax.sharding import PartitionSpec as P


MOST = 5
K = 128
H = 64
FOLD = H + 1
WIDTH = FOLD * K
UNIT = 8 * MOST
PIECE = MOST * H + 16
LINE = ("y", "core")
PLANE = ("x", "z")
ALL = ("x", "z", "y", "core")
NT = (((1,), (1,)), ((), ()))
VMEM = pl.BlockSpec(memory_space=pltpu.VMEM)
SMEM = pl.BlockSpec(memory_space=pltpu.SMEM)
ANY = pl.BlockSpec(memory_space=pl.ANY)

FIRST = (((1, 0), (0, 0)), ((0, 3), (0, 0)), ((3, 1), (0, 0)))
SECOND = (((2, 1), (3, 1)), ((3, 2), (3, 1)), ((2, 0), (1, 0)), ((0, 2), (0, 3)), ((3, 3), (0, 3)))
THIRD = (((2, 2), (2, 1)),)
EARLY = ((0, 0),) + tuple(d for d, _ in FIRST + SECOND)
LATE = tuple(d for d, _ in THIRD)
FORMED = EARLY + LATE


def negated(d):
    return ((-d[0]) % 4, (-d[1]) % 4)


TURNED = tuple(negated(d) for d in FORMED if negated(d) not in FORMED)


def plane_shift(x, shift):
    pairs = []
    for a in range(4):
        for b in range(4):
            pairs.append((a * 4 + b, (a + shift[0]) % 4 * 4 + (b + shift[1]) % 4))
    return lax.ppermute(x, PLANE, pairs)


def line_shift(x, shift, swap):
    pairs = []
    for a in range(4):
        for b in range(2):
            pairs.append((a * 2 + b, (a + shift) % 4 * 2 + (b + swap) % 2))
    return lax.ppermute(x, LINE, pairs)


def folded(square, half_diagonal):
    top, bottom = square[:H], square[H:]
    row = lax.broadcasted_iota(jnp.int32, (H, K), 0)
    lane = lax.broadcasted_iota(jnp.int32, (H, K), 1)
    turned = pltpu.roll(bottom, H, 1)
    kept = jnp.where(jnp.logical_and(lane < H, row > lane), turned, top)
    last = jnp.sum(jnp.where(lane == row + H, bottom, 0.0), axis=0, keepdims=True)
    if half_diagonal:
        kept = kept * jnp.where(row == lane, 0.5, 1.0)
        last = last * 0.5
    return kept, last


def fold_kernel(where, tiles, own_ref, *refs):
    outs, held, lasts, counts = refs[:8], refs[8], refs[9], refs[10]
    held[...] = jnp.zeros(held.shape, held.dtype)
    lasts[...] = jnp.zeros(lasts.shape, lasts.dtype)
    for k in range(8):
        counts[k] = 0
    y, core = where[1], where[2]
    mine = where[0] * 256 + y * 64 + core * 32

    def four(n, carry):
        for m in range(8):
            i = n * 8 + m
            t = tiles[mine + i]
            order = counts[t]
            counts[t] = order + 1
            goal = lax.rem(t // 2 - y + 4, 4) * 2 + lax.rem(t + core, 2)
            kept, last = folded(own_ref[i].astype(jnp.float32), False)
            row = pl.multiple_of(goal * PIECE + order * H, 16)
            held[pl.ds(row, H), :] = kept.astype(held.dtype)
            lasts[pl.ds(goal * 16 + order, 1), :] = last
        return carry

    lax.fori_loop(0, 4, four, 0)
    for k in range(8):
        outs[k][: MOST * H, :] = held[k * PIECE : k * PIECE + MOST * H, :]
        outs[k][MOST * H :, :] = lasts[k * 16 : (k + 1) * 16, :].astype(held.dtype)


def fold_call(where, tiles, own):
    return pl.pallas_call(
        fold_kernel,
        out_shape=[jax.ShapeDtypeStruct((PIECE, K), jnp.bfloat16)] * 8,
        in_specs=[SMEM, SMEM, VMEM],
        out_specs=[VMEM] * 8,
        scratch_shapes=[
            pltpu.VMEM((8 * PIECE, K), jnp.bfloat16),
            pltpu.VMEM((8 * 16, K), jnp.float32),
            pltpu.SMEM((8,), jnp.int32),
        ],
        name="fold",
    )(where, tiles, own)


def unit_kernel(*refs):
    pieces, out, turn = refs[:8], refs[8], refs[9]
    for k in range(8):
        for s in range(MOST):
            slot = k * MOST + s
            turn[pl.ds(slot, H, stride=UNIT), :] = pieces[k][s * H : (s + 1) * H, :].astype(jnp.float32)
        first = H * UNIT + k * MOST
        turn[first : first + MOST, :] = pieces[k][MOST * H :, :].astype(jnp.float32)[:MOST]
    for a in range(FOLD):
        out[:, a * K : (a + 1) * K] = turn[a * UNIT : (a + 1) * UNIT, :].astype(out.dtype)


def unit_call(pieces):
    return pl.pallas_call(
        unit_kernel,
        out_shape=jax.ShapeDtypeStruct((UNIT, WIDTH), jnp.bfloat16),
        in_specs=[VMEM] * 8,
        out_specs=VMEM,
        scratch_shapes=[pltpu.VMEM((FOLD * UNIT, K), jnp.float32)],
        name="unit",
    )(*pieces)


def prepare_kernel(where, primal, dual, right, left, sems):
    at = pl.multiple_of((where[1] * 2 + where[2]) * K, K)
    copies = []
    for t in range(8):
        rows, here = pl.ds(t * K, K), pl.ds(at, K)
        copies.append((dual.at[rows, here], right.at[t, :, pl.ds(0, K)]))
        copies.append((primal.at[rows, here], right.at[t, :, pl.ds(K, K)]))
        copies.append((primal.at[here, rows], left.at[t, :, pl.ds(0, K)]))
        copies.append((dual.at[here, rows], left.at[t, :, pl.ds(K, K)]))
    started = [pltpu.make_async_copy(a, b, sems.at[n]) for n, (a, b) in enumerate(copies)]
    for c in started:
        c.start()
    for c in started:
        c.wait()


def prepare_call(where, primal, dual):
    return pl.pallas_call(
        prepare_kernel,
        out_shape=[jax.ShapeDtypeStruct((8, K, 2 * K), jnp.bfloat16)] * 2,
        in_specs=[SMEM, ANY, ANY],
        out_specs=[VMEM] * 2,
        scratch_shapes=[pltpu.SemaphoreType.DMA((32,))],
        name="prepare",
    )(where, primal, dual)


STRIDE = 40


def reduce_kernel(plan, chained, where, tiles, right, left, *refs):
    n = len(plan)
    blocks = refs[:n]
    rest = refs[n + (1 if chained else 0) :]
    out, held, turn, stage, sems = rest
    line, y, core = where[0], where[1], where[2]
    loads, spot = [], 0
    for b, (dy, dcore, first, size) in enumerate(plan):
        copy = pltpu.make_async_copy(blocks[b], held.at[pl.ds(spot, size)], sems.at[b])
        copy.start()
        loads.append((copy, spot))
        spot += size
    stores = []
    for b, (dy, dcore, first, size) in enumerate(plan):
        copy, spot = loads[b]
        row = lax.rem(y + dy, 4) * 64 + lax.rem(core + dcore, 2) * 32 + first
        copy.wait()
        for m in range(size):
            t = tiles[line * 256 + row + m]
            wide = jnp.dot(held[spot + m], right[t], preferred_element_type=jnp.float32)
            wide = wide.astype(jnp.bfloat16)
            tall = jnp.concatenate([wide[:, :K], wide[:, K:]], axis=0)
            both = jnp.dot(left[t], tall, preferred_element_type=jnp.float32)
            kept, last = folded(both, True)
            turn[pl.ds(m, H, stride=STRIDE), :] = kept
            turn[H * STRIDE + m : H * STRIDE + m + 1, :] = last
        for a in range(FOLD):
            rows = turn[a * STRIDE : a * STRIDE + size, :].astype(stage.dtype)
            stage[spot : spot + size, a * K : (a + 1) * K] = rows
        goal = out.at[pl.ds(pl.multiple_of(row, 16), size)]
        store = pltpu.make_async_copy(stage.at[pl.ds(spot, size)], goal, sems.at[n + b])
        store.start()
        stores.append(store)
    for store in stores:
        store.wait()


def reduce_call(plan, where, tiles, blocks, right, left, total):
    n = len(blocks)
    args = [where, tiles, right, left, *blocks]
    specs = [SMEM, SMEM, VMEM, VMEM] + [ANY] * n
    aliases = {}
    if total is not None:
        aliases = {len(args): 0}
        args.append(total)
        specs.append(ANY)
    return pl.pallas_call(
        functools.partial(reduce_kernel, plan, total is not None),
        out_shape=jax.ShapeDtypeStruct((256, WIDTH), jnp.bfloat16),
        in_specs=specs,
        out_specs=ANY,
        scratch_shapes=[
            pltpu.VMEM((64, K, K), jnp.bfloat16),
            pltpu.VMEM((FOLD * STRIDE, K), jnp.float32),
            pltpu.VMEM((64, WIDTH), jnp.bfloat16),
            pltpu.SemaphoreType.DMA((2 * n,)),
        ],
        input_output_aliases=aliases,
        name="reduced",
    )(*args)


def contract_kernel(n, *refs):
    units, total, outs = refs[:n], refs[n], refs[n + 1 :]
    rows = jnp.concatenate([u[...] for u in units], axis=0)
    values = lax.dot_general(rows, total[...], NT, preferred_element_type=jnp.float32)
    for m in range(n):
        outs[m][...] = values[m * UNIT : (m + 1) * UNIT]


def contract_call(units, total):
    n = len(units)
    return pl.pallas_call(
        functools.partial(contract_kernel, n),
        out_shape=[jax.ShapeDtypeStruct((UNIT, 256), jnp.float32)] * n,
        in_specs=[VMEM] * (n + 1),
        out_specs=[VMEM] * n,
        name="contract",
    )(*units, total)


def gather_kernel(known, late, where, *refs):
    n, m = len(known), len(late)
    values, units, total, out = refs[:n], refs[n : n + m], refs[n + m], refs[n + m + 1]
    x, z = where[0] // 4, lax.rem(where[0], 4)

    def group(d):
        return lax.rem(x - d[0] + 4, 4) * 4 + lax.rem(z - d[1] + 4, 4)

    for d, ref in zip(known, values):
        out[group(d)] = ref[...]
    rows = jnp.concatenate([u[...] for u in units], axis=0) if m > 1 else units[0][...]
    formed = lax.dot_general(rows, total[...], NT, preferred_element_type=jnp.float32)
    for k, d in enumerate(late):
        out[group(d)] = formed[k * UNIT : (k + 1) * UNIT]


def gather_call(where, known, late, total):
    return pl.pallas_call(
        functools.partial(gather_kernel, tuple(known), tuple(late)),
        out_shape=jax.ShapeDtypeStruct((16, UNIT, 256), jnp.float32),
        in_specs=[SMEM] + [VMEM] * (len(known) + len(late) + 1),
        out_specs=VMEM,
        name="gather",
    )(where, *known.values(), *late.values(), total)


def final_kernel(flags, places_ref, landed, out):
    for g in range(2):
        places = places_ref[:, g : g + 1]
        slots = lax.broadcasted_iota(jnp.int32, (256, 8 * UNIT), 1)
        hot = (slots == places).astype(jnp.bfloat16)
        values = jnp.concatenate([landed[c, g] for c in range(8)], axis=0)
        high = values.astype(jnp.bfloat16)
        rest = values - high.astype(jnp.float32)
        low = rest.astype(jnp.bfloat16)
        picked = jnp.dot(hot, high, preferred_element_type=jnp.float32)
        picked = picked + jnp.dot(hot, low, preferred_element_type=jnp.float32)
        turned = flags[g] > 0

        @pl.when(turned)
        def _():
            out[:, g * 256 : (g + 1) * 256] = picked

        @pl.when(jnp.logical_not(turned))
        def _():
            out[:, g * 256 : (g + 1) * 256] = picked.T


def final_call(flags, places, landed):
    return pl.pallas_call(
        final_kernel,
        out_shape=jax.ShapeDtypeStruct((256, 512), jnp.float32),
        in_specs=[SMEM, VMEM, VMEM],
        out_specs=VMEM,
        name="final",
    )(flags, places, landed)


def steps(coeffs, tiles, primal, dual_inverse):
    x, z = lax.axis_index("x"), lax.axis_index("z")
    y, core = lax.axis_index("y"), lax.axis_index("core")
    line = x * 4 + z
    tile = y * 2 + core
    where = jnp.stack([line, y, core]).astype(jnp.int32)
    flat = tiles.reshape(4096)

    pieces = fold_call(where, flat, coeffs)
    routed = [pieces[0]]
    for k in range(1, 8):
        routed.append(line_shift(pieces[k], k // 2, k % 2))
    units = {(0, 0): unit_call(routed)}
    right, left = prepare_call(where, primal, dual_inverse)

    other = line_shift(coeffs, 0, 1)
    down = line_shift(coeffs, 1, 0)
    up = line_shift(coeffs, 3, 0)
    down_other = line_shift(down, 0, 1)
    up_other = line_shift(up, 0, 1)
    low = line_shift(down[:16], 1, 0)
    high = line_shift(up[16:], 3, 0)
    low_other = line_shift(low, 0, 1)
    high_other = line_shift(high, 0, 1)

    def formed(plan, blocks, total):
        return reduce_call(plan, where, flat, blocks, right, left, total)

    total = formed(((0, 0, 0, 32), (0, 1, 0, 32)), [coeffs, other], None)
    total = formed(((3, 0, 0, 32), (3, 1, 0, 32)), [down, down_other], total)
    total = formed(((1, 0, 0, 32), (1, 1, 0, 32)), [up, up_other], total)
    plan = ((2, 0, 0, 16), (2, 0, 16, 16), (2, 1, 0, 16), (2, 1, 16, 16))
    total = formed(plan, [low, high, low_other, high_other], total)

    for d, parent in FIRST + SECOND + THIRD:
        shift = ((d[0] - parent[0]) % 4, (d[1] - parent[1]) % 4)
        units[d] = plane_shift(units[parent], shift)

    values = contract_call([units[d] for d in EARLY], total)
    known = dict(zip(EARLY, values))
    for d in EARLY:
        if negated(d) in TURNED:
            known[negated(d)] = plane_shift(known[d], negated(d))
    ordered = gather_call(where, known, {d: units[d] for d in LATE}, total)
    landed = lax.all_to_all(ordered.reshape(8, 2, UNIT, 256), LINE, 0, 0, tiled=True)

    ids = tiles.reshape(128, 32)
    earlier = jnp.tril(jnp.ones((32, 32), jnp.int32), -1)
    same = (ids[:, :, None] == ids[:, None, :]).astype(jnp.int32)
    ordinal = jnp.sum(same * earlier[None], axis=2)
    block = jnp.arange(128, dtype=jnp.int32)[:, None] % 8
    step = (ids // 2 - block // 2) % 4
    swapped = (ids + block) % 2
    place = ids * UNIT + step * 2 * MOST + swapped * MOST + ordinal
    place = place.reshape(16, 256)
    flips = np.array([0 if (a, b) in FORMED else 1 for a in range(4) for b in range(4)], np.int32)
    targets = tile * 2 + jnp.arange(2, dtype=jnp.int32)
    apart = (x - targets // 4) % 4 * 4 + (z - targets % 4) % 4
    flags = jnp.take(jnp.asarray(flips), apart)
    row_place = lax.dynamic_slice_in_dim(place, line, 1, 0)
    col_place = lax.dynamic_slice_in_dim(place, tile * 2, 2, 0)
    places = jnp.where(flags[:, None] > 0, row_place, col_place)
    return final_call(flags, places.T, landed)


def solution(mesh):
    finer = Mesh(mesh.devices.reshape(4, 4, 4, 2), ALL)
    in_specs = (P(ALL, None, None), P(), P(), P())
    out_specs = P(PLANE, LINE)
    return jax.shard_map(
        steps, mesh=finer, in_specs=in_specs, out_specs=out_specs, check_vma=False
    )
```

profile of v0, /device:TPU:1, one launch (start us, length us, event | category | flops | bytes accessed | tf_op | source)
XLA Modules:
  0.0 169.8 jit_solution(8950248525507474085)
XLA Ops:
  0.0 2.1 %collective-permute-start.15 = (bf16[32,128,128]{2,1,0:T(8,128)(2,1)}, bf16[32,128,128]{2,1,0:T(8,128)(2,1)S(1)}, u32[]{:S(2)}, u32[]{:S(2)}) collective-permute-start(bf16[32,128,128]{2,1,0:T(8,128)(2,1)} %refs_0_.1), channel_id=1, source_target_pairs={{0,2},{1,3},{2,4},{3,5},{4,6},{5,7},{6,0},{7,1},{8,10},{9,11},{10,... | collective-permute-start | bytes 3145736 | tf_op jit(solution)/shard_map/ppermute | solution.py:56
  2.1 1.5 collective-permute-start.17
  4.2 2.7 %fold.1 = (bf16[336,128]{1,0:T(8,128)(2,1)}, bf16[336,128]{1,0:T(8,128)(2,1)}, bf16[336,128]{1,0:T(8,128)(2,1)}, bf16[336,128]{1,0:T(8,128)(2,1)}, bf16[336,128]...) custom-call(s32[3]{0:T(128)} %pad_add_fusion.where, ...), custom_call_target="tpu_custom_call" | custom-call | tf_op jit(solution)/shard_map/fold/pallas_call | solution.py:101
  6.9 1.0 collective-permute-start
  8.1 1.5 collective-permute-start.2
  9.6 2.4 %collective-permute-start.3 = (bf16[336,128]{1,0:T(8,128)(2,1)}, bf16[336,128]{1,0:T(8,128)(2,1)S(1)}, u32[]{:S(2)}, u32[]{:S(2)}) collective-permute-start(bf16[336,128]{1,0:T(8,128)(2,1)} %get-tuple-element.28), channel_id=1, source_target_pairs={{0,4},{1,5},{2,6},{3,7},{4,0},{5,1},{6,2},{7,3},{8,12},{9,13},{10,... | collective-permute-start | bytes 258056 | tf_op jit(solution)/shard_map/ppermute | solution.py:56
  12.0 16.4 %collective-permute-done.1.refs_2_ = bf16[336,128]{1,0:T(8,128)(2,1)S(1)} collective-permute-done((bf16[336,128]{1,0:T(8,128)(2,1)}, bf16[336,128]{1,0:T(8,128)(2,1)S(1)}, u32[]{:S(2)}, u32[]{:S(2)}) %collective-permute-start.1) | collective-permute-done | bytes 86048 | tf_op jit(solution)/shard_map/ppermute | solution.py:56
  28.4 4.1 %collective-permute-start.4 = (bf16[336,128]{1,0:T(8,128)(2,1)}, bf16[336,128]{1,0:T(8,128)(2,1)S(1)}, u32[]{:S(2)}, u32[]{:S(2)}) collective-permute-start(bf16[336,128]{1,0:T(8,128)(2,1)} %get-tuple-element.29), channel_id=1, source_target_pairs={{0,5},{1,4},{2,7},{3,6},{4,1},{5,0},{6,3},{7,2},{8,13},{9,12},{10,... | collective-permute-start | bytes 258056 | tf_op jit(solution)/shard_map/ppermute | solution.py:56
  32.5 0.8 collective-permute-start.5
  33.5 1.9 %collective-permute-done.4.refs_5_ = bf16[336,128]{1,0:T(8,128)(2,1)S(1)} collective-permute-done((bf16[336,128]{1,0:T(8,128)(2,1)}, bf16[336,128]{1,0:T(8,128)(2,1)S(1)}, u32[]{:S(2)}, u32[]{:S(2)}) %collective-permute-start.4) | collective-permute-done | bytes 86048 | tf_op jit(solution)/shard_map/ppermute | solution.py:56
  35.4 1.1 collective-permute-start.23
  36.7 1.5 collective-permute-done.6.refs_7_
  38.8 2.4 %unit.1.refs_0_ = bf16[40,8320]{1,0:T(8,128)(2,1)} custom-call(bf16[336,128]{1,0:T(8,128)(2,1)} %get-tuple-element.24.refs_0_, bf16[336,128]{1,0:T(8,128)(2,1)} %copy-done.12, bf16[336,128]{1,0:T(8,128)(2,1)} %copy-done.13, bf16[336,128]{1,0:T(8,128)(2,1)} %copy-done.14, bf16[336,128]{1,0:T(8,128)(2,1)} %copy-done.15, bf16[336,128]{1,0:T(8,128)(2,1)} %copy-done.16, ...), custom_call_target="tpu_custom_call" | custom-call | tf_op jit(solution)/shard_map/unit/pallas_call | solution.py:128
  41.3 3.8 %collective-permute-start.9 = (bf16[40,8320]{1,0:T(8,128)(2,1)}, bf16[40,8320]{1,0:T(8,128)(2,1)}, u32[]{:S(2)}, u32[]{:S(2)}) collective-permute-start(bf16[40,8320]{1,0:T(8,128)(2,1)} %unit.1.refs_0_), channel_id=1, source_target_pairs={{0,104},{8,112},{16,120},{24,96},{32,8},{40,16},{48,24},{56,0},{64... | collective-permute-start | bytes 1996808 | tf_op jit(solution)/shard_map/ppermute | solution.py:48
  45.1 1.1 collective-permute-start.8
  46.3 14.4 %collective-permute-done.9.refs_3_ = bf16[40,8320]{1,0:T(8,128)(2,1)} collective-permute-done((bf16[40,8320]{1,0:T(8,128)(2,1)}, bf16[40,8320]{1,0:T(8,128)(2,1)}, u32[]{:S(2)}, u32[]{:S(2)}) %collective-permute-start.9) | collective-permute-done | bytes 665632 | tf_op jit(solution)/shard_map/ppermute | solution.py:48
  60.7 1.5 collective-permute-start.22
  62.3 1.9 %collective-permute-start.16 = (bf16[16,128,128]{2,1,0:T(8,128)(2,1)S(1)}, bf16[16,128,128]{2,1,0:T(8,128)(2,1)S(1)}, u32[]{:S(2)}, u32[]{:S(2)}) collective-permute-start(bf16[16,128,128]{2,1,0:T(8,128)(2,1)S(1)} %slice.10), channel_id=1, source_target_pairs={{0,2},{1,3},{2,4},{3,5},{4,6},{5,7},{6,0},{7,1},{8,10},{9,11},{10,... | collective-permute-start | bytes 1572872 | tf_op jit(solution)/shard_map/ppermute | solution.py:56
  64.3 1.5 collective-permute-start.18
  65.7 2.4 %collective-permute-start.10 = (bf16[40,8320]{1,0:T(8,128)(2,1)}, bf16[40,8320]{1,0:T(8,128)(2,1)}, u32[]{:S(2)}, u32[]{:S(2)}) collective-permute-start(bf16[40,8320]{1,0:T(8,128)(2,1)} %collective-permute-done.9.refs_3_), channel_id=1, source_target_pairs={{0,96},{8,104},{16,112},{24,120},{32,0},{40,8},{48,16},{56,24},{64... | collective-permute-start | bytes 1996808 | tf_op jit(solution)/shard_map/ppermute | solution.py:48
  68.2 8.2 %collective-permute-done.16.refs_0_ = bf16[16,128,128]{2,1,0:T(8,128)(2,1)S(1)} collective-permute-done((bf16[16,128,128]{2,1,0:T(8,128)(2,1)S(1)}, bf16[16,128,128]{2,1,0:T(8,128)(2,1)S(1)}, u32[]{:S(2)}, u32[]{:S(2)}) %collective-permute-start.16) | collective-permute-done | bytes 524320 | tf_op jit(solution)/shard_map/ppermute | solution.py:56
  76.3 2.1 %collective-permute-start.19 = (bf16[16,128,128]{2,1,0:T(8,128)(2,1)S(1)}, bf16[16,128,128]{2,1,0:T(8,128)(2,1)S(1)}, u32[]{:S(2)}, u32[]{:S(2)}) collective-permute-start(bf16[16,128,128]{2,1,0:T(8,128)(2,1)S(1)} %collective-permute-done.16.refs_0_), channel_id=1, source_target_pairs={{0,1},{1,0},{2,3},{3,2},{4,5},{5,4},{6,7},{7,6},{8,9},{9,8},{10,11... | collective-permute-start | bytes 1572872 | tf_op jit(solution)/shard_map/ppermute | solution.py:56
  78.7 3.1 %collective-permute-done.10.refs_4_ = bf16[40,8320]{1,0:T(8,128)(2,1)} collective-permute-done((bf16[40,8320]{1,0:T(8,128)(2,1)}, bf16[40,8320]{1,0:T(8,128)(2,1)}, u32[]{:S(2)}, u32[]{:S(2)}) %collective-permute-start.10) | collective-permute-done | bytes 665632 | tf_op jit(solution)/shard_map/ppermute | solution.py:48
  82.4 0.6 collective-permute-start.12
  83.0 1.0 copy-done.5
  84.0 2.6 %collective-permute-start.13 = (bf16[40,8320]{1,0:T(8,128)(2,1)}, bf16[40,8320]{1,0:T(8,128)(2,1)}, u32[]{:S(2)}, u32[]{:S(2)}) collective-permute-start(bf16[40,8320]{1,0:T(8,128)(2,1)} %collective-permute-done.8.refs_2_), channel_id=1, source_target_pairs={{0,24},{8,0},{16,8},{24,16},{32,56},{40,32},{48,40},{56,48},{64,88... | collective-permute-start | bytes 1996808 | tf_op jit(solution)/shard_map/ppermute | solution.py:48
  86.7 2.7 %collective-permute-start.14 = (bf16[40,8320]{1,0:T(8,128)(2,1)}, bf16[40,8320]{1,0:T(8,128)(2,1)}, u32[]{:S(2)}, u32[]{:S(2)}) collective-permute-start(bf16[40,8320]{1,0:T(8,128)(2,1)} %collective-permute-done.8.refs_2_), channel_id=1, source_target_pairs={{0,96},{8,104},{16,112},{24,120},{32,0},{40,8},{48,16},{56,24},{64... | collective-permute-start | bytes 1996808 | tf_op jit(solution)/shard_map/ppermute | solution.py:48
  89.4 0.8 copy-done.11
  90.4 3.1 %prepare.1 = (bf16[8,128,256]{2,1,0:T(8,128)(2,1)}, bf16[8,128,256]{2,1,0:T(8,128)(2,1)}) custom-call(s32[3]{0:T(128)} %pad_add_fusion.where, bf16[1024,1024]{1,0:T(8,128)(2,1)} %primal.1, bf16[1024,1024]{1,0:T(8,128)(2,1)} %dual.1), custom_call_target="tpu_custom_call" | custom-call | tf_op jit(solution)/shard_map/prepare/pallas_call | solution.py:155
  93.6 6.3 %reduced.4.refs_2_ = bf16[256,8320]{1,0:T(8,128)(2,1)} custom-call(s32[3]{0:T(128)} %pad_add_fusion.where, s32[4096]{0:T(1024)} %bitcast.23, bf16[8,128,256]{2,1,0:T(8,128)(2,1)} %get-tuple-element.32.right, bf16[8,128,256]{2,1,0:T(8,128)(2,1)} %get-tuple-element.33.left, bf16[32,128,128]{2,1,0:T(8,128)(2,1)} %refs_0_.1, ...), custom_call_target="tpu_custom_call" | custom-call | tf_op jit(solution)/shard_map/reduced/pallas_call | solution.py:214
  99.9 6.3 %reduced.5.refs_2_ = bf16[256,8320]{1,0:T(8,128)(2,1)} custom-call(s32[3]{0:T(128)} %pad_add_fusion.where, s32[4096]{0:T(1024)} %bitcast.24, bf16[8,128,256]{2,1,0:T(8,128)(2,1)} %get-tuple-element.32.right, bf16[8,128,256]{2,1,0:T(8,128)(2,1)} %get-tuple-element.33.left, bf16[32,128,128]{2,1,0:T(8,128)(2,1)} %copy-done.2, ...), custom_call_target="tpu_custom_call", output_to_operand_aliasing={{}: (6, {})} | custom-call | tf_op jit(solution)/shard_map/reduced/pallas_call | solution.py:214
  106.2 6.3 %reduced.6.refs_4_ = bf16[256,8320]{1,0:T(8,128)(2,1)} custom-call(s32[3]{0:T(128)} %pad_add_fusion.where, s32[4096]{0:T(1024)} %bitcast.25, bf16[8,128,256]{2,1,0:T(8,128)(2,1)} %get-tuple-element.32.right, bf16[8,128,256]{2,1,0:T(8,128)(2,1)} %get-tuple-element.33.left, bf16[32,128,128]{2,1,0:T(8,128)(2,1)} %copy-done.3, ...), custom_call_target="tpu_custom_call", output_to_operand_aliasing={{}: (6, {})} | custom-call | tf_op jit(solution)/shard_map/reduced/pallas_call | solution.py:214
  112.5 7.0 %reduced.7.refs_9_.refs_16_ = bf16[256,8320]{1,0:T(8,128)(2,1)} custom-call(s32[3]{0:T(128)} %pad_add_fusion.where, s32[4096]{0:T(1024)} %bitcast.26, bf16[8,128,256]{2,1,0:T(8,128)(2,1)} %get-tuple-element.32.right, bf16[8,128,256]{2,1,0:T(8,128)(2,1)} %get-tuple-element.33.left, bf16[16,128,128]{2,1,0:T(8,128)(2,1)} %copy-done.8, ...), custom_call_target="tpu_custom_call", output_to_operand_aliasing={{}: (8, {})} | custom-call | tf_op jit(solution)/shard_map/reduced/pallas_call | solution.py:214
  119.5 6.5 %contract.1 = (f32[40,256]{1,0:T(8,128)}, f32[40,256]{1,0:T(8,128)}, f32[40,256]{1,0:T(8,128)}, f32[40,256]{1,0:T(8,128)}, f32[40,256]{1,0:T(8,128)}, /*index=5*...) custom-call(bf16[40,8320]{1,0:T(8,128)(2,1)} %unit.1.refs_0_, ...), custom_call_target="tpu_custom_call" | custom-call | tf_op jit(solution)/shard_map/contract/pallas_call | solution.py:240
  126.0 1.4 collective-permute-start.24
  127.6 0.9 collective-permute-start.25
  128.5 1.8 %collective-permute-start.26 = (f32[40,256]{1,0:T(8,128)}, f32[40,256]{1,0:T(8,128)S(1)}, u32[]{:S(2)}, u32[]{:S(2)}) collective-permute-start(f32[40,256]{1,0:T(8,128)} %get-tuple-element.37.refs_3_), channel_id=1, source_target_pairs={{0,56},{8,32},{16,40},{24,48},{32,88},{40,64},{48,72},{56,80},{64,... | collective-permute-start | bytes 122888 | tf_op jit(solution)/shard_map/ppermute | solution.py:48
  130.3 2.9 %collective-permute-start.27 = (f32[40,256]{1,0:T(8,128)}, f32[40,256]{1,0:T(8,128)S(1)}, u32[]{:S(2)}, u32[]{:S(2)}) collective-permute-start(f32[40,256]{1,0:T(8,128)} %get-tuple-element.38.refs_4_), channel_id=1, source_target_pairs={{0,88},{8,64},{16,72},{24,80},{32,120},{40,96},{48,104},{56,112},{... | collective-permute-start | bytes 122888 | tf_op jit(solution)/shard_map/ppermute | solution.py:48
  133.2 1.0 collective-permute-start.28
  134.4 1.3 collective-permute-done.27.refs_12_
  135.7 4.6 %collective-permute-done.28.refs_13_ = f32[40,256]{1,0:T(8,128)S(1)} collective-permute-done((f32[40,256]{1,0:T(8,128)}, f32[40,256]{1,0:T(8,128)S(1)}, u32[]{:S(2)}, u32[]{:S(2)}) %collective-permute-start.28) | collective-permute-done | bytes 40992 | tf_op jit(solution)/shard_map/ppermute | solution.py:48
  141.3 4.9 %gather.8 = f32[16,40,256]{2,1,0:T(8,128)} custom-call(s32[3]{0:T(128)} %pad_add_fusion.where, f32[40,256]{1,0:T(8,128)} %get-tuple-element.34.refs_0_, f32[40,256]{1,0:T(8,128)} %get-tuple-element.35.refs_1_, f32[40,256]{1,0:T(8,128)} %get-tuple-element.36.refs_2_, f32[40,256]{1,0:T(8,128)} %get-tuple-element.37.refs_3_, ...), custom_call_target="tpu_custom_call" | custom-call | tf_op jit(solution)/shard_map/gather/pallas_call | solution.py:266
  146.3 8.9 %all-to-all-start = ((f32[8,2,40,256]{3,2,1,0:T(8,128)}), f32[8,2,40,256]{3,2,1,0:T(8,128)S(1)}, u32[]{:S(2)}, u32[]{:S(2)}) async-start(f32[8,2,40,256]{3,2,1,0:T(8,128)} %bitcast.21), calls=%async_computation | async-start | bytes 1310720 | tf_op jit(solution)/shard_map/all_to_all | solution.py:351
  155.9 0.7 reduce.7
  158.4 0.8 select_bitcast_fusion.places_ref
  159.2 6.7 %all-to-all-done.landed = f32[8,2,40,256]{3,2,1,0:T(8,128)S(1)} async-done(((f32[8,2,40,256]{3,2,1,0:T(8,128)}), f32[8,2,40,256]{3,2,1,0:T(8,128)S(1)}, u32[]{:S(2)}, u32[]{:S(2)}) %all-to-all-start) | async-done | bytes 655392 | tf_op jit(solution)/shard_map/all_to_all | solution.py:351
  165.9 0.9 copy-done.1
  166.8 3.0 %final.1 = f32[256,512]{1,0:T(8,128)} custom-call(s32[2]{0:T(128)} %get-tuple-element.44.flags, s32[256,2]{1,0:T(8,128)} %select_bitcast_fusion.places_ref, f32[8,2,40,256]{3,2,1,0:T(8,128)} %copy-done.1), custom_call_target="tpu_custom_call" | custom-call | tf_op jit(solution)/shard_map/final/pallas_call | solution.py:298
  (99 shorter events, 7.0 us)
Async XLA Ops:
  0.0 90.2 %copy-start.6 = (s32[4096,1]{0,1:T(1,128)S(1)}, s32[4096,1]{0,1:T(1,128)}, u32[]{:S(2)}) copy-start(s32[4096,1]{0,1:T(1,128)} %param.6) | copy-start | bytes 49156
  0.0 45.1 %collective-permute-start.15 = (bf16[32,128,128]{2,1,0:T(8,128)(2,1)}, bf16[32,128,128]{2,1,0:T(8,128)(2,1)S(1)}, u32[]{:S(2)}, u32[]{:S(2)}) collective-permute-start(bf16[32,128,128]{2,1,0:T(8,128)(2,1)} %refs_0_.1), channel_id=1, source_target_pairs={{0,2},{1,3},{2,4},{3,5},{4,6},{5,7},{6,0},{7,1},{8,10},{9,11},{10,... | collective-permute-start | bytes 3145736 | tf_op jit(solution)/shard_map/ppermute | solution.py:56
  2.1 60.1 %collective-permute-start.17 = (bf16[32,128,128]{2,1,0:T(8,128)(2,1)}, bf16[32,128,128]{2,1,0:T(8,128)(2,1)S(1)}, u32[]{:S(2)}, u32[]{:S(2)}) collective-permute-start(bf16[32,128,128]{2,1,0:T(8,128)(2,1)} %refs_0_.1), channel_id=1, source_target_pairs={{0,6},{1,7},{2,0},{3,1},{4,2},{5,3},{6,4},{7,5},{8,14},{9,15},{10,... | collective-permute-start | bytes 3145736 | tf_op jit(solution)/shard_map/ppermute | solution.py:56
  6.9 2.7 %collective-permute-start = (bf16[336,128]{1,0:T(8,128)(2,1)}, bf16[336,128]{1,0:T(8,128)(2,1)S(1)}, u32[]{:S(2)}, u32[]{:S(2)}) collective-permute-start(bf16[336,128]{1,0:T(8,128)(2,1)} %get-tuple-element.25), channel_id=1, source_target_pairs={{0,1},{1,0},{2,3},{3,2},{4,5},{5,4},{6,7},{7,6},{8,9},{9,8},{10,11... | collective-permute-start | bytes 258056 | tf_op jit(solution)/shard_map/ppermute | solution.py:56
  7.9 20.5 %collective-permute-start.1 = (bf16[336,128]{1,0:T(8,128)(2,1)}, bf16[336,128]{1,0:T(8,128)(2,1)S(1)}, u32[]{:S(2)}, u32[]{:S(2)}) collective-permute-start(bf16[336,128]{1,0:T(8,128)(2,1)} %get-tuple-element.26), channel_id=1, source_target_pairs={{0,2},{1,3},{2,4},{3,5},{4,6},{5,7},{6,0},{7,1},{8,10},{9,11},{10,... | collective-permute-start | bytes 258056 | tf_op jit(solution)/shard_map/ppermute | solution.py:56
  8.1 24.4 %collective-permute-start.2 = (bf16[336,128]{1,0:T(8,128)(2,1)}, bf16[336,128]{1,0:T(8,128)(2,1)S(1)}, u32[]{:S(2)}, u32[]{:S(2)}) collective-permute-start(bf16[336,128]{1,0:T(8,128)(2,1)} %get-tuple-element.27), channel_id=1, source_target_pairs={{0,3},{1,2},{2,5},{3,4},{4,7},{5,6},{6,1},{7,0},{8,11},{9,10},{10,... | collective-permute-start | bytes 258056 | tf_op jit(solution)/shard_map/ppermute | solution.py:56
  9.6 28.6 %copy-start.12 = (bf16[336,128]{1,0:T(8,128)(2,1)}, bf16[336,128]{1,0:T(8,128)(2,1)S(1)}, u32[]{:S(2)}) copy-start(bf16[336,128]{1,0:T(8,128)(2,1)S(1)} %collective-permute-done.refs_1_) | copy-start | bytes 258052
  9.6 23.7 %collective-permute-start.3 = (bf16[336,128]{1,0:T(8,128)(2,1)}, bf16[336,128]{1,0:T(8,128)(2,1)S(1)}, u32[]{:S(2)}, u32[]{:S(2)}) collective-permute-start(bf16[336,128]{1,0:T(8,128)(2,1)} %get-tuple-element.28), channel_id=1, source_target_pairs={{0,4},{1,5},{2,6},{3,7},{4,0},{5,1},{6,2},{7,3},{8,12},{9,13},{10,... | collective-permute-start | bytes 258056 | tf_op jit(solution)/shard_map/ppermute | solution.py:56
  28.4 9.8 %copy-start.13 = (bf16[336,128]{1,0:T(8,128)(2,1)}, bf16[336,128]{1,0:T(8,128)(2,1)S(1)}, u32[]{:S(2)}) copy-start(bf16[336,128]{1,0:T(8,128)(2,1)S(1)} %collective-permute-done.1.refs_2_) | copy-start | bytes 258052
  28.4 7.0 %collective-permute-start.4 = (bf16[336,128]{1,0:T(8,128)(2,1)}, bf16[336,128]{1,0:T(8,128)(2,1)S(1)}, u32[]{:S(2)}, u32[]{:S(2)}) collective-permute-start(bf16[336,128]{1,0:T(8,128)(2,1)} %get-tuple-element.29), channel_id=1, source_target_pairs={{0,5},{1,4},{2,7},{3,6},{4,1},{5,0},{6,3},{7,2},{8,13},{9,12},{10,... | collective-permute-start | bytes 258056 | tf_op jit(solution)/shard_map/ppermute | solution.py:56
  32.5 5.7 %copy-start.14 = (bf16[336,128]{1,0:T(8,128)(2,1)}, bf16[336,128]{1,0:T(8,128)(2,1)S(1)}, u32[]{:S(2)}) copy-start(bf16[336,128]{1,0:T(8,128)(2,1)S(1)} %collective-permute-done.2.refs_3_) | copy-start | bytes 258052
  32.5 4.2 %collective-permute-start.5 = (bf16[336,128]{1,0:T(8,128)(2,1)}, bf16[336,128]{1,0:T(8,128)(2,1)S(1)}, u32[]{:S(2)}, u32[]{:S(2)}) collective-permute-start(bf16[336,128]{1,0:T(8,128)(2,1)} %get-tuple-element.30), channel_id=1, source_target_pairs={{0,6},{1,7},{2,0},{3,1},{4,2},{5,3},{6,4},{7,5},{8,14},{9,15},{10,... | collective-permute-start | bytes 258056 | tf_op jit(solution)/shard_map/ppermute | solution.py:56
  33.3 4.9 %copy-start.15 = (bf16[336,128]{1,0:T(8,128)(2,1)}, bf16[336,128]{1,0:T(8,128)(2,1)S(1)}, u32[]{:S(2)}) copy-start(bf16[336,128]{1,0:T(8,128)(2,1)S(1)} %collective-permute-done.3.refs_4_) | copy-start | bytes 258052
  33.3 4.9 %collective-permute-start.6 = (bf16[336,128]{1,0:T(8,128)(2,1)}, bf16[336,128]{1,0:T(8,128)(2,1)S(1)}, u32[]{:S(2)}, u32[]{:S(2)}) collective-permute-start(bf16[336,128]{1,0:T(8,128)(2,1)} %get-tuple-element.31), channel_id=1, source_target_pairs={{0,7},{1,6},{2,1},{3,0},{4,3},{5,2},{6,5},{7,4},{8,15},{9,14},{10,... | collective-permute-start | bytes 258056 | tf_op jit(solution)/shard_map/ppermute | solution.py:56
  35.4 30.4 %collective-permute-start.23 = (bf16[32,128,128]{2,1,0:T(8,128)(2,1)}, bf16[32,128,128]{2,1,0:T(8,128)(2,1)}, u32[]{:S(2)}, u32[]{:S(2)}) collective-permute-start(bf16[32,128,128]{2,1,0:T(8,128)(2,1)} %refs_0_.1), channel_id=1, source_target_pairs={{0,1},{1,0},{2,3},{3,2},{4,5},{5,4},{6,7},{7,6},{8,9},{9,8},{10,11... | collective-permute-start | bytes 3145736 | tf_op jit(solution)/shard_map/ppermute | solution.py:56
  41.3 19.4 %collective-permute-start.9 = (bf16[40,8320]{1,0:T(8,128)(2,1)}, bf16[40,8320]{1,0:T(8,128)(2,1)}, u32[]{:S(2)}, u32[]{:S(2)}) collective-permute-start(bf16[40,8320]{1,0:T(8,128)(2,1)} %unit.1.refs_0_), channel_id=1, source_target_pairs={{0,104},{8,112},{16,120},{24,96},{32,8},{40,16},{48,24},{56,0},{64... | collective-permute-start | bytes 1996808 | tf_op jit(solution)/shard_map/ppermute | solution.py:48
  45.1 17.2 %collective-permute-start.7 = (bf16[40,8320]{1,0:T(8,128)(2,1)}, bf16[40,8320]{1,0:T(8,128)(2,1)}, u32[]{:S(2)}, u32[]{:S(2)}) collective-permute-start(bf16[40,8320]{1,0:T(8,128)(2,1)} %unit.1.refs_0_), channel_id=1, source_target_pairs={{0,32},{8,40},{16,48},{24,56},{32,64},{40,72},{48,80},{56,88},{64,... | collective-permute-start | bytes 1996808 | tf_op jit(solution)/shard_map/ppermute | solution.py:48
  45.1 54.8 %copy-start.2 = (bf16[32,128,128]{2,1,0:T(8,128)(2,1)}, bf16[32,128,128]{2,1,0:T(8,128)(2,1)S(1)}, u32[]{:S(2)}) copy-start(bf16[32,128,128]{2,1,0:T(8,128)(2,1)S(1)} %collective-permute-done.15.refs_0_) | copy-start | bytes 3145732
  45.1 19.2 %collective-permute-start.8 = (bf16[40,8320]{1,0:T(8,128)(2,1)}, bf16[40,8320]{1,0:T(8,128)(2,1)}, u32[]{:S(2)}, u32[]{:S(2)}) collective-permute-start(bf16[40,8320]{1,0:T(8,128)(2,1)} %unit.1.refs_0_), channel_id=1, source_target_pairs={{0,24},{8,0},{16,8},{24,16},{32,56},{40,32},{48,40},{56,48},{64,88... | collective-permute-start | bytes 1996808 | tf_op jit(solution)/shard_map/ppermute | solution.py:48
  60.7 21.7 %collective-permute-start.22 = (bf16[32,128,128]{2,1,0:T(8,128)(2,1)S(1)}, bf16[32,128,128]{2,1,0:T(8,128)(2,1)S(1)}, u32[]{:S(2)}, u32[]{:S(2)}) collective-permute-start(bf16[32,128,128]{2,1,0:T(8,128)(2,1)S(1)} %collective-permute-done.15.refs_0_), channel_id=1, source_target_pairs={{0,1},{1,0},{2,3},{3,2},{4,5},{5,4},{6,7},{7,6},{8,9},{9,8},{10,11... | collective-permute-start | bytes 3145736 | tf_op jit(solution)/shard_map/ppermute | solution.py:56
  62.2 37.7 %copy-start.3 = (bf16[32,128,128]{2,1,0:T(8,128)(2,1)}, bf16[32,128,128]{2,1,0:T(8,128)(2,1)S(1)}, u32[]{:S(2)}) copy-start(bf16[32,128,128]{2,1,0:T(8,128)(2,1)S(1)} %collective-permute-done.17.refs_0_) | copy-start | bytes 3145732
  62.2 20.8 %collective-permute-start.21 = (bf16[32,128,128]{2,1,0:T(8,128)(2,1)S(1)}, bf16[32,128,128]{2,1,0:T(8,128)(2,1)S(1)}, u32[]{:S(2)}, u32[]{:S(2)}) collective-permute-start(bf16[32,128,128]{2,1,0:T(8,128)(2,1)S(1)} %collective-permute-done.17.refs_0_), channel_id=1, source_target_pairs={{0,1},{1,0},{2,3},{3,2},{4,5},{5,4},{6,7},{7,6},{8,9},{9,8},{10,11... | collective-permute-start | bytes 3145736 | tf_op jit(solution)/shard_map/ppermute | solution.py:56
  62.3 14.1 %collective-permute-start.16 = (bf16[16,128,128]{2,1,0:T(8,128)(2,1)S(1)}, bf16[16,128,128]{2,1,0:T(8,128)(2,1)S(1)}, u32[]{:S(2)}, u32[]{:S(2)}) collective-permute-start(bf16[16,128,128]{2,1,0:T(8,128)(2,1)S(1)} %slice.10), channel_id=1, source_target_pairs={{0,2},{1,3},{2,4},{3,5},{4,6},{5,7},{6,0},{7,1},{8,10},{9,11},{10,... | collective-permute-start | bytes 1572872 | tf_op jit(solution)/shard_map/ppermute | solution.py:56
  64.3 14.2 %collective-permute-start.18 = (bf16[16,128,128]{2,1,0:T(8,128)(2,1)S(1)}, bf16[16,128,128]{2,1,0:T(8,128)(2,1)S(1)}, u32[]{:S(2)}, u32[]{:S(2)}) collective-permute-start(bf16[16,128,128]{2,1,0:T(8,128)(2,1)S(1)} %slice.11), channel_id=1, source_target_pairs={{0,6},{1,7},{2,0},{3,1},{4,2},{5,3},{6,4},{7,5},{8,14},{9,15},{10,... | collective-permute-start | bytes 1572872 | tf_op jit(solution)/shard_map/ppermute | solution.py:56
  65.7 16.1 %collective-permute-start.10 = (bf16[40,8320]{1,0:T(8,128)(2,1)}, bf16[40,8320]{1,0:T(8,128)(2,1)}, u32[]{:S(2)}, u32[]{:S(2)}) collective-permute-start(bf16[40,8320]{1,0:T(8,128)(2,1)} %collective-permute-done.9.refs_3_), channel_id=1, source_target_pairs={{0,96},{8,104},{16,112},{24,120},{32,0},{40,8},{48,16},{56,24},{64... | collective-permute-start | bytes 1996808 | tf_op jit(solution)/shard_map/ppermute | solution.py:48
  76.3 10.3 %copy-start.8 = (bf16[16,128,128]{2,1,0:T(8,128)(2,1)}, bf16[16,128,128]{2,1,0:T(8,128)(2,1)S(1)}, u32[]{:S(2)}) copy-start(bf16[16,128,128]{2,1,0:T(8,128)(2,1)S(1)} %collective-permute-done.16.refs_0_) | copy-start | bytes 1572868
  76.3 10.3 %collective-permute-start.19 = (bf16[16,128,128]{2,1,0:T(8,128)(2,1)S(1)}, bf16[16,128,128]{2,1,0:T(8,128)(2,1)S(1)}, u32[]{:S(2)}, u32[]{:S(2)}) collective-permute-start(bf16[16,128,128]{2,1,0:T(8,128)(2,1)S(1)} %collective-permute-done.16.refs_0_), channel_id=1, source_target_pairs={{0,1},{1,0},{2,3},{3,2},{4,5},{5,4},{6,7},{7,6},{8,9},{9,8},{10,11... | collective-permute-start | bytes 1572872 | tf_op jit(solution)/shard_map/ppermute | solution.py:56
  78.5 8.2 %copy-start.9 = (bf16[16,128,128]{2,1,0:T(8,128)(2,1)}, bf16[16,128,128]{2,1,0:T(8,128)(2,1)S(1)}, u32[]{:S(2)}) copy-start(bf16[16,128,128]{2,1,0:T(8,128)(2,1)S(1)} %collective-permute-done.18.refs_1_) | copy-start | bytes 1572868
  78.5 10.9 %collective-permute-start.20 = (bf16[16,128,128]{2,1,0:T(8,128)(2,1)S(1)}, bf16[16,128,128]{2,1,0:T(8,128)(2,1)S(1)}, u32[]{:S(2)}, u32[]{:S(2)}) collective-permute-start(bf16[16,128,128]{2,1,0:T(8,128)(2,1)S(1)} %collective-permute-done.18.refs_1_), channel_id=1, source_target_pairs={{0,1},{1,0},{2,3},{3,2},{4,5},{5,4},{6,7},{7,6},{8,9},{9,8},{10,11... | collective-permute-start | bytes 1572872 | tf_op jit(solution)/shard_map/ppermute | solution.py:56
  81.8 37.6 %collective-permute-start.11 = (bf16[40,8320]{1,0:T(8,128)(2,1)}, bf16[40,8320]{1,0:T(8,128)(2,1)}, u32[]{:S(2)}, u32[]{:S(2)}) collective-permute-start(bf16[40,8320]{1,0:T(8,128)(2,1)} %collective-permute-done.9.refs_3_), channel_id=1, source_target_pairs={{0,8},{8,16},{16,24},{24,0},{32,40},{40,48},{48,56},{56,32},{64,72... | collective-permute-start | bytes 1996808 | tf_op jit(solution)/shard_map/ppermute | solution.py:48
  82.4 17.5 %copy-start.4 = (bf16[32,128,128]{2,1,0:T(8,128)(2,1)}, bf16[32,128,128]{2,1,0:T(8,128)(2,1)S(1)}, u32[]{:S(2)}) copy-start(bf16[32,128,128]{2,1,0:T(8,128)(2,1)S(1)} %collective-permute-done.22.refs_1_) | copy-start | bytes 3145732
  82.4 37.1 %collective-permute-start.12 = (bf16[40,8320]{1,0:T(8,128)(2,1)}, bf16[40,8320]{1,0:T(8,128)(2,1)}, u32[]{:S(2)}, u32[]{:S(2)}) collective-permute-start(bf16[40,8320]{1,0:T(8,128)(2,1)} %collective-permute-done.7.refs_1_), channel_id=1, source_target_pairs={{0,32},{8,40},{16,48},{24,56},{32,64},{40,72},{48,80},{56,88},{64,... | collective-permute-start | bytes 1996808 | tf_op jit(solution)/shard_map/ppermute | solution.py:48
  84.0 35.4 %collective-permute-start.13 = (bf16[40,8320]{1,0:T(8,128)(2,1)}, bf16[40,8320]{1,0:T(8,128)(2,1)}, u32[]{:S(2)}, u32[]{:S(2)}) collective-permute-start(bf16[40,8320]{1,0:T(8,128)(2,1)} %collective-permute-done.8.refs_2_), channel_id=1, source_target_pairs={{0,24},{8,0},{16,8},{24,16},{32,56},{40,32},{48,40},{56,48},{64,88... | collective-permute-start | bytes 1996808 | tf_op jit(solution)/shard_map/ppermute | solution.py:48
  86.7 32.8 %collective-permute-start.14 = (bf16[40,8320]{1,0:T(8,128)(2,1)}, bf16[40,8320]{1,0:T(8,128)(2,1)}, u32[]{:S(2)}, u32[]{:S(2)}) collective-permute-start(bf16[40,8320]{1,0:T(8,128)(2,1)} %collective-permute-done.8.refs_2_), channel_id=1, source_target_pairs={{0,96},{8,104},{16,112},{24,120},{32,0},{40,8},{48,16},{56,24},{64... | collective-permute-start | bytes 1996808 | tf_op jit(solution)/shard_map/ppermute | solution.py:48
  90.2 42.9 %collective-permute-start.30 = (bf16[40,8320]{1,0:T(8,128)(2,1)}, bf16[40,8320]{1,0:T(8,128)(2,1)}, u32[]{:S(2)}, u32[]{:S(2)}) collective-permute-start(bf16[40,8320]{1,0:T(8,128)(2,1)} %collective-permute-done.10.refs_4_), channel_id=1, source_target_pairs={{0,8},{8,16},{16,24},{24,0},{32,40},{40,48},{48,56},{56,32},{64,72... | collective-permute-start | bytes 1996808 | tf_op jit(solution)/shard_map/ppermute | solution.py:48
  126.0 30.0 %copy-start.7 = (s32[4096,1]{0,1:T(1,128)S(1)}, s32[4096,1]{0,1:T(1,128)}, u32[]{:S(2)}) copy-start(s32[4096,1]{0,1:T(1,128)} %param.6) | copy-start | bytes 49156
  126.0 30.8 %copy-start = (s32[16]{0:T(128)S(1)}, s32[16]{0:T(128)}, u32[]{:S(2)}) copy-start(s32[16]{0:T(128)} %constant.146.clone) | copy-start | bytes 196
  126.0 8.1 %collective-permute-start.24 = (f32[40,256]{1,0:T(8,128)}, f32[40,256]{1,0:T(8,128)S(1)}, u32[]{:S(2)}, u32[]{:S(2)}) collective-permute-start(f32[40,256]{1,0:T(8,128)} %get-tuple-element.35.refs_1_), channel_id=1, source_target_pairs={{0,96},{8,104},{16,112},{24,120},{32,0},{40,8},{48,16},{56,24},{64... | collective-permute-start | bytes 122888 | tf_op jit(solution)/shard_map/ppermute | solution.py:48
  127.6 6.8 %collective-permute-start.25 = (f32[40,256]{1,0:T(8,128)}, f32[40,256]{1,0:T(8,128)S(1)}, u32[]{:S(2)}, u32[]{:S(2)}) collective-permute-start(f32[40,256]{1,0:T(8,128)} %get-tuple-element.36.refs_2_), channel_id=1, source_target_pairs={{0,8},{8,16},{16,24},{24,0},{32,40},{40,48},{48,56},{56,32},{64,72... | collective-permute-start | bytes 122888 | tf_op jit(solution)/shard_map/ppermute | solution.py:48
  128.5 6.0 %collective-permute-start.26 = (f32[40,256]{1,0:T(8,128)}, f32[40,256]{1,0:T(8,128)S(1)}, u32[]{:S(2)}, u32[]{:S(2)}) collective-permute-start(f32[40,256]{1,0:T(8,128)} %get-tuple-element.37.refs_3_), channel_id=1, source_target_pairs={{0,56},{8,32},{16,40},{24,48},{32,88},{40,64},{48,72},{56,80},{64,... | collective-permute-start | bytes 122888 | tf_op jit(solution)/shard_map/ppermute | solution.py:48
  130.3 5.5 %collective-permute-start.27 = (f32[40,256]{1,0:T(8,128)}, f32[40,256]{1,0:T(8,128)S(1)}, u32[]{:S(2)}, u32[]{:S(2)}) collective-permute-start(f32[40,256]{1,0:T(8,128)} %get-tuple-element.38.refs_4_), channel_id=1, source_target_pairs={{0,88},{8,64},{16,72},{24,80},{32,120},{40,96},{48,104},{56,112},{... | collective-permute-start | bytes 122888 | tf_op jit(solution)/shard_map/ppermute | solution.py:48
  133.2 7.2 %collective-permute-start.28 = (f32[40,256]{1,0:T(8,128)}, f32[40,256]{1,0:T(8,128)S(1)}, u32[]{:S(2)}, u32[]{:S(2)}) collective-permute-start(f32[40,256]{1,0:T(8,128)} %get-tuple-element.39.refs_5_), channel_id=1, source_target_pairs={{0,48},{8,56},{16,32},{24,40},{32,80},{40,88},{48,64},{56,72},{64,... | collective-permute-start | bytes 122888 | tf_op jit(solution)/shard_map/ppermute | solution.py:48
  134.1 6.6 %copy-start.19 = (f32[40,256]{1,0:T(8,128)}, f32[40,256]{1,0:T(8,128)S(1)}, u32[]{:S(2)}) copy-start(f32[40,256]{1,0:T(8,128)S(1)} %collective-permute-done.24.refs_9_) | copy-start | bytes 122884
  134.1 6.6 %collective-permute-start.29 = (f32[40,256]{1,0:T(8,128)}, f32[40,256]{1,0:T(8,128)S(1)}, u32[]{:S(2)}, u32[]{:S(2)}) collective-permute-start(f32[40,256]{1,0:T(8,128)} %get-tuple-element.42.refs_8_), channel_id=1, source_target_pairs={{0,40},{8,48},{16,56},{24,32},{32,72},{40,80},{48,88},{56,64},{64,... | collective-permute-start | bytes 122888 | tf_op jit(solution)/shard_map/ppermute | solution.py:48
  134.4 6.3 %copy-start.20 = (f32[40,256]{1,0:T(8,128)}, f32[40,256]{1,0:T(8,128)S(1)}, u32[]{:S(2)}) copy-start(f32[40,256]{1,0:T(8,128)S(1)} %collective-permute-done.25.refs_10_) | copy-start | bytes 122884
  134.4 6.3 %copy-start.21 = (f32[40,256]{1,0:T(8,128)}, f32[40,256]{1,0:T(8,128)S(1)}, u32[]{:S(2)}) copy-start(f32[40,256]{1,0:T(8,128)S(1)} %collective-permute-done.26.refs_11_) | copy-start | bytes 122884
  135.7 5.0 %copy-start.22 = (f32[40,256]{1,0:T(8,128)}, f32[40,256]{1,0:T(8,128)S(1)}, u32[]{:S(2)}) copy-start(f32[40,256]{1,0:T(8,128)S(1)} %collective-permute-done.27.refs_12_) | copy-start | bytes 122884
  146.3 19.6 %all-to-all-start = ((f32[8,2,40,256]{3,2,1,0:T(8,128)}), f32[8,2,40,256]{3,2,1,0:T(8,128)S(1)}, u32[]{:S(2)}, u32[]{:S(2)}) async-start(f32[8,2,40,256]{3,2,1,0:T(8,128)} %bitcast.21), calls=%async_computation | async-start | bytes 1310720 | tf_op jit(solution)/shard_map/all_to_all | solution.py:351
  (9 other events, 11.7 us)
where the time goes:
time: 170 us
  waiting for transfers between devices  58.7 us (35%)
  starting transfers between devices  53.2 us (31%)
  Pallas kernels  48.4 us (28%)
  local copies, waits for them, and re-layouts  5.9 us (3%)
  other arithmetic  3.21 us (2%)
    ppermute x16, waiting for transfers between devices, line_shift(): return lax.ppermute(x, LINE, pairs)  28.2 us
    pallas_call x4, Pallas kernels, reduce_call(): pl.pallas_call(functools.partial(reduce_kernel, plan, total is not None),...  25.8 us
    ppermute x15, waiting for transfers between devices, plane_shift(): return lax.ppermute(x, PLANE, pairs)  23.8 us
    ppermute x16, starting transfers between devices, line_shift(): return lax.ppermute(x, LINE, pairs)  22.3 us
    ppermute x15, starting transfers between devices, plane_shift(): return lax.ppermute(x, PLANE, pairs)  22.1 us
    all_to_all x1, starting transfers between devices, steps(): lax.all_to_all(ordered.reshape(8, 2, UNIT, 256), LINE, 0, 0, tiled=True)  8.86 us
    all_to_all x1, waiting for transfers between devices, steps(): lax.all_to_all(ordered.reshape(8, 2, UNIT, 256), LINE, 0, 0, tiled=True)  6.71 us
    pallas_call x1, Pallas kernels, contract_call(): pl.pallas_call(functools.partial(contract_kernel, n), out_shape=[jax.Shap...  6.47 us
  transfers between devices with their start and end apart: 32, of which 11 were waited for; matrix products, arithmetic and copies ran while one was open for 3% of the time, Pallas kernels for 24%

commit v1 on v0

v1 whole, which is shorter than its diff:
```python
import functools

import jax
import jax.numpy as jnp
from jax import lax
from jax.experimental import pallas as pl
from jax.experimental.pallas import tpu as pltpu
from jax.sharding import Mesh
from jax.sharding import PartitionSpec as P


MOST = 5
K = 128
H = 64
FOLD = H + 1
WIDTH = FOLD * K
UNIT = 8 * MOST
PIECE = MOST * H + 16
LINE = ("y", "core")
PLANE = ("x", "z")
ALL = ("x", "z", "y", "core")
NT = (((1,), (1,)), ((), ()))
VMEM = pl.BlockSpec(memory_space=pltpu.VMEM)
SMEM = pl.BlockSpec(memory_space=pltpu.SMEM)
HBM = pl.BlockSpec(memory_space=pltpu.HBM)

LIMIT = pltpu.CompilerParams(vmem_limit_bytes=20 << 20)


def near(x):
    return pltpu.with_memory_space_constraint(x, pltpu.VMEM)


def far(x):
    return pltpu.with_memory_space_constraint(x, pltpu.HBM)


def made(*shape, dtype=jnp.bfloat16):
    return pltpu.VMEM(shape, dtype)


FIRST = (((1, 0), (0, 0)), ((0, 3), (0, 0)), ((3, 1), (0, 0)))
SECOND = (((3, 3), (0, 3)), ((3, 2), (3, 1)), ((2, 3), (1, 0)))
THIRD = (((2, 0), (1, 0)), ((0, 2), (0, 3)), ((2, 2), (3, 2)))
EARLY = ((0, 0),) + tuple(d for d, _ in FIRST + SECOND)
LATE = tuple(d for d, _ in THIRD)
FORMED = EARLY + LATE


def negated(d):
    return ((-d[0]) % 4, (-d[1]) % 4)


TURNED = tuple(negated(d) for d in FORMED if negated(d) not in FORMED)


def plane_shift(x, shift):
    pairs = []
    for a in range(4):
        for b in range(4):
            pairs.append((a * 4 + b, (a + shift[0]) % 4 * 4 + (b + shift[1]) % 4))
    return lax.ppermute(x, PLANE, pairs)


def line_shift(x, shift, swap):
    pairs = []
    for a in range(4):
        for b in range(2):
            pairs.append((a * 2 + b, (a + shift) % 4 * 2 + (b + swap) % 2))
    return lax.ppermute(x, LINE, pairs)


def folded(square, half_diagonal):
    top, bottom = square[:H], square[H:]
    row = lax.broadcasted_iota(jnp.int32, (H, K), 0)
    lane = lax.broadcasted_iota(jnp.int32, (H, K), 1)
    turned = pltpu.roll(bottom, H, 1)
    kept = jnp.where(jnp.logical_and(lane < H, row > lane), turned, top)
    last = jnp.sum(jnp.where(lane == row + H, bottom, 0.0), axis=0, keepdims=True)
    if half_diagonal:
        kept = kept * jnp.where(row == lane, 0.5, 1.0)
        last = last * 0.5
    return kept, last


def fold_kernel(where, tiles, own_ref, *refs):
    outs, held, lasts, counts = refs[:8], refs[8], refs[9], refs[10]
    held[...] = jnp.zeros(held.shape, held.dtype)
    lasts[...] = jnp.zeros(lasts.shape, lasts.dtype)
    for k in range(8):
        counts[k] = 0
    y, core = where[1], where[2]
    mine = where[0] * 256 + y * 64 + core * 32

    def four(n, carry):
        for m in range(8):
            i = n * 8 + m
            t = tiles[mine + i]
            order = counts[t]
            counts[t] = order + 1
            goal = lax.rem(t // 2 - y + 4, 4) * 2 + lax.rem(t + core, 2)
            kept, last = folded(own_ref[i].astype(jnp.float32), False)
            row = pl.multiple_of(goal * PIECE + order * H, 16)
            held[pl.ds(row, H), :] = kept.astype(held.dtype)
            lasts[pl.ds(goal * 16 + order, 1), :] = last
        return carry

    lax.fori_loop(0, 4, four, 0)
    for k in range(8):
        outs[k][: MOST * H, :] = held[k * PIECE : k * PIECE + MOST * H, :]
        outs[k][MOST * H :, :] = lasts[k * 16 : (k + 1) * 16, :].astype(held.dtype)


def fold_call(where, tiles, own):
    return pl.pallas_call(
        fold_kernel,
        out_shape=[made(PIECE, K)] * 8,
        in_specs=[SMEM, SMEM, VMEM],
        out_specs=[VMEM] * 8,
        scratch_shapes=[
            pltpu.VMEM((8 * PIECE, K), jnp.bfloat16),
            pltpu.VMEM((8 * 16, K), jnp.float32),
            pltpu.SMEM((8,), jnp.int32),
        ],
        compiler_params=LIMIT,
        name="fold",
    )(where, tiles, own)


def unit_kernel(*refs):
    pieces, out, turn = refs[:8], refs[8], refs[9]
    for k in range(8):
        for s in range(MOST):
            slot = k * MOST + s
            turn[pl.ds(slot, H, stride=UNIT), :] = pieces[k][s * H : (s + 1) * H, :].astype(jnp.float32)
        first = H * UNIT + k * MOST
        turn[first : first + MOST, :] = pieces[k][MOST * H :, :].astype(jnp.float32)[:MOST]
    for a in range(FOLD):
        out[:, a * K : (a + 1) * K] = turn[a * UNIT : (a + 1) * UNIT, :].astype(out.dtype)


def unit_call(pieces):
    return pl.pallas_call(
        unit_kernel,
        out_shape=made(UNIT, WIDTH),
        in_specs=[VMEM] * 8,
        out_specs=VMEM,
        scratch_shapes=[pltpu.VMEM((FOLD * UNIT, K), jnp.float32)],
        compiler_params=LIMIT,
        name="unit",
    )(*[near(p) for p in pieces])


def prepare_kernel(where, primal, dual, right, left, sems):
    at = pl.multiple_of((where[1] * 2 + where[2]) * K, K)
    copies = []
    for t in range(8):
        rows, here = pl.ds(t * K, K), pl.ds(at, K)
        copies.append((dual.at[rows, here], right.at[t, :, pl.ds(0, K)]))
        copies.append((primal.at[rows, here], right.at[t, :, pl.ds(K, K)]))
        copies.append((primal.at[here, rows], left.at[t, :, pl.ds(0, K)]))
        copies.append((dual.at[here, rows], left.at[t, :, pl.ds(K, K)]))
    started = [pltpu.make_async_copy(a, b, sems.at[n]) for n, (a, b) in enumerate(copies)]
    for c in started:
        c.start()
    for c in started:
        c.wait()


def prepare_call(where, primal, dual):
    return pl.pallas_call(
        prepare_kernel,
        out_shape=[made(8, K, 2 * K)] * 2,
        in_specs=[SMEM, HBM, HBM],
        out_specs=[VMEM] * 2,
        scratch_shapes=[pltpu.SemaphoreType.DMA((32,))],
        compiler_params=LIMIT,
        name="prepare",
    )(where, far(primal), far(dual))


STRIDE = 40


def reduce_kernel(plan, chained, where, tiles, right, left, *refs):
    n = len(plan)
    blocks = refs[:n]
    out, *turns = refs[n + (1 if chained else 0) :]
    y, core = where[1], where[2]
    for b, (dy, dcore) in enumerate(plan):
        row = lax.rem(y + dy, 4) * 64 + lax.rem(core + dcore, 2) * 32
        turn = turns[b % 2]
        for m in range(32):
            t = tiles[row + m]
            wide = jnp.dot(blocks[b][m], right[t], preferred_element_type=jnp.float32)
            wide = wide.astype(jnp.bfloat16)
            tall = jnp.concatenate([wide[:, :K], wide[:, K:]], axis=0)
            both = jnp.dot(left[t], tall, preferred_element_type=jnp.float32)
            kept, last = folded(both, True)
            turn[pl.ds(m, H, stride=STRIDE), :] = kept
            turn[H * STRIDE + m : H * STRIDE + m + 1, :] = last
        rows = pl.ds(pl.multiple_of(row, 32), 32)
        for a in range(FOLD):
            part = turn[a * STRIDE : a * STRIDE + 32, :].astype(out.dtype)
            out[rows, a * K : (a + 1) * K] = part


def reduce_call(plan, where, tiles, blocks, right, left, total):
    n = len(blocks)
    args = [where, tiles, near(right), near(left), *[near(b) for b in blocks]]
    specs = [SMEM, SMEM, VMEM, VMEM] + [VMEM] * n
    aliases = {}
    if total is not None:
        aliases = {len(args): 0}
        args.append(near(total))
        specs.append(VMEM)
    return pl.pallas_call(
        functools.partial(reduce_kernel, plan, total is not None),
        out_shape=made(256, WIDTH),
        in_specs=specs,
        out_specs=VMEM,
        scratch_shapes=[
            pltpu.VMEM((FOLD * STRIDE, K), jnp.float32),
            pltpu.VMEM((FOLD * STRIDE, K), jnp.float32),
        ],
        input_output_aliases=aliases,
        compiler_params=LIMIT,
        name="reduced",
    )(*args)


def contract_kernel(n, *refs):
    units, total, outs = refs[:n], refs[n], refs[n + 1 :]
    rows = jnp.concatenate([u[...] for u in units], axis=0) if n > 1 else units[0][...]
    values = lax.dot_general(rows, total[...], NT, preferred_element_type=jnp.float32)
    for m in range(n):
        outs[m][...] = values[m * UNIT : (m + 1) * UNIT]


def contract_call(units, total):
    n = len(units)
    return pl.pallas_call(
        functools.partial(contract_kernel, n),
        out_shape=[made(UNIT, 256, dtype=jnp.float32)] * n,
        in_specs=[VMEM] * (n + 1),
        out_specs=[VMEM] * n,
        compiler_params=LIMIT,
        name="contract",
    )(*[near(u) for u in units], near(total))


def gather_kernel(known, where, *refs):
    values, out = refs[:-1], refs[-1]
    x, z = where[0] // 4, lax.rem(where[0], 4)
    for d, ref in zip(known, values):
        group = lax.rem(x - d[0] + 4, 4) * 4 + lax.rem(z - d[1] + 4, 4)
        out[group] = ref[...]


def gather_call(where, known):
    return pl.pallas_call(
        functools.partial(gather_kernel, tuple(known)),
        out_shape=made(16, UNIT, 256, dtype=jnp.float32),
        in_specs=[SMEM] + [VMEM] * len(known),
        out_specs=VMEM,
        compiler_params=LIMIT,
        name="gather",
    )(where, *[near(v) for v in known.values()])


FORMED_BITS = sum(1 << (d[0] * 4 + d[1]) for d in FORMED)


def final_kernel(where, ids_ref, landed, out):
    line, y, core = where[0], where[1], where[2]
    x, z = line // 4, lax.rem(line, 4)
    target = (y * 2 + core) * 2
    pairs = [ids_ref[pl.ds(2 * n, 2), :] for n in (line, target, target + 1)]
    ids = jnp.concatenate(pairs + [pairs[0]], axis=0)
    lane = lax.broadcasted_iota(jnp.int32, (8, K), 1)
    half = lax.broadcasted_iota(jnp.int32, (8, K), 0) % 2
    ordinal = jnp.zeros((8, K), jnp.int32)
    for s in range(1, 32):
        same = jnp.logical_and(pltpu.roll(ids, s, 1) == ids, (lane & 31) >= s)
        ordinal = ordinal + same.astype(jnp.int32)
    block = half * 4 + (lane >> 5)
    step = ((ids >> 1) - (block >> 1)) & 3
    place = ids * UNIT + step * (2 * MOST) + ((ids + block) & 1) * MOST + ordinal
    columns = place.T
    mine = jnp.concatenate([columns[:, 0:1], columns[:, 1:2]], axis=0)
    slots = lax.broadcasted_iota(jnp.int32, (256, 8 * UNIT), 1)
    for g in range(2):
        goal = target + g
        apart = lax.rem(x - goal // 4 + 4, 4) * 4 + lax.rem(z - lax.rem(goal, 4) + 4, 4)
        straight = (FORMED_BITS >> apart) & 1
        other = jnp.concatenate(
            [columns[:, 2 + 2 * g : 3 + 2 * g], columns[:, 3 + 2 * g : 4 + 2 * g]], axis=0
        )
        hot = (slots == jnp.where(straight > 0, other, mine)).astype(jnp.bfloat16)
        values = jnp.concatenate([landed[c, g] for c in range(8)], axis=0)
        high = values.astype(jnp.bfloat16)
        rest = values - high.astype(jnp.float32)
        low = rest.astype(jnp.bfloat16)
        picked = jnp.dot(hot, high, preferred_element_type=jnp.float32)
        picked = picked + jnp.dot(hot, low, preferred_element_type=jnp.float32)

        @pl.when(straight == 0)
        def _():
            out[:, g * 256 : (g + 1) * 256] = picked

        @pl.when(straight > 0)
        def _():
            out[:, g * 256 : (g + 1) * 256] = picked.T


def final_call(where, ids, landed):
    return pl.pallas_call(
        final_kernel,
        out_shape=jax.ShapeDtypeStruct((256, 512), jnp.float32),
        in_specs=[SMEM, VMEM, VMEM],
        out_specs=VMEM,
        compiler_params=LIMIT,
        name="final",
    )(where, ids, near(landed))


def steps(coeffs, tiles, primal, dual_inverse):
    x, z = lax.axis_index("x"), lax.axis_index("z")
    y, core = lax.axis_index("y"), lax.axis_index("core")
    line = x * 4 + z
    where = jnp.stack([line, y, core]).astype(jnp.int32)
    flat = tiles.reshape(4096)
    line_ids = lax.dynamic_slice_in_dim(flat, line * 256, 256, 0)

    pieces = fold_call(where, flat, coeffs)
    routed = [pieces[0]]
    for k in range(1, 8):
        routed.append(line_shift(pieces[k], k // 2, k % 2))
    units = {(0, 0): unit_call(routed)}
    right, left = prepare_call(where, primal, dual_inverse)

    other = line_shift(coeffs, 0, 1)
    down = line_shift(coeffs, 1, 0)
    up = line_shift(coeffs, 3, 0)
    across = line_shift(coeffs, 2, 0)
    down_other = line_shift(down, 0, 1)
    up_other = line_shift(up, 0, 1)
    across_other = line_shift(across, 0, 1)

    def formed(plan, blocks, total):
        return reduce_call(plan, where, line_ids, blocks, right, left, total)

    total = formed(((0, 0), (0, 1)), [coeffs, other], None)
    plan = ((3, 0), (3, 1), (1, 0), (1, 1))
    total = formed(plan, [down, down_other, up, up_other], total)
    total = formed(((2, 0), (2, 1)), [across, across_other], total)

    for d, parent in FIRST + SECOND + THIRD:
        shift = ((d[0] - parent[0]) % 4, (d[1] - parent[1]) % 4)
        units[d] = plane_shift(units[parent], shift)

    values = contract_call([units[d] for d in EARLY], total)
    known = dict(zip(EARLY, values))
    for d in EARLY:
        if negated(d) in TURNED:
            known[negated(d)] = plane_shift(known[d], negated(d))
    values = contract_call([units[d] for d in LATE], total)
    known.update(zip(LATE, values))
    ordered = gather_call(where, known)
    landed = lax.all_to_all(ordered.reshape(8, 2, UNIT, 256), LINE, 0, 0, tiled=True)

    return final_call(where, tiles.reshape(32, K), landed)


def solution(mesh):
    finer = Mesh(mesh.devices.reshape(4, 4, 4, 2), ALL)
    in_specs = (P(ALL, None, None), P(), P(), P())
    out_specs = P(PLANE, LINE)
    return jax.shard_map(
        steps, mesh=finer, in_specs=in_specs, out_specs=out_specs, check_vma=False
    )
```

time: 170 us -> 148 us (0.87)
  Pallas kernels: 48.4 us -> 26.6 us
  blocking collectives: 0 us -> 19.5 us
  starting transfers between devices: 53.2 us -> 37.5 us
  other arithmetic: 3.21 us -> 0.08 us
  waiting for transfers between devices: 58.7 us -> 56.8 us
    all_to_all x0 -> x1, blocking collectives: none -> 19.5 us  [steps(): lax.all_to_all(ordered.reshape(8, 2, UNIT, 256), LINE, 0, 0, tiled=True)]
    ppermute x15, waiting for transfers between devices: 23.8 us -> 37 us  [plane_shift(): return lax.ppermute(x, PLANE, pairs)]
    pallas_call x4 -> x3, Pallas kernels: 25.8 us -> 12.8 us  [reduce_call(): pl.pallas_call(functools.partial(reduce_kernel, plan, total is not None),...]
    all_to_all x1 -> x0, starting transfers between devices: 8.86 us -> none  [steps(): lax.all_to_all(ordered.reshape(8, 2, UNIT, 256), LINE, 0, 0, tiled=True)]
    pallas_call x5 -> x6, Pallas kernels: 19.6 us -> 11 us  [the longest x2 6.16 us: contract_call(): pl.pallas_call(functools.partial(contract_kernel, n), out_shape=[made(UNI...]
    ppermute x16 -> x14, waiting for transfers between devices: 28.2 us -> 19.8 us  [line_shift(): return lax.ppermute(x, LINE, pairs)]
    ppermute x16 -> x14, starting transfers between devices: 22.3 us -> 14.8 us  [line_shift(): return lax.ppermute(x, LINE, pairs)]
    all_to_all x1 -> x0, waiting for transfers between devices: 6.71 us -> none  [steps(): lax.all_to_all(ordered.reshape(8, 2, UNIT, 256), LINE, 0, 0, tiled=True)]
  transfers between devices with their start and end apart: 32 -> 29, of which waited for: 11 -> 9; matrix products, arithmetic and copies ran while one was open for 3% -> 0% of each run, Pallas kernels for 24% -> 14%
where the time goes in v1:
time: 148 us; the launch traced here: 147 us
  waiting for transfers between devices  56.8 us (38%)
  starting transfers between devices  37.5 us (25%)
  Pallas kernels  26.6 us (18%)
  blocking collectives  19.5 us (13%)
  local copies, waits for them, and re-layouts  6.61 us (4%)
    ppermute x15, waiting for transfers between devices, plane_shift(): return lax.ppermute(x, PLANE, pairs)  37 us
    ppermute x15, starting transfers between devices, plane_shift(): return lax.ppermute(x, PLANE, pairs)  22.7 us
    ppermute x14, waiting for transfers between devices, line_shift(): return lax.ppermute(x, LINE, pairs)  19.8 us
    all_to_all x1, blocking collectives, steps(): lax.all_to_all(ordered.reshape(8, 2, UNIT, 256), LINE, 0, 0, tiled=True)  19.5 us
    ppermute x14, starting transfers between devices, line_shift(): return lax.ppermute(x, LINE, pairs)  14.8 us
    pallas_call x3, Pallas kernels, reduce_call(): pl.pallas_call(functools.partial(reduce_kernel, plan, total is not None),...  12.8 us
    unnamed x28, local copies, waits for them, and re-layouts  6.6 us
    pallas_call x2, Pallas kernels, contract_call(): pl.pallas_call(functools.partial(contract_kernel, n), out_shape=[made(UNI...  6.16 us
  transfers between devices with their start and end apart: 29, of which 9 were waited for; matrix products, arithmetic and copies ran while one was open for 0% of the time, Pallas kernels for 14%

profile of v1, /device:TPU:1, one launch (start us, length us, event | category | flops | bytes accessed | tf_op | source)
XLA Modules:
  0.0 147.5 jit_solution(15655082609754005141)
XLA Ops:
  0.1 0.7 copy-done.12
  0.8 1.9 %fold.1 = (bf16[336,128]{1,0:T(8,128)(2,1)S(1)}, bf16[336,128]{1,0:T(8,128)(2,1)S(1)}, bf16[336,128]{1,0:T(8,128)(2,1)S(1)}, bf16[336,128]{1,0:T(8,128)(2,1)S(1)...) custom-call(s32[3]{0:T(128)S(1)} %pad_add_fusion.where, ...), custom_call_target="tpu_custom_call" | custom-call | tf_op jit(solution)/shard_map/fold/pallas_call | solution.py:115
  2.7 1.5 collective-permute-start
  4.1 1.4 collective-permute-start.1
  5.5 1.5 %collective-permute-start.2 = (bf16[336,128]{1,0:T(8,128)(2,1)S(1)}, bf16[336,128]{1,0:T(8,128)(2,1)S(1)}, u32[]{:S(2)}, u32[]{:S(2)}) collective-permute-start(bf16[336,128]{1,0:T(8,128)(2,1)S(1)} %get-tuple-element.28), channel_id=1, source_target_pairs={{0,3},{1,2},{2,5},{3,4},{4,7},{5,6},{6,1},{7,0},{8,11},{9,10},{10,... | collective-permute-start | bytes 258056 | tf_op jit(solution)/shard_map/ppermute | solution.py:70
  7.1 1.2 collective-permute-start.3
  8.2 2.1 %collective-permute-start.4 = (bf16[336,128]{1,0:T(8,128)(2,1)S(1)}, bf16[336,128]{1,0:T(8,128)(2,1)S(1)}, u32[]{:S(2)}, u32[]{:S(2)}) collective-permute-start(bf16[336,128]{1,0:T(8,128)(2,1)S(1)} %get-tuple-element.30), channel_id=1, source_target_pairs={{0,5},{1,4},{2,7},{3,6},{4,1},{5,0},{6,3},{7,2},{8,13},{9,12},{10,... | collective-permute-start | bytes 258056 | tf_op jit(solution)/shard_map/ppermute | solution.py:70
  10.4 1.4 collective-permute-start.5
  11.8 0.6 collective-permute-start.6
  12.3 1.1 collective-permute-start.15
  13.5 0.9 collective-permute-done.3.refs_4_
  14.4 0.6 collective-permute-start.17
  15.0 1.5 %collective-permute-done.4.refs_5_ = bf16[336,128]{1,0:T(8,128)(2,1)S(1)} collective-permute-done((bf16[336,128]{1,0:T(8,128)(2,1)S(1)}, bf16[336,128]{1,0:T(8,128)(2,1)S(1)}, u32[]{:S(2)}, u32[]{:S(2)}) %collective-permute-start.4) | collective-permute-done | bytes 86048 | tf_op jit(solution)/shard_map/ppermute | solution.py:70
  16.5 2.2 %collective-permute-start.13 = (bf16[32,128,128]{2,1,0:T(8,128)(2,1)}, bf16[32,128,128]{2,1,0:T(8,128)(2,1)S(1)}, u32[]{:S(2)}, u32[]{:S(2)}) collective-permute-start(bf16[32,128,128]{2,1,0:T(8,128)(2,1)} %refs_0_.1), channel_id=1, source_target_pairs={{0,4},{1,5},{2,6},{3,7},{4,0},{5,1},{6,2},{7,3},{8,12},{9,13},{10,... | collective-permute-start | bytes 3145736 | tf_op jit(solution)/shard_map/ppermute | solution.py:70
  19.1 3.9 %collective-permute-start.9 = (bf16[40,8320]{1,0:T(8,128)(2,1)S(1)}, bf16[40,8320]{1,0:T(8,128)(2,1)S(1)}, u32[]{:S(2)}, u32[]{:S(2)}) collective-permute-start(bf16[40,8320]{1,0:T(8,128)(2,1)S(1)} %unit.1.refs_0_), channel_id=1, source_target_pairs={{0,104},{8,112},{16,120},{24,96},{32,8},{40,16},{48,24},{56,0},{64... | collective-permute-start | bytes 1996808 | tf_op jit(solution)/shard_map/ppermute | solution.py:62
  23.0 16.1 %collective-permute-done.9.refs_3_ = bf16[40,8320]{1,0:T(8,128)(2,1)S(1)} collective-permute-done((bf16[40,8320]{1,0:T(8,128)(2,1)S(1)}, bf16[40,8320]{1,0:T(8,128)(2,1)S(1)}, u32[]{:S(2)}, u32[]{:S(2)}) %collective-permute-start.9) | collective-permute-done | bytes 665632 | tf_op jit(solution)/shard_map/ppermute | solution.py:62
  39.1 1.8 %collective-permute-start.8 = (bf16[40,8320]{1,0:T(8,128)(2,1)S(1)}, bf16[40,8320]{1,0:T(8,128)(2,1)}, u32[]{:S(2)}, u32[]{:S(2)}) collective-permute-start(bf16[40,8320]{1,0:T(8,128)(2,1)S(1)} %unit.1.refs_0_), channel_id=1, source_target_pairs={{0,24},{8,0},{16,8},{24,16},{32,56},{40,32},{48,40},{56,48},{64,88... | collective-permute-start | bytes 1996808 | tf_op jit(solution)/shard_map/ppermute | solution.py:62
  41.0 0.7 collective-permute-start.19
  41.7 1.0 copy-done.2
  42.7 0.5 collective-permute-start.18
  43.2 1.0 copy-done.4
  44.2 17.4 %collective-permute-done.13.refs_0_ = bf16[32,128,128]{2,1,0:T(8,128)(2,1)S(1)} collective-permute-done((bf16[32,128,128]{2,1,0:T(8,128)(2,1)}, bf16[32,128,128]{2,1,0:T(8,128)(2,1)S(1)}, u32[]{:S(2)}, u32[]{:S(2)}) %collective-permute-start.13) | collective-permute-done | bytes 1048608 | tf_op jit(solution)/shard_map/ppermute | solution.py:70
  61.6 1.6 %collective-permute-start.11 = (bf16[40,8320]{1,0:T(8,128)(2,1)S(1)}, bf16[40,8320]{1,0:T(8,128)(2,1)}, u32[]{:S(2)}, u32[]{:S(2)}) collective-permute-start(bf16[40,8320]{1,0:T(8,128)(2,1)S(1)} %collective-permute-done.9.refs_3_), channel_id=1, source_target_pairs={{0,8},{8,16},{16,24},{24,0},{32,40},{40,48},{48,56},{56,32},{64,72... | collective-permute-start | bytes 1996808 | tf_op jit(solution)/shard_map/ppermute | solution.py:62
  63.2 0.9 copy-done.10
  64.1 1.0 copy-done
  65.2 2.5 %collective-permute-start.10 = (bf16[40,8320]{1,0:T(8,128)(2,1)}, bf16[40,8320]{1,0:T(8,128)(2,1)}, u32[]{:S(2)}, u32[]{:S(2)}) collective-permute-start(bf16[40,8320]{1,0:T(8,128)(2,1)} %collective-permute-done.8.refs_2_), channel_id=1, source_target_pairs={{0,96},{8,104},{16,112},{24,120},{32,0},{40,8},{48,16},{56,24},{64... | collective-permute-start | bytes 1996808 | tf_op jit(solution)/shard_map/ppermute | solution.py:62
  67.6 12.6 %collective-permute-done.11.refs_5_ = bf16[40,8320]{1,0:T(8,128)(2,1)} collective-permute-done((bf16[40,8320]{1,0:T(8,128)(2,1)S(1)}, bf16[40,8320]{1,0:T(8,128)(2,1)}, u32[]{:S(2)}, u32[]{:S(2)}) %collective-permute-start.11) | collective-permute-done | bytes 665632 | tf_op jit(solution)/shard_map/ppermute | solution.py:62
  80.3 2.1 %collective-permute-start.12 = (bf16[40,8320]{1,0:T(8,128)(2,1)}, bf16[40,8320]{1,0:T(8,128)(2,1)}, u32[]{:S(2)}, u32[]{:S(2)}) collective-permute-start(bf16[40,8320]{1,0:T(8,128)(2,1)} %collective-permute-done.7.refs_1_), channel_id=1, source_target_pairs={{0,56},{8,32},{16,40},{24,48},{32,88},{40,64},{48,72},{56,80},{64,... | collective-permute-start | bytes 1996808 | tf_op jit(solution)/shard_map/ppermute | solution.py:62
  82.4 1.0 copy-done.6
  83.4 1.2 collective-permute-start.26
  84.6 1.0 copy-done.8
  85.7 1.5 collective-permute-start.28
  87.2 2.0 %prepare.1 = (bf16[8,128,256]{2,1,0:T(8,128)(2,1)S(1)}, bf16[8,128,256]{2,1,0:T(8,128)(2,1)S(1)}) custom-call(s32[3]{0:T(128)S(1)} %pad_add_fusion.where, bf16[1024,1024]{1,0:T(8,128)(2,1)} %primal.1, bf16[1024,1024]{1,0:T(8,128)(2,1)} %dual.1), custom_call_target="tpu_custom_call" | custom-call | tf_op jit(solution)/shard_map/prepare/pallas_call | solution.py:171
  89.3 4.1 %reduced.3.refs_4_ = bf16[256,8320]{1,0:T(8,128)(2,1)S(1)} custom-call(s32[3]{0:T(128)S(1)} %pad_add_fusion.where, s32[256]{0:T(256)S(1)} %bitcast.10, bf16[8,128,256]{2,1,0:T(8,128)(2,1)S(1)} %get-tuple-element.33.right, bf16[8,128,256]{2,1,0:T(8,128)(2,1)S(1)} %get-tuple-element.34.left, bf16[32,128,128]{2,1,0:T(8,128)(2,1)} %refs_0_.1, ...), custom_call_target="tpu_custom_call" | custom-call | tf_op jit(solution)/shard_map/reduced/pallas_call | solution.py:217
  93.4 5.5 %reduced.4.refs_2_ = bf16[256,8320]{1,0:T(8,128)(2,1)S(1)} custom-call(s32[3]{0:T(128)S(1)} %pad_add_fusion.where, s32[256]{0:T(256)S(1)} %bitcast.11, bf16[8,128,256]{2,1,0:T(8,128)(2,1)S(1)} %get-tuple-element.33.right, bf16[8,128,256]{2,1,0:T(8,128)(2,1)S(1)} %get-tuple-element.34.left, ...), custom_call_target="tpu_custom_call", output_to_operand_aliasing={{}: (8, {})} | custom-call | tf_op jit(solution)/shard_map/reduced/pallas_call | solution.py:217
  98.9 3.2 %reduced.5.refs_7_.refs_3_ = bf16[256,8320]{1,0:T(8,128)(2,1)S(1)} custom-call(s32[3]{0:T(128)S(1)} %pad_add_fusion.where, s32[256]{0:T(256)S(1)} %bitcast.12, bf16[8,128,256]{2,1,0:T(8,128)(2,1)S(1)} %get-tuple-element.33.right, bf16[8,128,256]{2,1,0:T(8,128)(2,1)S(1)} %get-tuple-element.34.left, ...), custom_call_target="tpu_custom_call", output_to_operand_aliasing={{}: (6, {})} | custom-call | tf_op jit(solution)/shard_map/reduced/pallas_call | solution.py:217
  102.2 3.4 %contract.2 = (f32[40,256]{1,0:T(8,128)S(1)}, f32[40,256]{1,0:T(8,128)S(1)}, f32[40,256]{1,0:T(8,128)S(1)}, f32[40,256]{1,0:T(8,128)S(1)}, f32[40,256]{1,0:T(8,1...) custom-call(bf16[40,8320]{1,0:T(8,128)(2,1)S(1)} %unit.1.refs_0_, ...), custom_call_target="tpu_custom_call" | custom-call | tf_op jit(solution)/shard_map/contract/pallas_call | solution.py:242
  105.9 1.4 collective-permute-start.21
  107.3 4.8 %collective-permute-done.26.refs_0_ = bf16[40,8320]{1,0:T(8,128)(2,1)S(1)} collective-permute-done((bf16[40,8320]{1,0:T(8,128)(2,1)}, bf16[40,8320]{1,0:T(8,128)(2,1)S(1)}, u32[]{:S(2)}, u32[]{:S(2)}) %collective-permute-start.26) | collective-permute-done | bytes 665632 | tf_op jit(solution)/shard_map/ppermute | solution.py:62
  112.1 1.8 %collective-permute-done.27.refs_1_ = bf16[40,8320]{1,0:T(8,128)(2,1)} collective-permute-done((bf16[40,8320]{1,0:T(8,128)(2,1)}, bf16[40,8320]{1,0:T(8,128)(2,1)}, u32[]{:S(2)}, u32[]{:S(2)}) %collective-permute-start.27) | collective-permute-done | bytes 665632 | tf_op jit(solution)/shard_map/ppermute | solution.py:62
  113.8 0.4 collective-permute-start.23
  114.3 3.8 %collective-permute-start.24 = (f32[40,256]{1,0:T(8,128)S(1)}, f32[40,256]{1,0:T(8,128)S(1)}, u32[]{:S(2)}, u32[]{:S(2)}) collective-permute-start(f32[40,256]{1,0:T(8,128)S(1)} %get-tuple-element.40.refs_5_), channel_id=1, source_target_pairs={{0,48},{8,56},{16,32},{24,40},{32,80},{40,88},{48,64},{56,72},{64,... | collective-permute-start | bytes 122888 | tf_op jit(solution)/shard_map/ppermute | solution.py:62
  118.1 2.0 %collective-permute-start.25 = (f32[40,256]{1,0:T(8,128)S(1)}, f32[40,256]{1,0:T(8,128)S(1)}, u32[]{:S(2)}, u32[]{:S(2)}) collective-permute-start(f32[40,256]{1,0:T(8,128)S(1)} %get-tuple-element.41.refs_6_), channel_id=1, source_target_pairs={{0,72},{8,80},{16,88},{24,64},{32,104},{40,112},{48,120},{56,96},{... | collective-permute-start | bytes 122888 | tf_op jit(solution)/shard_map/ppermute | solution.py:62
  120.1 2.8 %contract.3 = (f32[40,256]{1,0:T(8,128)S(1)}, f32[40,256]{1,0:T(8,128)S(1)}, f32[40,256]{1,0:T(8,128)S(1)}) custom-call(bf16[40,8320]{1,0:T(8,128)(2,1)S(1)} %collective-permute-done.26.refs_0_, bf16[40,8320]{1,0:T(8,128)(2,1)} %collective-permute-done.27.refs_1_, bf16[40,8320]{1,0:T(8,128)(2,1)} %collective-permute-done.28.refs_2_, ...), custom_call_target="tpu_custom_call" | custom-call | tf_op jit(solution)/shard_map/contract/pallas_call | solution.py:242
  123.0 1.6 %collective-permute-done.25.refs_12_ = f32[40,256]{1,0:T(8,128)S(1)} collective-permute-done((f32[40,256]{1,0:T(8,128)S(1)}, f32[40,256]{1,0:T(8,128)S(1)}, u32[]{:S(2)}, u32[]{:S(2)}) %collective-permute-start.25) | collective-permute-done | bytes 40992 | tf_op jit(solution)/shard_map/ppermute | solution.py:62
  124.5 0.6 gather.1
  125.2 19.5 %all_to_all.5.landed = f32[8,2,40,256]{3,2,1,0:T(8,128)S(1)} all-to-all(f32[8,2,40,256]{3,2,1,0:T(8,128)S(1)} %bitcast.7), channel_id=1, replica_groups=mesh['x'=4,'z'=4,'y'=4,'core'=2] {'y','core'}, dimensions={0} | all-to-all | bytes 1310720 | tf_op jit(solution)/shard_map/all_to_all | solution.py:370
  144.7 2.8 %final.1 = f32[256,512]{1,0:T(8,128)} custom-call(s32[3]{0:T(128)S(1)} %pad_add_fusion.where, s32[32,128]{1,0:T(8,128)S(1)} %bitcast.9, f32[8,2,40,256]{3,2,1,0:T(8,128)S(1)} %all_to_all.5.landed), custom_call_target="tpu_custom_call" | custom-call | tf_op jit(solution)/shard_map/final/pallas_call | solution.py:317
  (51 shorter events, 1.1 us)
Async XLA Ops:
  0.0 89.2 %copy-start.13 = (s32[4096,1]{0,1:T(1,128)S(1)}, s32[4096,1]{0,1:T(1,128)}, u32[]{:S(2)}) copy-start(s32[4096,1]{0,1:T(1,128)} %param.5) | copy-start | bytes 49156
  0.1 0.7 copy-start.12
  2.7 7.7 %collective-permute-start = (bf16[336,128]{1,0:T(8,128)(2,1)S(1)}, bf16[336,128]{1,0:T(8,128)(2,1)S(1)}, u32[]{:S(2)}, u32[]{:S(2)}) collective-permute-start(bf16[336,128]{1,0:T(8,128)(2,1)S(1)} %get-tuple-element.26), channel_id=1, source_target_pairs={{0,1},{1,0},{2,3},{3,2},{4,5},{5,4},{6,7},{7,6},{8,9},{9,8},{10,11... | collective-permute-start | bytes 258056 | tf_op jit(solution)/shard_map/ppermute | solution.py:70
  4.1 7.6 %collective-permute-start.1 = (bf16[336,128]{1,0:T(8,128)(2,1)S(1)}, bf16[336,128]{1,0:T(8,128)(2,1)S(1)}, u32[]{:S(2)}, u32[]{:S(2)}) collective-permute-start(bf16[336,128]{1,0:T(8,128)(2,1)S(1)} %get-tuple-element.27), channel_id=1, source_target_pairs={{0,2},{1,3},{2,4},{3,5},{4,6},{5,7},{6,0},{7,1},{8,10},{9,11},{10,... | collective-permute-start | bytes 258056 | tf_op jit(solution)/shard_map/ppermute | solution.py:70
  5.5 6.8 %collective-permute-start.2 = (bf16[336,128]{1,0:T(8,128)(2,1)S(1)}, bf16[336,128]{1,0:T(8,128)(2,1)S(1)}, u32[]{:S(2)}, u32[]{:S(2)}) collective-permute-start(bf16[336,128]{1,0:T(8,128)(2,1)S(1)} %get-tuple-element.28), channel_id=1, source_target_pairs={{0,3},{1,2},{2,5},{3,4},{4,7},{5,6},{6,1},{7,0},{8,11},{9,10},{10,... | collective-permute-start | bytes 258056 | tf_op jit(solution)/shard_map/ppermute | solution.py:70
  7.1 7.3 %collective-permute-start.3 = (bf16[336,128]{1,0:T(8,128)(2,1)S(1)}, bf16[336,128]{1,0:T(8,128)(2,1)S(1)}, u32[]{:S(2)}, u32[]{:S(2)}) collective-permute-start(bf16[336,128]{1,0:T(8,128)(2,1)S(1)} %get-tuple-element.29), channel_id=1, source_target_pairs={{0,4},{1,5},{2,6},{3,7},{4,0},{5,1},{6,2},{7,3},{8,12},{9,13},{10,... | collective-permute-start | bytes 258056 | tf_op jit(solution)/shard_map/ppermute | solution.py:70
  8.2 8.3 %collective-permute-start.4 = (bf16[336,128]{1,0:T(8,128)(2,1)S(1)}, bf16[336,128]{1,0:T(8,128)(2,1)S(1)}, u32[]{:S(2)}, u32[]{:S(2)}) collective-permute-start(bf16[336,128]{1,0:T(8,128)(2,1)S(1)} %get-tuple-element.30), channel_id=1, source_target_pairs={{0,5},{1,4},{2,7},{3,6},{4,1},{5,0},{6,3},{7,2},{8,13},{9,12},{10,... | collective-permute-start | bytes 258056 | tf_op jit(solution)/shard_map/ppermute | solution.py:70
  10.4 8.3 %collective-permute-start.5 = (bf16[336,128]{1,0:T(8,128)(2,1)S(1)}, bf16[336,128]{1,0:T(8,128)(2,1)S(1)}, u32[]{:S(2)}, u32[]{:S(2)}) collective-permute-start(bf16[336,128]{1,0:T(8,128)(2,1)S(1)} %get-tuple-element.31), channel_id=1, source_target_pairs={{0,6},{1,7},{2,0},{3,1},{4,2},{5,3},{6,4},{7,5},{8,14},{9,15},{10,... | collective-permute-start | bytes 258056 | tf_op jit(solution)/shard_map/ppermute | solution.py:70
  11.8 7.0 %collective-permute-start.6 = (bf16[336,128]{1,0:T(8,128)(2,1)S(1)}, bf16[336,128]{1,0:T(8,128)(2,1)S(1)}, u32[]{:S(2)}, u32[]{:S(2)}) collective-permute-start(bf16[336,128]{1,0:T(8,128)(2,1)S(1)} %get-tuple-element.32), channel_id=1, source_target_pairs={{0,7},{1,6},{2,1},{3,0},{4,3},{5,2},{6,5},{7,4},{8,15},{9,14},{10,... | collective-permute-start | bytes 258056 | tf_op jit(solution)/shard_map/ppermute | solution.py:70
  12.3 29.3 %collective-permute-start.15 = (bf16[32,128,128]{2,1,0:T(8,128)(2,1)}, bf16[32,128,128]{2,1,0:T(8,128)(2,1)S(1)}, u32[]{:S(2)}, u32[]{:S(2)}) collective-permute-start(bf16[32,128,128]{2,1,0:T(8,128)(2,1)} %refs_0_.1), channel_id=1, source_target_pairs={{0,2},{1,3},{2,4},{3,5},{4,6},{5,7},{6,0},{7,1},{8,10},{9,11},{10,... | collective-permute-start | bytes 3145736 | tf_op jit(solution)/shard_map/ppermute | solution.py:70
  14.4 28.3 %collective-permute-start.17 = (bf16[32,128,128]{2,1,0:T(8,128)(2,1)}, bf16[32,128,128]{2,1,0:T(8,128)(2,1)S(1)}, u32[]{:S(2)}, u32[]{:S(2)}) collective-permute-start(bf16[32,128,128]{2,1,0:T(8,128)(2,1)} %refs_0_.1), channel_id=1, source_target_pairs={{0,6},{1,7},{2,0},{3,1},{4,2},{5,3},{6,4},{7,5},{8,14},{9,15},{10,... | collective-permute-start | bytes 3145736 | tf_op jit(solution)/shard_map/ppermute | solution.py:70
  16.5 45.1 %collective-permute-start.13 = (bf16[32,128,128]{2,1,0:T(8,128)(2,1)}, bf16[32,128,128]{2,1,0:T(8,128)(2,1)S(1)}, u32[]{:S(2)}, u32[]{:S(2)}) collective-permute-start(bf16[32,128,128]{2,1,0:T(8,128)(2,1)} %refs_0_.1), channel_id=1, source_target_pairs={{0,4},{1,5},{2,6},{3,7},{4,0},{5,1},{6,2},{7,3},{8,12},{9,13},{10,... | collective-permute-start | bytes 3145736 | tf_op jit(solution)/shard_map/ppermute | solution.py:70
  19.1 20.0 %collective-permute-start.9 = (bf16[40,8320]{1,0:T(8,128)(2,1)S(1)}, bf16[40,8320]{1,0:T(8,128)(2,1)S(1)}, u32[]{:S(2)}, u32[]{:S(2)}) collective-permute-start(bf16[40,8320]{1,0:T(8,128)(2,1)S(1)} %unit.1.refs_0_), channel_id=1, source_target_pairs={{0,104},{8,112},{16,120},{24,96},{32,8},{40,16},{48,24},{56,0},{64... | collective-permute-start | bytes 1996808 | tf_op jit(solution)/shard_map/ppermute | solution.py:62
  23.0 18.0 %collective-permute-start.7 = (bf16[40,8320]{1,0:T(8,128)(2,1)S(1)}, bf16[40,8320]{1,0:T(8,128)(2,1)}, u32[]{:S(2)}, u32[]{:S(2)}) collective-permute-start(bf16[40,8320]{1,0:T(8,128)(2,1)S(1)} %unit.1.refs_0_), channel_id=1, source_target_pairs={{0,32},{8,40},{16,48},{24,56},{32,64},{40,72},{48,80},{56,88},{64,... | collective-permute-start | bytes 1996808 | tf_op jit(solution)/shard_map/ppermute | solution.py:62
  39.1 22.5 %collective-permute-start.8 = (bf16[40,8320]{1,0:T(8,128)(2,1)S(1)}, bf16[40,8320]{1,0:T(8,128)(2,1)}, u32[]{:S(2)}, u32[]{:S(2)}) collective-permute-start(bf16[40,8320]{1,0:T(8,128)(2,1)S(1)} %unit.1.refs_0_), channel_id=1, source_target_pairs={{0,24},{8,0},{16,8},{24,16},{32,56},{40,32},{48,40},{56,48},{64,88... | collective-permute-start | bytes 1996808 | tf_op jit(solution)/shard_map/ppermute | solution.py:62
  41.0 23.1 %collective-permute-start.19 = (bf16[32,128,128]{2,1,0:T(8,128)(2,1)}, bf16[32,128,128]{2,1,0:T(8,128)(2,1)S(1)}, u32[]{:S(2)}, u32[]{:S(2)}) collective-permute-start(bf16[32,128,128]{2,1,0:T(8,128)(2,1)} %refs_0_.1), channel_id=1, source_target_pairs={{0,1},{1,0},{2,3},{3,2},{4,5},{5,4},{6,7},{7,6},{8,9},{9,8},{10,11... | collective-permute-start | bytes 3145736 | tf_op jit(solution)/shard_map/ppermute | solution.py:70
  41.7 40.7 %collective-permute-start.16 = (bf16[32,128,128]{2,1,0:T(8,128)(2,1)S(1)}, bf16[32,128,128]{2,1,0:T(8,128)(2,1)S(1)}, u32[]{:S(2)}, u32[]{:S(2)}) collective-permute-start(bf16[32,128,128]{2,1,0:T(8,128)(2,1)S(1)} %collective-permute-done.15.refs_0_), channel_id=1, source_target_pairs={{0,1},{1,0},{2,3},{3,2},{4,5},{5,4},{6,7},{7,6},{8,9},{9,8},{10,11... | collective-permute-start | bytes 3145736 | tf_op jit(solution)/shard_map/ppermute | solution.py:70
  41.7 1.0 copy-start.2
  42.7 41.9 %collective-permute-start.18 = (bf16[32,128,128]{2,1,0:T(8,128)(2,1)S(1)}, bf16[32,128,128]{2,1,0:T(8,128)(2,1)S(1)}, u32[]{:S(2)}, u32[]{:S(2)}) collective-permute-start(bf16[32,128,128]{2,1,0:T(8,128)(2,1)S(1)} %collective-permute-done.17.refs_2_), channel_id=1, source_target_pairs={{0,1},{1,0},{2,3},{3,2},{4,5},{5,4},{6,7},{7,6},{8,9},{9,8},{10,11... | collective-permute-start | bytes 3145736 | tf_op jit(solution)/shard_map/ppermute | solution.py:70
  43.2 1.0 copy-start.4
  61.6 24.1 %collective-permute-start.14 = (bf16[32,128,128]{2,1,0:T(8,128)(2,1)S(1)}, bf16[32,128,128]{2,1,0:T(8,128)(2,1)S(1)}, u32[]{:S(2)}, u32[]{:S(2)}) collective-permute-start(bf16[32,128,128]{2,1,0:T(8,128)(2,1)S(1)} %collective-permute-done.13.refs_0_), channel_id=1, source_target_pairs={{0,1},{1,0},{2,3},{3,2},{4,5},{5,4},{6,7},{7,6},{8,9},{9,8},{10,11... | collective-permute-start | bytes 3145736 | tf_op jit(solution)/shard_map/ppermute | solution.py:70
  61.6 18.7 %collective-permute-start.11 = (bf16[40,8320]{1,0:T(8,128)(2,1)S(1)}, bf16[40,8320]{1,0:T(8,128)(2,1)}, u32[]{:S(2)}, u32[]{:S(2)}) collective-permute-start(bf16[40,8320]{1,0:T(8,128)(2,1)S(1)} %collective-permute-done.9.refs_3_), channel_id=1, source_target_pairs={{0,8},{8,16},{16,24},{24,0},{32,40},{40,48},{48,56},{56,32},{64,72... | collective-permute-start | bytes 1996808 | tf_op jit(solution)/shard_map/ppermute | solution.py:62
  63.2 0.9 copy-start.10
  64.1 1.0 copy-start
  65.2 37.0 %collective-permute-start.10 = (bf16[40,8320]{1,0:T(8,128)(2,1)}, bf16[40,8320]{1,0:T(8,128)(2,1)}, u32[]{:S(2)}, u32[]{:S(2)}) collective-permute-start(bf16[40,8320]{1,0:T(8,128)(2,1)} %collective-permute-done.8.refs_2_), channel_id=1, source_target_pairs={{0,96},{8,104},{16,112},{24,120},{32,0},{40,8},{48,16},{56,24},{64... | collective-permute-start | bytes 1996808 | tf_op jit(solution)/shard_map/ppermute | solution.py:62
  80.3 21.9 %collective-permute-start.12 = (bf16[40,8320]{1,0:T(8,128)(2,1)}, bf16[40,8320]{1,0:T(8,128)(2,1)}, u32[]{:S(2)}, u32[]{:S(2)}) collective-permute-start(bf16[40,8320]{1,0:T(8,128)(2,1)} %collective-permute-done.7.refs_1_), channel_id=1, source_target_pairs={{0,56},{8,32},{16,40},{24,48},{32,88},{40,64},{48,72},{56,80},{64,... | collective-permute-start | bytes 1996808 | tf_op jit(solution)/shard_map/ppermute | solution.py:62
  82.4 1.0 copy-start.6
  83.4 28.7 %collective-permute-start.26 = (bf16[40,8320]{1,0:T(8,128)(2,1)}, bf16[40,8320]{1,0:T(8,128)(2,1)S(1)}, u32[]{:S(2)}, u32[]{:S(2)}) collective-permute-start(bf16[40,8320]{1,0:T(8,128)(2,1)} %collective-permute-done.7.refs_1_), channel_id=1, source_target_pairs={{0,32},{8,40},{16,48},{24,56},{32,64},{40,72},{48,80},{56,88},{64,... | collective-permute-start | bytes 1996808 | tf_op jit(solution)/shard_map/ppermute | solution.py:62
  84.6 1.0 copy-start.8
  85.6 28.3 %collective-permute-start.27 = (bf16[40,8320]{1,0:T(8,128)(2,1)}, bf16[40,8320]{1,0:T(8,128)(2,1)}, u32[]{:S(2)}, u32[]{:S(2)}) collective-permute-start(bf16[40,8320]{1,0:T(8,128)(2,1)} %collective-permute-done.8.refs_2_), channel_id=1, source_target_pairs={{0,24},{8,0},{16,8},{24,16},{32,56},{40,32},{48,40},{56,48},{64,88... | collective-permute-start | bytes 1996808 | tf_op jit(solution)/shard_map/ppermute | solution.py:62
  85.7 28.6 %collective-permute-start.28 = (bf16[40,8320]{1,0:T(8,128)(2,1)}, bf16[40,8320]{1,0:T(8,128)(2,1)}, u32[]{:S(2)}, u32[]{:S(2)}) collective-permute-start(bf16[40,8320]{1,0:T(8,128)(2,1)} %collective-permute-done.11.refs_5_), channel_id=1, source_target_pairs={{0,96},{8,104},{16,112},{24,120},{32,0},{40,8},{48,16},{56,24},{64... | collective-permute-start | bytes 1996808 | tf_op jit(solution)/shard_map/ppermute | solution.py:62
  87.2 2.1 %copy-start.1 = (bf16[32,128,128]{2,1,0:T(8,128)(2,1)S(1)}, bf16[32,128,128]{2,1,0:T(8,128)(2,1)}, u32[]{:S(2)}) copy-start(bf16[32,128,128]{2,1,0:T(8,128)(2,1)} %copy-done) | copy-start | bytes 3145732
  89.2 4.1 %copy-start.3 = (bf16[32,128,128]{2,1,0:T(8,128)(2,1)S(1)}, bf16[32,128,128]{2,1,0:T(8,128)(2,1)}, u32[]{:S(2)}) copy-start(bf16[32,128,128]{2,1,0:T(8,128)(2,1)} %copy-done.2) | copy-start | bytes 3145732
  89.2 4.1 %copy-start.5 = (bf16[32,128,128]{2,1,0:T(8,128)(2,1)S(1)}, bf16[32,128,128]{2,1,0:T(8,128)(2,1)}, u32[]{:S(2)}) copy-start(bf16[32,128,128]{2,1,0:T(8,128)(2,1)} %copy-done.4) | copy-start | bytes 3145732
  89.2 4.1 %copy-start.7 = (bf16[32,128,128]{2,1,0:T(8,128)(2,1)S(1)}, bf16[32,128,128]{2,1,0:T(8,128)(2,1)}, u32[]{:S(2)}) copy-start(bf16[32,128,128]{2,1,0:T(8,128)(2,1)} %copy-done.6) | copy-start | bytes 3145732
  89.2 4.1 %copy-start.9 = (bf16[32,128,128]{2,1,0:T(8,128)(2,1)S(1)}, bf16[32,128,128]{2,1,0:T(8,128)(2,1)}, u32[]{:S(2)}) copy-start(bf16[32,128,128]{2,1,0:T(8,128)(2,1)} %copy-done.8) | copy-start | bytes 3145732
  98.9 3.3 %copy-start.11 = (bf16[40,8320]{1,0:T(8,128)(2,1)S(1)}, bf16[40,8320]{1,0:T(8,128)(2,1)}, u32[]{:S(2)}) copy-start(bf16[40,8320]{1,0:T(8,128)(2,1)} %copy-done.10) | copy-start | bytes 1996804
  105.5 12.5 %collective-permute-start.20 = (f32[40,256]{1,0:T(8,128)S(1)}, f32[40,256]{1,0:T(8,128)S(1)}, u32[]{:S(2)}, u32[]{:S(2)}) collective-permute-start(f32[40,256]{1,0:T(8,128)S(1)} %get-tuple-element.36.refs_1_), channel_id=1, source_target_pairs={{0,96},{8,104},{16,112},{24,120},{32,0},{40,8},{48,16},{56,24},{64... | collective-permute-start | bytes 122888 | tf_op jit(solution)/shard_map/ppermute | solution.py:62
  105.9 17.1 %collective-permute-start.21 = (f32[40,256]{1,0:T(8,128)S(1)}, f32[40,256]{1,0:T(8,128)S(1)}, u32[]{:S(2)}, u32[]{:S(2)}) collective-permute-start(f32[40,256]{1,0:T(8,128)S(1)} %get-tuple-element.37.refs_2_), channel_id=1, source_target_pairs={{0,8},{8,16},{16,24},{24,0},{32,40},{40,48},{48,56},{56,32},{64,72... | collective-permute-start | bytes 122888 | tf_op jit(solution)/shard_map/ppermute | solution.py:62
  112.1 10.9 %collective-permute-start.22 = (f32[40,256]{1,0:T(8,128)S(1)}, f32[40,256]{1,0:T(8,128)S(1)}, u32[]{:S(2)}, u32[]{:S(2)}) collective-permute-start(f32[40,256]{1,0:T(8,128)S(1)} %get-tuple-element.38.refs_3_), channel_id=1, source_target_pairs={{0,56},{8,32},{16,40},{24,48},{32,88},{40,64},{48,72},{56,80},{64,... | collective-permute-start | bytes 122888 | tf_op jit(solution)/shard_map/ppermute | solution.py:62
  113.8 9.1 %collective-permute-start.23 = (f32[40,256]{1,0:T(8,128)S(1)}, f32[40,256]{1,0:T(8,128)S(1)}, u32[]{:S(2)}, u32[]{:S(2)}) collective-permute-start(f32[40,256]{1,0:T(8,128)S(1)} %get-tuple-element.39.refs_4_), channel_id=1, source_target_pairs={{0,40},{8,48},{16,56},{24,32},{32,72},{40,80},{48,88},{56,64},{64,... | collective-permute-start | bytes 122888 | tf_op jit(solution)/shard_map/ppermute | solution.py:62
  114.3 8.7 %collective-permute-start.24 = (f32[40,256]{1,0:T(8,128)S(1)}, f32[40,256]{1,0:T(8,128)S(1)}, u32[]{:S(2)}, u32[]{:S(2)}) collective-permute-start(f32[40,256]{1,0:T(8,128)S(1)} %get-tuple-element.40.refs_5_), channel_id=1, source_target_pairs={{0,48},{8,56},{16,32},{24,40},{32,80},{40,88},{48,64},{56,72},{64,... | collective-permute-start | bytes 122888 | tf_op jit(solution)/shard_map/ppermute | solution.py:62
  118.1 6.5 %collective-permute-start.25 = (f32[40,256]{1,0:T(8,128)S(1)}, f32[40,256]{1,0:T(8,128)S(1)}, u32[]{:S(2)}, u32[]{:S(2)}) collective-permute-start(f32[40,256]{1,0:T(8,128)S(1)} %get-tuple-element.41.refs_6_), channel_id=1, source_target_pairs={{0,72},{8,80},{16,88},{24,64},{32,104},{40,112},{48,120},{56,96},{... | collective-permute-start | bytes 122888 | tf_op jit(solution)/shard_map/ppermute | solution.py:62

commit v2 on v1

--- a/solution.py
+++ b/solution.py
@@ -40,11 +40,12 @@
 
 
 FIRST = (((1, 0), (0, 0)), ((0, 3), (0, 0)), ((3, 1), (0, 0)))
-SECOND = (((3, 3), (0, 3)), ((3, 2), (3, 1)), ((2, 3), (1, 0)))
-THIRD = (((2, 0), (1, 0)), ((0, 2), (0, 3)), ((2, 2), (3, 2)))
+SECOND = (((3, 2), (3, 1)), ((2, 1), (3, 1)), ((2, 0), (1, 0)), ((0, 2), (0, 3)))
+THIRD = (((1, 1), (1, 0)), ((2, 2), (3, 2)))
 EARLY = ((0, 0),) + tuple(d for d, _ in FIRST + SECOND)
-LATE = tuple(d for d, _ in THIRD)
-FORMED = EARLY + LATE
+MIDDLE = ((1, 1),)
+LATE = ((2, 2),)
+FORMED = EARLY + MIDDLE + LATE
 
 
 def negated(d):
@@ -83,8 +84,20 @@
     return kept, last
 
 
+def unfolded(kept, last):
+    row = lax.broadcasted_iota(jnp.int32, (H, K), 0)
+    lane = lax.broadcasted_iota(jnp.int32, (H, K), 1)
+    turned = kept.T
+    wide = jnp.concatenate([turned, turned], axis=1)
+    head, tail = wide[:H], wide[H:]
+    top = jnp.where(jnp.logical_and(lane < H, row > lane), head, kept)
+    corner = pltpu.roll(jnp.where(row > lane, kept, head), H, 1)
+    right = jnp.where(lane == row + H, last, corner)
+    return jnp.concatenate([top, jnp.where(lane < H, tail, right)], axis=0)
+
+
 def fold_kernel(where, tiles, own_ref, *refs):
-    outs, held, lasts, counts = refs[:8], refs[8], refs[9], refs[10]
+    outs, plain, held, lasts, ends, counts = refs[:8], *refs[8:]
     held[...] = jnp.zeros(held.shape, held.dtype)
     lasts[...] = jnp.zeros(lasts.shape, lasts.dtype)
     for k in range(8):
@@ -101,11 +114,15 @@
             goal = lax.rem(t // 2 - y + 4, 4) * 2 + lax.rem(t + core, 2)
             kept, last = folded(own_ref[i].astype(jnp.float32), False)
             row = pl.multiple_of(goal * PIECE + order * H, 16)
-            held[pl.ds(row, H), :] = kept.astype(held.dtype)
+            kept = kept.astype(held.dtype)
+            held[pl.ds(row, H), :] = kept
+            plain[pl.ds(pl.multiple_of(i * H, H), H), :] = kept
+            ends[pl.ds(i, 1), :] = last
             lasts[pl.ds(goal * 16 + order, 1), :] = last
         return carry
 
     lax.fori_loop(0, 4, four, 0)
+    plain[32 * H :, :] = ends[...].astype(plain.dtype)
     for k in range(8):
         outs[k][: MOST * H, :] = held[k * PIECE : k * PIECE + MOST * H, :]
         outs[k][MOST * H :, :] = lasts[k * 16 : (k + 1) * 16, :].astype(held.dtype)
@@ -114,12 +131,13 @@
 def fold_call(where, tiles, own):
     return pl.pallas_call(
         fold_kernel,
-        out_shape=[made(PIECE, K)] * 8,
+        out_shape=[made(PIECE, K)] * 8 + [made(32 * H + 32, K)],
         in_specs=[SMEM, SMEM, VMEM],
-        out_specs=[VMEM] * 8,
+        out_specs=[VMEM] * 9,
         scratch_shapes=[
             pltpu.VMEM((8 * PIECE, K), jnp.bfloat16),
             pltpu.VMEM((8 * 16, K), jnp.float32),
+            pltpu.VMEM((32, K), jnp.float32),
             pltpu.SMEM((8,), jnp.int32),
         ],
         compiler_params=LIMIT,
@@ -190,9 +208,17 @@
     for b, (dy, dcore) in enumerate(plan):
         row = lax.rem(y + dy, 4) * 64 + lax.rem(core + dcore, 2) * 32
         turn = turns[b % 2]
+        packed = len(blocks[b].shape) == 2
+        if packed:
+            ends = blocks[b][32 * H :, :].astype(jnp.float32)
         for m in range(32):
             t = tiles[row + m]
-            wide = jnp.dot(blocks[b][m], right[t], preferred_element_type=jnp.float32)
+            if packed:
+                kept = blocks[b][m * H : (m + 1) * H, :].astype(jnp.float32)
+                square = unfolded(kept, ends[m : m + 1]).astype(jnp.bfloat16)
+            else:
+                square = blocks[b][m]
+            wide = jnp.dot(square, right[t], preferred_element_type=jnp.float32)
             wide = wide.astype(jnp.bfloat16)
             tall = jnp.concatenate([wide[:, :K], wide[:, K:]], axis=0)
             both = jnp.dot(left[t], tall, preferred_element_type=jnp.float32)
@@ -250,19 +276,24 @@
 
 
 def gather_kernel(known, where, *refs):
-    values, out = refs[:-1], refs[-1]
-    x, z = where[0] // 4, lax.rem(where[0], 4)
+    n = len(known)
+    values, outs, held = refs[:n], refs[n : n + 8], refs[n + 8]
+    x, z, y, core = where[0] // 4, lax.rem(where[0], 4), where[1], where[2]
     for d, ref in zip(known, values):
-        group = lax.rem(x - d[0] + 4, 4) * 4 + lax.rem(z - d[1] + 4, 4)
-        out[group] = ref[...]
+        column, row = lax.rem(x - d[0] + 4, 4), lax.rem(z - d[1] + 4, 4)
+        goal = lax.rem(column - y + 4, 4) * 2 + lax.rem(row // 2 + core, 2)
+        held[goal * 2 + lax.rem(row, 2)] = ref[...]
+    for k in range(8):
+        outs[k][...] = held[2 * k : 2 * k + 2]
 
 
 def gather_call(where, known):
     return pl.pallas_call(
         functools.partial(gather_kernel, tuple(known)),
-        out_shape=made(16, UNIT, 256, dtype=jnp.float32),
+        out_shape=[made(2, UNIT, 256, dtype=jnp.float32)] * 8,
         in_specs=[SMEM] + [VMEM] * len(known),
-        out_specs=VMEM,
+        out_specs=[VMEM] * 8,
+        scratch_shapes=[pltpu.VMEM((16, UNIT, 256), jnp.float32)],
         compiler_params=LIMIT,
         name="gather",
     )(where, *[near(v) for v in known.values()])
@@ -271,12 +302,19 @@
 FORMED_BITS = sum(1 << (d[0] * 4 + d[1]) for d in FORMED)
 
 
-def final_kernel(where, ids_ref, landed, out):
+def straight_of(where, g):
+    x, z = where[0] // 4, lax.rem(where[0], 4)
+    goal = (where[1] * 2 + where[2]) * 2 + g
+    apart = lax.rem(x - goal // 4 + 4, 4) * 4 + lax.rem(z - lax.rem(goal, 4) + 4, 4)
+    return goal, (FORMED_BITS >> apart) & 1
+
+
+def places_kernel(where, ids_ref, hot_ref):
     line, y, core = where[0], where[1], where[2]
-    x, z = line // 4, lax.rem(line, 4)
-    target = (y * 2 + core) * 2
-    pairs = [ids_ref[pl.ds(2 * n, 2), :] for n in (line, target, target + 1)]
-    ids = jnp.concatenate(pairs + [pairs[0]], axis=0)
+    goals = [straight_of(where, g) for g in range(2)]
+    lines = [jnp.where(straight > 0, goal, line) for goal, straight in goals]
+    pairs = [ids_ref[pl.ds(2 * n, 2), :] for n in lines]
+    ids = jnp.concatenate(pairs + pairs, axis=0)
     lane = lax.broadcasted_iota(jnp.int32, (8, K), 1)
     half = lax.broadcasted_iota(jnp.int32, (8, K), 0) % 2
     ordinal = jnp.zeros((8, K), jnp.int32)
@@ -285,22 +323,36 @@
         ordinal = ordinal + same.astype(jnp.int32)
     block = half * 4 + (lane >> 5)
     step = ((ids >> 1) - (block >> 1)) & 3
-    place = ids * UNIT + step * (2 * MOST) + ((ids + block) & 1) * MOST + ordinal
+    source = ((y - (ids >> 1)) & 3) * 2 + ((ids + core) & 1)
+    place = source * UNIT + step * (2 * MOST) + ((ids + block) & 1) * MOST + ordinal
     columns = place.T
-    mine = jnp.concatenate([columns[:, 0:1], columns[:, 1:2]], axis=0)
     slots = lax.broadcasted_iota(jnp.int32, (256, 8 * UNIT), 1)
     for g in range(2):
-        goal = target + g
-        apart = lax.rem(x - goal // 4 + 4, 4) * 4 + lax.rem(z - lax.rem(goal, 4) + 4, 4)
-        straight = (FORMED_BITS >> apart) & 1
-        other = jnp.concatenate(
-            [columns[:, 2 + 2 * g : 3 + 2 * g], columns[:, 3 + 2 * g : 4 + 2 * g]], axis=0
+        chosen = jnp.concatenate(
+            [columns[:, 2 * g : 2 * g + 1], columns[:, 2 * g + 1 : 2 * g + 2]], axis=0
         )
-        hot = (slots == jnp.where(straight > 0, other, mine)).astype(jnp.bfloat16)
-        values = jnp.concatenate([landed[c, g] for c in range(8)], axis=0)
+        hot_ref[g] = (slots == chosen).astype(hot_ref.dtype)
+
+
+def places_call(where, ids):
+    return pl.pallas_call(
+        places_kernel,
+        out_shape=made(2, 256, 8 * UNIT),
+        in_specs=[SMEM, VMEM],
+        out_specs=VMEM,
+        compiler_params=LIMIT,
+        name="places",
+    )(where, ids)
+
+
+def final_kernel(where, hot_ref, *refs):
+    landed, out = refs[:8], refs[8]
+    for g in range(2):
+        _, straight = straight_of(where, g)
+        values = jnp.concatenate([ref[g] for ref in landed], axis=0)
         high = values.astype(jnp.bfloat16)
-        rest = values - high.astype(jnp.float32)
-        low = rest.astype(jnp.bfloat16)
+        low = (values - high.astype(jnp.float32)).astype(jnp.bfloat16)
+        hot = hot_ref[g]
         picked = jnp.dot(hot, high, preferred_element_type=jnp.float32)
         picked = picked + jnp.dot(hot, low, preferred_element_type=jnp.float32)
 
@@ -313,15 +365,15 @@
             out[:, g * 256 : (g + 1) * 256] = picked.T
 
 
-def final_call(where, ids, landed):
+def final_call(where, hot, landed):
     return pl.pallas_call(
         final_kernel,
         out_shape=jax.ShapeDtypeStruct((256, 512), jnp.float32),
-        in_specs=[SMEM, VMEM, VMEM],
+        in_specs=[SMEM] + [VMEM] * 9,
         out_specs=VMEM,
         compiler_params=LIMIT,
         name="final",
-    )(where, ids, near(landed))
+    )(where, near(hot), *[near(v) for v in landed])
 
 
 def steps(coeffs, tiles, primal, dual_inverse):
@@ -332,7 +384,7 @@
     flat = tiles.reshape(4096)
     line_ids = lax.dynamic_slice_in_dim(flat, line * 256, 256, 0)
 
-    pieces = fold_call(where, flat, coeffs)
+    *pieces, plain = fold_call(where, flat, coeffs)
     routed = [pieces[0]]
     for k in range(1, 8):
         routed.append(line_shift(pieces[k], k // 2, k % 2))
@@ -340,9 +392,9 @@
     right, left = prepare_call(where, primal, dual_inverse)
 
     other = line_shift(coeffs, 0, 1)
-    down = line_shift(coeffs, 1, 0)
-    up = line_shift(coeffs, 3, 0)
-    across = line_shift(coeffs, 2, 0)
+    down = line_shift(plain, 1, 0)
+    up = line_shift(plain, 3, 0)
+    across = line_shift(plain, 2, 0)
     down_other = line_shift(down, 0, 1)
     up_other = line_shift(up, 0, 1)
     across_other = line_shift(across, 0, 1)
@@ -351,25 +403,27 @@
         return reduce_call(plan, where, line_ids, blocks, right, left, total)
 
     total = formed(((0, 0), (0, 1)), [coeffs, other], None)
-    plan = ((3, 0), (3, 1), (1, 0), (1, 1))
-    total = formed(plan, [down, down_other, up, up_other], total)
+    total = formed(((3, 0), (3, 1)), [down, down_other], total)
+    total = formed(((1, 0), (1, 1)), [up, up_other], total)
     total = formed(((2, 0), (2, 1)), [across, across_other], total)
 
     for d, parent in FIRST + SECOND + THIRD:
         shift = ((d[0] - parent[0]) % 4, (d[1] - parent[1]) % 4)
         units[d] = plane_shift(units[parent], shift)
 
-    values = contract_call([units[d] for d in EARLY], total)
-    known = dict(zip(EARLY, values))
-    for d in EARLY:
+    known = {}
+    for part in (EARLY, MIDDLE, LATE):
+        values = contract_call([units[d] for d in part], total)
+        known.update(zip(part, values))
+    for d in EARLY + MIDDLE:
         if negated(d) in TURNED:
             known[negated(d)] = plane_shift(known[d], negated(d))
-    values = contract_call([units[d] for d in LATE], total)
-    known.update(zip(LATE, values))
     ordered = gather_call(where, known)
-    landed = lax.all_to_all(ordered.reshape(8, 2, UNIT, 256), LINE, 0, 0, tiled=True)
-
-    return final_call(where, tiles.reshape(32, K), landed)
+    landed = [ordered[0]]
+    for k in range(1, 8):
+        landed.append(line_shift(ordered[k], k // 2, k % 2))
+    hot = places_call(where, tiles.reshape(32, K))
+    return final_call(where, hot, landed)
 
 
 def solution(mesh):

time: 148 us -> 134 us (0.905)
  waiting for transfers between devices: 56.8 us -> 33.6 us
  blocking collectives: 19.5 us -> 0 us
  starting transfers between devices: 37.5 us -> 56.8 us
  Pallas kernels: 26.6 us -> 35.6 us
    ppermute x15, waiting for transfers between devices: 37 us -> 13.8 us  [plane_shift(): return lax.ppermute(x, PLANE, pairs)]
    ppermute x14 -> x21, starting transfers between devices: 14.8 us -> 34.7 us  [line_shift(): return lax.ppermute(x, LINE, pairs)]
    all_to_all x1 -> x0, blocking collectives: 19.5 us -> none  [steps(): lax.all_to_all(ordered.reshape(8, 2, UNIT, 256), LINE, 0, 0, tiled=True)]
    pallas_call x3 -> x4, Pallas kernels: 12.8 us -> 20.1 us  [reduce_call(): pl.pallas_call(functools.partial(reduce_kernel, plan, total is not None),...]
    pallas_call x2 -> x3, Pallas kernels: 6.16 us -> 7.65 us  [contract_call(): pl.pallas_call(functools.partial(contract_kernel, n), out_shape=[made(UNI...]
    unnamed x28 -> x32, local copies, waits for them, and re-layouts: 6.6 us -> 6.9 us
    ppermute x14 -> x21, waiting for transfers between devices: 19.8 us -> 19.9 us  [line_shift(): return lax.ppermute(x, LINE, pairs)]
  transfers between devices with their start and end apart: 29 -> 36, of which waited for: 9 -> 11; matrix products, arithmetic and copies ran while one was open for 0% -> 0% of each run, Pallas kernels for 14% -> 23%
where the time goes in v2:
time: 134 us; the launch traced here: 133 us
  starting transfers between devices  56.8 us (42%)
  Pallas kernels  35.6 us (27%)
  waiting for transfers between devices  33.6 us (25%)
  local copies, waits for them, and re-layouts  6.92 us (5%)
    ppermute x21, starting transfers between devices, line_shift(): return lax.ppermute(x, LINE, pairs)  34.7 us
    ppermute x15, starting transfers between devices, plane_shift(): return lax.ppermute(x, PLANE, pairs)  22 us
    pallas_call x4, Pallas kernels, reduce_call(): pl.pallas_call(functools.partial(reduce_kernel, plan, total is not None),...  20.1 us
    ppermute x21, waiting for transfers between devices, line_shift(): return lax.ppermute(x, LINE, pairs)  19.9 us
    ppermute x15, waiting for transfers between devices, plane_shift(): return lax.ppermute(x, PLANE, pairs)  13.8 us
    pallas_call x3, Pallas kernels, contract_call(): pl.pallas_call(functools.partial(contract_kernel, n), out_shape=[made(UNI...  7.65 us
    unnamed x32, local copies, waits for them, and re-layouts  6.9 us
  transfers between devices with their start and end apart: 36, of which 11 were waited for; matrix products, arithmetic and copies ran while one was open for 0% of the time, Pallas kernels for 23%

profile of v2, /device:TPU:1, one launch (start us, length us, event | category | flops | bytes accessed | tf_op | source)
XLA Modules:
  0.0 133.3 jit_solution(10802027329588396846)
XLA Ops:
  0.1 1.2 copy-done
  2.0 1.4 %fold.1 = (bf16[336,128]{1,0:T(8,128)(2,1)S(1)}, bf16[336,128]{1,0:T(8,128)(2,1)S(1)}, bf16[336,128]{1,0:T(8,128)(2,1)S(1)}, bf16[336,128]{1,0:T(8,128)(2,1)S(1)...) custom-call(s32[3]{0:T(128)S(1)} %pad_add_fusion.where, ...), custom_call_target="tpu_custom_call" | custom-call | tf_op jit(solution)/shard_map/fold/pallas_call | solution.py:132
  3.5 2.2 %collective-permute-start.18 = (bf16[2080,128]{1,0:T(8,128)(2,1)S(1)}, bf16[2080,128]{1,0:T(8,128)(2,1)S(1)}, u32[]{:S(2)}, u32[]{:S(2)}) collective-permute-start(bf16[2080,128]{1,0:T(8,128)(2,1)S(1)} %get-tuple-element.42), channel_id=1, source_target_pairs={{0,2},{1,3},{2,4},{3,5},{4,6},{5,7},{6,0},{7,1},{8,10},{9,11},{10,... | collective-permute-start | bytes 1597448 | tf_op jit(solution)/shard_map/ppermute | solution.py:71
  5.7 1.5 %collective-permute-start.16 = (bf16[2080,128]{1,0:T(8,128)(2,1)S(1)}, bf16[2080,128]{1,0:T(8,128)(2,1)S(1)}, u32[]{:S(2)}, u32[]{:S(2)}) collective-permute-start(bf16[2080,128]{1,0:T(8,128)(2,1)S(1)} %get-tuple-element.42), channel_id=1, source_target_pairs={{0,6},{1,7},{2,0},{3,1},{4,2},{5,3},{6,4},{7,5},{8,14},{9,15},{10,... | collective-permute-start | bytes 1597448 | tf_op jit(solution)/shard_map/ppermute | solution.py:71
  7.2 1.0 collective-permute-start
  8.4 1.5 %collective-permute-start.2 = (bf16[336,128]{1,0:T(8,128)(2,1)S(1)}, bf16[336,128]{1,0:T(8,128)(2,1)S(1)}, u32[]{:S(2)}, u32[]{:S(2)}) collective-permute-start(bf16[336,128]{1,0:T(8,128)(2,1)S(1)} %get-tuple-element.35), channel_id=1, source_target_pairs={{0,3},{1,2},{2,5},{3,4},{4,7},{5,6},{6,1},{7,0},{8,11},{9,10},{10,... | collective-permute-start | bytes 258056 | tf_op jit(solution)/shard_map/ppermute | solution.py:71
  9.8 2.4 %collective-permute-start.3 = (bf16[336,128]{1,0:T(8,128)(2,1)S(1)}, bf16[336,128]{1,0:T(8,128)(2,1)S(1)}, u32[]{:S(2)}, u32[]{:S(2)}) collective-permute-start(bf16[336,128]{1,0:T(8,128)(2,1)S(1)} %get-tuple-element.36), channel_id=1, source_target_pairs={{0,4},{1,5},{2,6},{3,7},{4,0},{5,1},{6,2},{7,3},{8,12},{9,13},{10,... | collective-permute-start | bytes 258056 | tf_op jit(solution)/shard_map/ppermute | solution.py:71
  12.2 8.4 %collective-permute-done.1.refs_2_ = bf16[336,128]{1,0:T(8,128)(2,1)S(1)} collective-permute-done((bf16[336,128]{1,0:T(8,128)(2,1)S(1)}, bf16[336,128]{1,0:T(8,128)(2,1)S(1)}, u32[]{:S(2)}, u32[]{:S(2)}) %collective-permute-start.1) | collective-permute-done | bytes 86048 | tf_op jit(solution)/shard_map/ppermute | solution.py:71
  20.6 4.1 %collective-permute-start.4 = (bf16[336,128]{1,0:T(8,128)(2,1)S(1)}, bf16[336,128]{1,0:T(8,128)(2,1)S(1)}, u32[]{:S(2)}, u32[]{:S(2)}) collective-permute-start(bf16[336,128]{1,0:T(8,128)(2,1)S(1)} %get-tuple-element.37), channel_id=1, source_target_pairs={{0,5},{1,4},{2,7},{3,6},{4,1},{5,0},{6,3},{7,2},{8,13},{9,12},{10,... | collective-permute-start | bytes 258056 | tf_op jit(solution)/shard_map/ppermute | solution.py:71
  25.7 2.1 %collective-permute-done.4.refs_5_ = bf16[336,128]{1,0:T(8,128)(2,1)S(1)} collective-permute-done((bf16[336,128]{1,0:T(8,128)(2,1)S(1)}, bf16[336,128]{1,0:T(8,128)(2,1)S(1)}, u32[]{:S(2)}, u32[]{:S(2)}) %collective-permute-start.4) | collective-permute-done | bytes 86048 | tf_op jit(solution)/shard_map/ppermute | solution.py:71
  27.8 0.8 collective-permute-done.5.refs_6_
  28.6 1.5 %collective-permute-done.6.refs_7_ = bf16[336,128]{1,0:T(8,128)(2,1)S(1)} collective-permute-done((bf16[336,128]{1,0:T(8,128)(2,1)S(1)}, bf16[336,128]{1,0:T(8,128)(2,1)S(1)}, u32[]{:S(2)}, u32[]{:S(2)}) %collective-permute-start.6) | collective-permute-done | bytes 86048 | tf_op jit(solution)/shard_map/ppermute | solution.py:71
  30.5 3.9 %collective-permute-start.9 = (bf16[40,8320]{1,0:T(8,128)(2,1)S(1)}, bf16[40,8320]{1,0:T(8,128)(2,1)}, u32[]{:S(2)}, u32[]{:S(2)}) collective-permute-start(bf16[40,8320]{1,0:T(8,128)(2,1)S(1)} %unit.1.refs_0_), channel_id=1, source_target_pairs={{0,104},{8,112},{16,120},{24,96},{32,8},{40,16},{48,24},{56,0},{64... | collective-permute-start | bytes 1996808 | tf_op jit(solution)/shard_map/ppermute | solution.py:63
  34.4 1.2 collective-permute-start.8
  35.6 1.6 %collective-permute-start.20 = (bf16[32,128,128]{2,1,0:T(8,128)(2,1)}, bf16[32,128,128]{2,1,0:T(8,128)(2,1)S(1)}, u32[]{:S(2)}, u32[]{:S(2)}) collective-permute-start(bf16[32,128,128]{2,1,0:T(8,128)(2,1)} %refs_0_.1), channel_id=1, source_target_pairs={{0,1},{1,0},{2,3},{3,2},{4,5},{5,4},{6,7},{7,6},{8,9},{9,8},{10,11... | collective-permute-start | bytes 3145736 | tf_op jit(solution)/shard_map/ppermute | solution.py:71
  37.2 2.0 %collective-permute-start.14 = (bf16[2080,128]{1,0:T(8,128)(2,1)S(1)}, bf16[2080,128]{1,0:T(8,128)(2,1)S(1)}, u32[]{:S(2)}, u32[]{:S(2)}) collective-permute-start(bf16[2080,128]{1,0:T(8,128)(2,1)S(1)} %get-tuple-element.42), channel_id=1, source_target_pairs={{0,4},{1,5},{2,6},{3,7},{4,0},{5,1},{6,2},{7,3},{8,12},{9,13},{10,... | collective-permute-start | bytes 1597448 | tf_op jit(solution)/shard_map/ppermute | solution.py:71
  39.2 10.5 %collective-permute-done.9.refs_3_ = bf16[40,8320]{1,0:T(8,128)(2,1)} collective-permute-done((bf16[40,8320]{1,0:T(8,128)(2,1)S(1)}, bf16[40,8320]{1,0:T(8,128)(2,1)}, u32[]{:S(2)}, u32[]{:S(2)}) %collective-permute-start.9) | collective-permute-done | bytes 665632 | tf_op jit(solution)/shard_map/ppermute | solution.py:63
  49.7 2.6 %collective-permute-done.14.refs_0_ = bf16[2080,128]{1,0:T(8,128)(2,1)S(1)} collective-permute-done((bf16[2080,128]{1,0:T(8,128)(2,1)S(1)}, bf16[2080,128]{1,0:T(8,128)(2,1)S(1)}, u32[]{:S(2)}, u32[]{:S(2)}) %collective-permute-start.14) | collective-permute-done | bytes 532512 | tf_op jit(solution)/shard_map/ppermute | solution.py:71
  52.2 0.9 collective-permute-start.19
  56.4 0.8 copy-done.8
  57.2 3.0 %collective-permute-start.11 = (bf16[40,8320]{1,0:T(8,128)(2,1)}, bf16[40,8320]{1,0:T(8,128)(2,1)}, u32[]{:S(2)}, u32[]{:S(2)}) collective-permute-start(bf16[40,8320]{1,0:T(8,128)(2,1)} %collective-permute-done.9.refs_3_), channel_id=1, source_target_pairs={{0,96},{8,104},{16,112},{24,120},{32,0},{40,8},{48,16},{56,24},{64... | collective-permute-start | bytes 1996808 | tf_op jit(solution)/shard_map/ppermute | solution.py:63
  60.2 0.8 copy-done.10
  61.9 2.3 %collective-permute-start.13 = (bf16[40,8320]{1,0:T(8,128)(2,1)}, bf16[40,8320]{1,0:T(8,128)(2,1)}, u32[]{:S(2)}, u32[]{:S(2)}) collective-permute-start(bf16[40,8320]{1,0:T(8,128)(2,1)} %collective-permute-done.8.refs_2_), channel_id=1, source_target_pairs={{0,24},{8,0},{16,8},{24,16},{32,56},{40,32},{48,40},{56,48},{64,88... | collective-permute-start | bytes 1996808 | tf_op jit(solution)/shard_map/ppermute | solution.py:63
  64.1 2.0 %collective-permute-done.10.refs_4_ = bf16[40,8320]{1,0:T(8,128)(2,1)} collective-permute-done((bf16[40,8320]{1,0:T(8,128)(2,1)}, bf16[40,8320]{1,0:T(8,128)(2,1)}, u32[]{:S(2)}, u32[]{:S(2)}) %collective-permute-start.10) | collective-permute-done | bytes 665632 | tf_op jit(solution)/shard_map/ppermute | solution.py:63
  66.2 2.0 %collective-permute-start.22 = (bf16[40,8320]{1,0:T(8,128)(2,1)}, bf16[40,8320]{1,0:T(8,128)(2,1)S(1)}, u32[]{:S(2)}, u32[]{:S(2)}) collective-permute-start(bf16[40,8320]{1,0:T(8,128)(2,1)} %collective-permute-done.10.refs_4_), channel_id=1, source_target_pairs={{0,96},{8,104},{16,112},{24,120},{32,0},{40,8},{48,16},{56,24},{64... | collective-permute-start | bytes 1996808 | tf_op jit(solution)/shard_map/ppermute | solution.py:63
  68.2 2.0 %prepare.1 = (bf16[8,128,256]{2,1,0:T(8,128)(2,1)S(1)}, bf16[8,128,256]{2,1,0:T(8,128)(2,1)S(1)}) custom-call(s32[3]{0:T(128)S(1)} %pad_add_fusion.where, bf16[1024,1024]{1,0:T(8,128)(2,1)} %primal.1, bf16[1024,1024]{1,0:T(8,128)(2,1)} %dual.1), custom_call_target="tpu_custom_call" | custom-call | tf_op jit(solution)/shard_map/prepare/pallas_call | solution.py:189
  70.3 3.2 %reduced.4.refs_2_ = bf16[256,8320]{1,0:T(8,128)(2,1)S(1)} custom-call(s32[3]{0:T(128)S(1)} %pad_add_fusion.where, s32[256]{0:T(256)S(1)} %bitcast.8, bf16[8,128,256]{2,1,0:T(8,128)(2,1)S(1)} %get-tuple-element.40.right, bf16[8,128,256]{2,1,0:T(8,128)(2,1)S(1)} %get-tuple-element.41.left, bf16[32,128,128]{2,1,0:T(8,128)(2,1)S(1)} %copy-done.1, ...), custom_call_target="tpu_custom_call" | custom-call | tf_op jit(solution)/shard_map/reduced/pallas_call | solution.py:243
  73.5 5.6 %reduced.5.refs_2_ = bf16[256,8320]{1,0:T(8,128)(2,1)S(1)} custom-call(s32[3]{0:T(128)S(1)} %pad_add_fusion.where, s32[256]{0:T(256)S(1)} %bitcast.9, bf16[8,128,256]{2,1,0:T(8,128)(2,1)S(1)} %get-tuple-element.40.right, bf16[8,128,256]{2,1,0:T(8,128)(2,1)S(1)} %get-tuple-element.41.left, ...), custom_call_target="tpu_custom_call", output_to_operand_aliasing={{}: (6, {})} | custom-call | tf_op jit(solution)/shard_map/reduced/pallas_call | solution.py:243
  79.1 5.6 %reduced.6.refs_2_ = bf16[256,8320]{1,0:T(8,128)(2,1)S(1)} custom-call(s32[3]{0:T(128)S(1)} %pad_add_fusion.where, s32[256]{0:T(256)S(1)} %bitcast.10, bf16[8,128,256]{2,1,0:T(8,128)(2,1)S(1)} %get-tuple-element.40.right, bf16[8,128,256]{2,1,0:T(8,128)(2,1)S(1)} %get-tuple-element.41.left, ...), custom_call_target="tpu_custom_call", output_to_operand_aliasing={{}: (6, {})} | custom-call | tf_op jit(solution)/shard_map/reduced/pallas_call | solution.py:243
  84.7 5.8 %reduced.7.refs_8_.refs_1_ = bf16[256,8320]{1,0:T(8,128)(2,1)S(1)} custom-call(s32[3]{0:T(128)S(1)} %pad_add_fusion.where, s32[256]{0:T(256)S(1)} %bitcast.11, bf16[8,128,256]{2,1,0:T(8,128)(2,1)S(1)} %get-tuple-element.40.right, bf16[8,128,256]{2,1,0:T(8,128)(2,1)S(1)} %get-tuple-element.41.left, ...), custom_call_target="tpu_custom_call", output_to_operand_aliasing={{}: (6, {})} | custom-call | tf_op jit(solution)/shard_map/reduced/pallas_call | solution.py:243
  90.5 2.4 %contract.4.refs_8_ = f32[40,256]{1,0:T(8,128)S(1)} custom-call(bf16[40,8320]{1,0:T(8,128)(2,1)} %collective-permute-done.21.refs_0_, bf16[256,8320]{1,0:T(8,128)(2,1)S(1)} %reduced.7.refs_8_.refs_1_), custom_call_target="tpu_custom_call" | custom-call | tf_op jit(solution)/shard_map/contract/pallas_call | solution.py:268
  93.0 1.1 collective-permute-start.28
  94.1 3.9 %contract.3 = (f32[40,256]{1,0:T(8,128)S(1)}, f32[40,256]{1,0:T(8,128)S(1)}, f32[40,256]{1,0:T(8,128)S(1)}, f32[40,256]{1,0:T(8,128)S(1)}, f32[40,256]{1,0:T(8,1...) custom-call(bf16[40,8320]{1,0:T(8,128)(2,1)S(1)} %unit.1.refs_0_, ...), custom_call_target="tpu_custom_call" | custom-call | tf_op jit(solution)/shard_map/contract/pallas_call | solution.py:268
  98.1 1.4 %collective-permute-start.24 = (f32[40,256]{1,0:T(8,128)S(1)}, f32[40,256]{1,0:T(8,128)S(1)}, u32[]{:S(2)}, u32[]{:S(2)}) collective-permute-start(f32[40,256]{1,0:T(8,128)S(1)} %get-tuple-element.45.refs_2_), channel_id=1, source_target_pairs={{0,8},{8,16},{16,24},{24,0},{32,40},{40,48},{48,56},{56,32},{64,72... | collective-permute-start | bytes 122888 | tf_op jit(solution)/shard_map/ppermute | solution.py:63
  99.5 2.5 %collective-permute-start.25 = (f32[40,256]{1,0:T(8,128)S(1)}, f32[40,256]{1,0:T(8,128)S(1)}, u32[]{:S(2)}, u32[]{:S(2)}) collective-permute-start(f32[40,256]{1,0:T(8,128)S(1)} %get-tuple-element.46.refs_3_), channel_id=1, source_target_pairs={{0,56},{8,32},{16,40},{24,48},{32,88},{40,64},{48,72},{56,80},{64,... | collective-permute-start | bytes 122888 | tf_op jit(solution)/shard_map/ppermute | solution.py:63
  102.4 4.0 %collective-permute-start.27 = (f32[40,256]{1,0:T(8,128)S(1)}, f32[40,256]{1,0:T(8,128)S(1)}, u32[]{:S(2)}, u32[]{:S(2)}) collective-permute-start(f32[40,256]{1,0:T(8,128)S(1)} %get-tuple-element.48.refs_5_), channel_id=1, source_target_pairs={{0,88},{8,64},{16,72},{24,80},{32,120},{40,96},{48,104},{56,112},{... | collective-permute-start | bytes 122888 | tf_op jit(solution)/shard_map/ppermute | solution.py:63
  106.4 1.3 %contract.5.refs_9_ = f32[40,256]{1,0:T(8,128)S(1)} custom-call(bf16[40,8320]{1,0:T(8,128)(2,1)S(1)} %collective-permute-done.22.refs_0_, bf16[256,8320]{1,0:T(8,128)(2,1)S(1)} %reduced.7.refs_8_.refs_1_), custom_call_target="tpu_custom_call" | custom-call | tf_op jit(solution)/shard_map/contract/pallas_call | solution.py:268
  107.8 1.2 collective-permute-done.26.refs_13_
  109.6 7.4 %collective-permute-start.29 = (f32[2,40,256]{2,1,0:T(8,128)S(1)}, f32[2,40,256]{2,1,0:T(8,128)S(1)}, u32[]{:S(2)}, u32[]{:S(2)}) collective-permute-start(f32[2,40,256]{2,1,0:T(8,128)S(1)} %get-tuple-element.52), channel_id=1, source_target_pairs={{0,1},{1,0},{2,3},{3,2},{4,5},{5,4},{6,7},{7,6},{8,9},{9,8},{10,11... | collective-permute-start | bytes 245768 | tf_op jit(solution)/shard_map/ppermute | solution.py:71
  117.0 1.9 %collective-permute-start.30 = (f32[2,40,256]{2,1,0:T(8,128)S(1)}, f32[2,40,256]{2,1,0:T(8,128)S(1)}, u32[]{:S(2)}, u32[]{:S(2)}) collective-permute-start(f32[2,40,256]{2,1,0:T(8,128)S(1)} %get-tuple-element.53), channel_id=1, source_target_pairs={{0,2},{1,3},{2,4},{3,5},{4,6},{5,7},{6,0},{7,1},{8,10},{9,11},{10,... | collective-permute-start | bytes 245768 | tf_op jit(solution)/shard_map/ppermute | solution.py:71
  119.0 2.6 %collective-permute-start.32 = (f32[2,40,256]{2,1,0:T(8,128)S(1)}, f32[2,40,256]{2,1,0:T(8,128)S(1)}, u32[]{:S(2)}, u32[]{:S(2)}) collective-permute-start(f32[2,40,256]{2,1,0:T(8,128)S(1)} %get-tuple-element.55), channel_id=1, source_target_pairs={{0,4},{1,5},{2,6},{3,7},{4,0},{5,1},{6,2},{7,3},{8,12},{9,13},{10,... | collective-permute-start | bytes 245768 | tf_op jit(solution)/shard_map/ppermute | solution.py:71
  121.5 0.9 collective-permute-start.33
  122.5 2.7 %collective-permute-start.34 = (f32[2,40,256]{2,1,0:T(8,128)S(1)}, f32[2,40,256]{2,1,0:T(8,128)S(1)}, u32[]{:S(2)}, u32[]{:S(2)}) collective-permute-start(f32[2,40,256]{2,1,0:T(8,128)S(1)} %get-tuple-element.57), channel_id=1, source_target_pairs={{0,6},{1,7},{2,0},{3,1},{4,2},{5,3},{6,4},{7,5},{8,14},{9,15},{10,... | collective-permute-start | bytes 245768 | tf_op jit(solution)/shard_map/ppermute | solution.py:71
  125.6 1.0 places.1.hot_ref
  126.6 0.9 collective-permute-done.32.refs_4_
  127.5 2.0 %collective-permute-done.33.refs_5_ = f32[2,40,256]{2,1,0:T(8,128)S(1)} collective-permute-done((f32[2,40,256]{2,1,0:T(8,128)S(1)}, f32[2,40,256]{2,1,0:T(8,128)S(1)}, u32[]{:S(2)}, u32[]{:S(2)}) %collective-permute-start.33) | collective-permute-done | bytes 81952 | tf_op jit(solution)/shard_map/ppermute | solution.py:71
  129.5 1.5 %collective-permute-done.35.refs_7_ = f32[2,40,256]{2,1,0:T(8,128)S(1)} collective-permute-done((f32[2,40,256]{2,1,0:T(8,128)S(1)}, f32[2,40,256]{2,1,0:T(8,128)S(1)}, u32[]{:S(2)}, u32[]{:S(2)}) %collective-permute-start.35) | collective-permute-done | bytes 81952 | tf_op jit(solution)/shard_map/ppermute | solution.py:71
  130.9 2.3 %final.1 = f32[256,512]{1,0:T(8,128)} custom-call(s32[3]{0:T(128)S(1)} %pad_add_fusion.where, bf16[2,256,320]{2,1,0:T(8,128)(2,1)S(1)} %places.1.hot_ref, f32[2,40,256]{2,1,0:T(8,128)S(1)} %get-tuple-element.51.refs_0_, f32[2,40,256]{2,1,0:T(8,128)S(1)} %collective-permute-done.29.refs_1_, f32[2,40,256]{2,1,0:T(8,128)S(1)} %collective-permute-done.30.refs_2_, ...), custom_call_target="tpu_custom_call" | custom-call | tf_op jit(solution)/shard_map/final/pallas_call | solution.py:369
  (71 shorter events, 8.0 us)
Async XLA Ops:
  0.0 70.2 %copy-start.15 = (s32[4096,1]{0,1:T(1,128)S(1)}, s32[4096,1]{0,1:T(1,128)}, u32[]{:S(2)}) copy-start(s32[4096,1]{0,1:T(1,128)} %param.5) | copy-start | bytes 49156
  0.1 1.2 copy-start
  2.0 68.2 %copy-start.1 = (bf16[32,128,128]{2,1,0:T(8,128)(2,1)S(1)}, bf16[32,128,128]{2,1,0:T(8,128)(2,1)}, u32[]{:S(2)}) copy-start(bf16[32,128,128]{2,1,0:T(8,128)(2,1)} %refs_0_.1) | copy-start | bytes 3145732
  3.5 32.1 %collective-permute-start.18 = (bf16[2080,128]{1,0:T(8,128)(2,1)S(1)}, bf16[2080,128]{1,0:T(8,128)(2,1)S(1)}, u32[]{:S(2)}, u32[]{:S(2)}) collective-permute-start(bf16[2080,128]{1,0:T(8,128)(2,1)S(1)} %get-tuple-element.42), channel_id=1, source_target_pairs={{0,2},{1,3},{2,4},{3,5},{4,6},{5,7},{6,0},{7,1},{8,10},{9,11},{10,... | collective-permute-start | bytes 1597448 | tf_op jit(solution)/shard_map/ppermute | solution.py:71
  5.7 31.5 %collective-permute-start.16 = (bf16[2080,128]{1,0:T(8,128)(2,1)S(1)}, bf16[2080,128]{1,0:T(8,128)(2,1)S(1)}, u32[]{:S(2)}, u32[]{:S(2)}) collective-permute-start(bf16[2080,128]{1,0:T(8,128)(2,1)S(1)} %get-tuple-element.42), channel_id=1, source_target_pairs={{0,6},{1,7},{2,0},{3,1},{4,2},{5,3},{6,4},{7,5},{8,14},{9,15},{10,... | collective-permute-start | bytes 1597448 | tf_op jit(solution)/shard_map/ppermute | solution.py:71
  7.2 2.6 %collective-permute-start = (bf16[336,128]{1,0:T(8,128)(2,1)S(1)}, bf16[336,128]{1,0:T(8,128)(2,1)S(1)}, u32[]{:S(2)}, u32[]{:S(2)}) collective-permute-start(bf16[336,128]{1,0:T(8,128)(2,1)S(1)} %get-tuple-element.33), channel_id=1, source_target_pairs={{0,1},{1,0},{2,3},{3,2},{4,5},{5,4},{6,7},{7,6},{8,9},{9,8},{10,11... | collective-permute-start | bytes 258056 | tf_op jit(solution)/shard_map/ppermute | solution.py:71
  8.2 12.5 %collective-permute-start.1 = (bf16[336,128]{1,0:T(8,128)(2,1)S(1)}, bf16[336,128]{1,0:T(8,128)(2,1)S(1)}, u32[]{:S(2)}, u32[]{:S(2)}) collective-permute-start(bf16[336,128]{1,0:T(8,128)(2,1)S(1)} %get-tuple-element.34), channel_id=1, source_target_pairs={{0,2},{1,3},{2,4},{3,5},{4,6},{5,7},{6,0},{7,1},{8,10},{9,11},{10,... | collective-permute-start | bytes 258056 | tf_op jit(solution)/shard_map/ppermute | solution.py:71
  8.4 16.4 %collective-permute-start.2 = (bf16[336,128]{1,0:T(8,128)(2,1)S(1)}, bf16[336,128]{1,0:T(8,128)(2,1)S(1)}, u32[]{:S(2)}, u32[]{:S(2)}) collective-permute-start(bf16[336,128]{1,0:T(8,128)(2,1)S(1)} %get-tuple-element.35), channel_id=1, source_target_pairs={{0,3},{1,2},{2,5},{3,4},{4,7},{5,6},{6,1},{7,0},{8,11},{9,10},{10,... | collective-permute-start | bytes 258056 | tf_op jit(solution)/shard_map/ppermute | solution.py:71
  9.8 15.7 %collective-permute-start.3 = (bf16[336,128]{1,0:T(8,128)(2,1)S(1)}, bf16[336,128]{1,0:T(8,128)(2,1)S(1)}, u32[]{:S(2)}, u32[]{:S(2)}) collective-permute-start(bf16[336,128]{1,0:T(8,128)(2,1)S(1)} %get-tuple-element.36), channel_id=1, source_target_pairs={{0,4},{1,5},{2,6},{3,7},{4,0},{5,1},{6,2},{7,3},{8,12},{9,13},{10,... | collective-permute-start | bytes 258056 | tf_op jit(solution)/shard_map/ppermute | solution.py:71
  20.6 7.1 %collective-permute-start.4 = (bf16[336,128]{1,0:T(8,128)(2,1)S(1)}, bf16[336,128]{1,0:T(8,128)(2,1)S(1)}, u32[]{:S(2)}, u32[]{:S(2)}) collective-permute-start(bf16[336,128]{1,0:T(8,128)(2,1)S(1)} %get-tuple-element.37), channel_id=1, source_target_pairs={{0,5},{1,4},{2,7},{3,6},{4,1},{5,0},{6,3},{7,2},{8,13},{9,12},{10,... | collective-permute-start | bytes 258056 | tf_op jit(solution)/shard_map/ppermute | solution.py:71
  24.8 3.8 %collective-permute-start.5 = (bf16[336,128]{1,0:T(8,128)(2,1)S(1)}, bf16[336,128]{1,0:T(8,128)(2,1)S(1)}, u32[]{:S(2)}, u32[]{:S(2)}) collective-permute-start(bf16[336,128]{1,0:T(8,128)(2,1)S(1)} %get-tuple-element.38), channel_id=1, source_target_pairs={{0,6},{1,7},{2,0},{3,1},{4,2},{5,3},{6,4},{7,5},{8,14},{9,15},{10,... | collective-permute-start | bytes 258056 | tf_op jit(solution)/shard_map/ppermute | solution.py:71
  25.5 4.6 %collective-permute-start.6 = (bf16[336,128]{1,0:T(8,128)(2,1)S(1)}, bf16[336,128]{1,0:T(8,128)(2,1)S(1)}, u32[]{:S(2)}, u32[]{:S(2)}) collective-permute-start(bf16[336,128]{1,0:T(8,128)(2,1)S(1)} %get-tuple-element.39), channel_id=1, source_target_pairs={{0,7},{1,6},{2,1},{3,0},{4,3},{5,2},{6,5},{7,4},{8,15},{9,14},{10,... | collective-permute-start | bytes 258056 | tf_op jit(solution)/shard_map/ppermute | solution.py:71
  30.5 19.2 %collective-permute-start.9 = (bf16[40,8320]{1,0:T(8,128)(2,1)S(1)}, bf16[40,8320]{1,0:T(8,128)(2,1)}, u32[]{:S(2)}, u32[]{:S(2)}) collective-permute-start(bf16[40,8320]{1,0:T(8,128)(2,1)S(1)} %unit.1.refs_0_), channel_id=1, source_target_pairs={{0,104},{8,112},{16,120},{24,96},{32,8},{40,16},{48,24},{56,0},{64... | collective-permute-start | bytes 1996808 | tf_op jit(solution)/shard_map/ppermute | solution.py:63
  34.4 19.6 %collective-permute-start.7 = (bf16[40,8320]{1,0:T(8,128)(2,1)S(1)}, bf16[40,8320]{1,0:T(8,128)(2,1)}, u32[]{:S(2)}, u32[]{:S(2)}) collective-permute-start(bf16[40,8320]{1,0:T(8,128)(2,1)S(1)} %unit.1.refs_0_), channel_id=1, source_target_pairs={{0,32},{8,40},{16,48},{24,56},{32,64},{40,72},{48,80},{56,88},{64,... | collective-permute-start | bytes 1996808 | tf_op jit(solution)/shard_map/ppermute | solution.py:63
  34.4 20.4 %collective-permute-start.8 = (bf16[40,8320]{1,0:T(8,128)(2,1)S(1)}, bf16[40,8320]{1,0:T(8,128)(2,1)}, u32[]{:S(2)}, u32[]{:S(2)}) collective-permute-start(bf16[40,8320]{1,0:T(8,128)(2,1)S(1)} %unit.1.refs_0_), channel_id=1, source_target_pairs={{0,24},{8,0},{16,8},{24,16},{32,56},{40,32},{48,40},{56,48},{64,88... | collective-permute-start | bytes 1996808 | tf_op jit(solution)/shard_map/ppermute | solution.py:63
  35.6 20.5 %collective-permute-start.20 = (bf16[32,128,128]{2,1,0:T(8,128)(2,1)}, bf16[32,128,128]{2,1,0:T(8,128)(2,1)S(1)}, u32[]{:S(2)}, u32[]{:S(2)}) collective-permute-start(bf16[32,128,128]{2,1,0:T(8,128)(2,1)} %refs_0_.1), channel_id=1, source_target_pairs={{0,1},{1,0},{2,3},{3,2},{4,5},{5,4},{6,7},{7,6},{8,9},{9,8},{10,11... | collective-permute-start | bytes 3145736 | tf_op jit(solution)/shard_map/ppermute | solution.py:71
  37.2 15.1 %collective-permute-start.14 = (bf16[2080,128]{1,0:T(8,128)(2,1)S(1)}, bf16[2080,128]{1,0:T(8,128)(2,1)S(1)}, u32[]{:S(2)}, u32[]{:S(2)}) collective-permute-start(bf16[2080,128]{1,0:T(8,128)(2,1)S(1)} %get-tuple-element.42), channel_id=1, source_target_pairs={{0,4},{1,5},{2,6},{3,7},{4,0},{5,1},{6,2},{7,3},{8,12},{9,13},{10,... | collective-permute-start | bytes 1597448 | tf_op jit(solution)/shard_map/ppermute | solution.py:71
  49.7 16.5 %collective-permute-start.10 = (bf16[40,8320]{1,0:T(8,128)(2,1)}, bf16[40,8320]{1,0:T(8,128)(2,1)}, u32[]{:S(2)}, u32[]{:S(2)}) collective-permute-start(bf16[40,8320]{1,0:T(8,128)(2,1)} %collective-permute-done.9.refs_3_), channel_id=1, source_target_pairs={{0,8},{8,16},{16,24},{24,0},{32,40},{40,48},{48,56},{56,32},{64,72... | collective-permute-start | bytes 1996808 | tf_op jit(solution)/shard_map/ppermute | solution.py:63
  52.2 4.1 %collective-permute-start.19 = (bf16[2080,128]{1,0:T(8,128)(2,1)S(1)}, bf16[2080,128]{1,0:T(8,128)(2,1)S(1)}, u32[]{:S(2)}, u32[]{:S(2)}) collective-permute-start(bf16[2080,128]{1,0:T(8,128)(2,1)S(1)} %collective-permute-done.18.refs_0_), channel_id=1, source_target_pairs={{0,1},{1,0},{2,3},{3,2},{4,5},{5,4},{6,7},{7,6},{8,9},{9,8},{10,11... | collective-permute-start | bytes 1597448 | tf_op jit(solution)/shard_map/ppermute | solution.py:71
  54.0 6.2 %collective-permute-start.17 = (bf16[2080,128]{1,0:T(8,128)(2,1)S(1)}, bf16[2080,128]{1,0:T(8,128)(2,1)S(1)}, u32[]{:S(2)}, u32[]{:S(2)}) collective-permute-start(bf16[2080,128]{1,0:T(8,128)(2,1)S(1)} %collective-permute-done.16.refs_0_), channel_id=1, source_target_pairs={{0,1},{1,0},{2,3},{3,2},{4,5},{5,4},{6,7},{7,6},{8,9},{9,8},{10,11... | collective-permute-start | bytes 1597448 | tf_op jit(solution)/shard_map/ppermute | solution.py:71
  54.8 6.2 %collective-permute-start.15 = (bf16[2080,128]{1,0:T(8,128)(2,1)S(1)}, bf16[2080,128]{1,0:T(8,128)(2,1)S(1)}, u32[]{:S(2)}, u32[]{:S(2)}) collective-permute-start(bf16[2080,128]{1,0:T(8,128)(2,1)S(1)} %collective-permute-done.14.refs_0_), channel_id=1, source_target_pairs={{0,1},{1,0},{2,3},{3,2},{4,5},{5,4},{6,7},{7,6},{8,9},{9,8},{10,11... | collective-permute-start | bytes 1597448 | tf_op jit(solution)/shard_map/ppermute | solution.py:71
  56.1 34.4 %collective-permute-start.21 = (bf16[40,8320]{1,0:T(8,128)(2,1)}, bf16[40,8320]{1,0:T(8,128)(2,1)}, u32[]{:S(2)}, u32[]{:S(2)}) collective-permute-start(bf16[40,8320]{1,0:T(8,128)(2,1)} %collective-permute-done.7.refs_1_), channel_id=1, source_target_pairs={{0,8},{8,16},{16,24},{24,0},{32,40},{40,48},{48,56},{56,32},{64,72... | collective-permute-start | bytes 1996808 | tf_op jit(solution)/shard_map/ppermute | solution.py:63
  56.4 0.8 copy-start.8
  57.2 36.9 %collective-permute-start.11 = (bf16[40,8320]{1,0:T(8,128)(2,1)}, bf16[40,8320]{1,0:T(8,128)(2,1)}, u32[]{:S(2)}, u32[]{:S(2)}) collective-permute-start(bf16[40,8320]{1,0:T(8,128)(2,1)} %collective-permute-done.9.refs_3_), channel_id=1, source_target_pairs={{0,96},{8,104},{16,112},{24,120},{32,0},{40,8},{48,16},{56,24},{64... | collective-permute-start | bytes 1996808 | tf_op jit(solution)/shard_map/ppermute | solution.py:63
  60.2 0.9 copy-start.10
  61.0 33.1 %collective-permute-start.12 = (bf16[40,8320]{1,0:T(8,128)(2,1)}, bf16[40,8320]{1,0:T(8,128)(2,1)}, u32[]{:S(2)}, u32[]{:S(2)}) collective-permute-start(bf16[40,8320]{1,0:T(8,128)(2,1)} %collective-permute-done.7.refs_1_), channel_id=1, source_target_pairs={{0,32},{8,40},{16,48},{24,56},{32,64},{40,72},{48,80},{56,88},{64,... | collective-permute-start | bytes 1996808 | tf_op jit(solution)/shard_map/ppermute | solution.py:63
  61.0 0.8 copy-start.12
  61.9 32.2 %collective-permute-start.13 = (bf16[40,8320]{1,0:T(8,128)(2,1)}, bf16[40,8320]{1,0:T(8,128)(2,1)}, u32[]{:S(2)}, u32[]{:S(2)}) collective-permute-start(bf16[40,8320]{1,0:T(8,128)(2,1)} %collective-permute-done.8.refs_2_), channel_id=1, source_target_pairs={{0,24},{8,0},{16,8},{24,16},{32,56},{40,32},{48,40},{56,48},{64,88... | collective-permute-start | bytes 1996808 | tf_op jit(solution)/shard_map/ppermute | solution.py:63
  66.2 36.2 %collective-permute-start.22 = (bf16[40,8320]{1,0:T(8,128)(2,1)}, bf16[40,8320]{1,0:T(8,128)(2,1)S(1)}, u32[]{:S(2)}, u32[]{:S(2)}) collective-permute-start(bf16[40,8320]{1,0:T(8,128)(2,1)} %collective-permute-done.10.refs_4_), channel_id=1, source_target_pairs={{0,96},{8,104},{16,112},{24,120},{32,0},{40,8},{48,16},{56,24},{64... | collective-permute-start | bytes 1996808 | tf_op jit(solution)/shard_map/ppermute | solution.py:63
  70.2 3.2 %copy-start.3 = (bf16[2080,128]{1,0:T(8,128)(2,1)S(1)}, bf16[2080,128]{1,0:T(8,128)(2,1)}, u32[]{:S(2)}) copy-start(bf16[2080,128]{1,0:T(8,128)(2,1)} %copy-done.2) | copy-start | bytes 1597444
  70.2 3.2 %copy-start.9 = (bf16[2080,128]{1,0:T(8,128)(2,1)S(1)}, bf16[2080,128]{1,0:T(8,128)(2,1)}, u32[]{:S(2)}) copy-start(bf16[2080,128]{1,0:T(8,128)(2,1)} %copy-done.8) | copy-start | bytes 1597444
  73.5 5.6 %copy-start.5 = (bf16[2080,128]{1,0:T(8,128)(2,1)S(1)}, bf16[2080,128]{1,0:T(8,128)(2,1)}, u32[]{:S(2)}) copy-start(bf16[2080,128]{1,0:T(8,128)(2,1)} %copy-done.4) | copy-start | bytes 1597444
  73.5 5.6 %copy-start.11 = (bf16[2080,128]{1,0:T(8,128)(2,1)S(1)}, bf16[2080,128]{1,0:T(8,128)(2,1)}, u32[]{:S(2)}) copy-start(bf16[2080,128]{1,0:T(8,128)(2,1)} %copy-done.10) | copy-start | bytes 1597444
  79.1 5.6 %copy-start.7 = (bf16[2080,128]{1,0:T(8,128)(2,1)S(1)}, bf16[2080,128]{1,0:T(8,128)(2,1)}, u32[]{:S(2)}) copy-start(bf16[2080,128]{1,0:T(8,128)(2,1)} %copy-done.6) | copy-start | bytes 1597444
  79.1 5.6 %copy-start.13 = (bf16[2080,128]{1,0:T(8,128)(2,1)S(1)}, bf16[2080,128]{1,0:T(8,128)(2,1)}, u32[]{:S(2)}) copy-start(bf16[2080,128]{1,0:T(8,128)(2,1)} %copy-done.12) | copy-start | bytes 1597444
  93.0 9.0 %collective-permute-start.28 = (f32[40,256]{1,0:T(8,128)S(1)}, f32[40,256]{1,0:T(8,128)S(1)}, u32[]{:S(2)}, u32[]{:S(2)}) collective-permute-start(f32[40,256]{1,0:T(8,128)S(1)} %contract.4.refs_8_), channel_id=1, source_target_pairs={{0,120},{8,96},{16,104},{24,112},{32,24},{40,0},{48,8},{56,16},{64... | collective-permute-start | bytes 122888 | tf_op jit(solution)/shard_map/ppermute | solution.py:63
  98.0 9.7 %collective-permute-start.23 = (f32[40,256]{1,0:T(8,128)S(1)}, f32[40,256]{1,0:T(8,128)S(1)}, u32[]{:S(2)}, u32[]{:S(2)}) collective-permute-start(f32[40,256]{1,0:T(8,128)S(1)} %get-tuple-element.44.refs_1_), channel_id=1, source_target_pairs={{0,96},{8,104},{16,112},{24,120},{32,0},{40,8},{48,16},{56,24},{64... | collective-permute-start | bytes 122888 | tf_op jit(solution)/shard_map/ppermute | solution.py:63
  98.1 9.6 %collective-permute-start.24 = (f32[40,256]{1,0:T(8,128)S(1)}, f32[40,256]{1,0:T(8,128)S(1)}, u32[]{:S(2)}, u32[]{:S(2)}) collective-permute-start(f32[40,256]{1,0:T(8,128)S(1)} %get-tuple-element.45.refs_2_), channel_id=1, source_target_pairs={{0,8},{8,16},{16,24},{24,0},{32,40},{40,48},{48,56},{56,32},{64,72... | collective-permute-start | bytes 122888 | tf_op jit(solution)/shard_map/ppermute | solution.py:63
  99.5 8.3 %collective-permute-start.25 = (f32[40,256]{1,0:T(8,128)S(1)}, f32[40,256]{1,0:T(8,128)S(1)}, u32[]{:S(2)}, u32[]{:S(2)}) collective-permute-start(f32[40,256]{1,0:T(8,128)S(1)} %get-tuple-element.46.refs_3_), channel_id=1, source_target_pairs={{0,56},{8,32},{16,40},{24,48},{32,88},{40,64},{48,72},{56,80},{64,... | collective-permute-start | bytes 122888 | tf_op jit(solution)/shard_map/ppermute | solution.py:63
  102.0 6.9 %collective-permute-start.26 = (f32[40,256]{1,0:T(8,128)S(1)}, f32[40,256]{1,0:T(8,128)S(1)}, u32[]{:S(2)}, u32[]{:S(2)}) collective-permute-start(f32[40,256]{1,0:T(8,128)S(1)} %get-tuple-element.47.refs_4_), channel_id=1, source_target_pairs={{0,48},{8,56},{16,32},{24,40},{32,80},{40,88},{48,64},{56,72},{64,... | collective-permute-start | bytes 122888 | tf_op jit(solution)/shard_map/ppermute | solution.py:63
  102.4 6.6 %collective-permute-start.27 = (f32[40,256]{1,0:T(8,128)S(1)}, f32[40,256]{1,0:T(8,128)S(1)}, u32[]{:S(2)}, u32[]{:S(2)}) collective-permute-start(f32[40,256]{1,0:T(8,128)S(1)} %get-tuple-element.48.refs_5_), channel_id=1, source_target_pairs={{0,88},{8,64},{16,72},{24,80},{32,120},{40,96},{48,104},{56,112},{... | collective-permute-start | bytes 122888 | tf_op jit(solution)/shard_map/ppermute | solution.py:63
  109.6 12.8 %collective-permute-start.29 = (f32[2,40,256]{2,1,0:T(8,128)S(1)}, f32[2,40,256]{2,1,0:T(8,128)S(1)}, u32[]{:S(2)}, u32[]{:S(2)}) collective-permute-start(f32[2,40,256]{2,1,0:T(8,128)S(1)} %get-tuple-element.52), channel_id=1, source_target_pairs={{0,1},{1,0},{2,3},{3,2},{4,5},{5,4},{6,7},{7,6},{8,9},{9,8},{10,11... | collective-permute-start | bytes 245768 | tf_op jit(solution)/shard_map/ppermute | solution.py:71
  117.0 8.2 %collective-permute-start.30 = (f32[2,40,256]{2,1,0:T(8,128)S(1)}, f32[2,40,256]{2,1,0:T(8,128)S(1)}, u32[]{:S(2)}, u32[]{:S(2)}) collective-permute-start(f32[2,40,256]{2,1,0:T(8,128)S(1)} %get-tuple-element.53), channel_id=1, source_target_pairs={{0,2},{1,3},{2,4},{3,5},{4,6},{5,7},{6,0},{7,1},{8,10},{9,11},{10,... | collective-permute-start | bytes 245768 | tf_op jit(solution)/shard_map/ppermute | solution.py:71
  118.9 7.6 %collective-permute-start.31 = (f32[2,40,256]{2,1,0:T(8,128)S(1)}, f32[2,40,256]{2,1,0:T(8,128)S(1)}, u32[]{:S(2)}, u32[]{:S(2)}) collective-permute-start(f32[2,40,256]{2,1,0:T(8,128)S(1)} %get-tuple-element.54), channel_id=1, source_target_pairs={{0,3},{1,2},{2,5},{3,4},{4,7},{5,6},{6,1},{7,0},{8,11},{9,10},{10,... | collective-permute-start | bytes 245768 | tf_op jit(solution)/shard_map/ppermute | solution.py:71
  119.0 8.5 %collective-permute-start.32 = (f32[2,40,256]{2,1,0:T(8,128)S(1)}, f32[2,40,256]{2,1,0:T(8,128)S(1)}, u32[]{:S(2)}, u32[]{:S(2)}) collective-permute-start(f32[2,40,256]{2,1,0:T(8,128)S(1)} %get-tuple-element.55), channel_id=1, source_target_pairs={{0,4},{1,5},{2,6},{3,7},{4,0},{5,1},{6,2},{7,3},{8,12},{9,13},{10,... | collective-permute-start | bytes 245768 | tf_op jit(solution)/shard_map/ppermute | solution.py:71
  121.5 7.9 %collective-permute-start.33 = (f32[2,40,256]{2,1,0:T(8,128)S(1)}, f32[2,40,256]{2,1,0:T(8,128)S(1)}, u32[]{:S(2)}, u32[]{:S(2)}) collective-permute-start(f32[2,40,256]{2,1,0:T(8,128)S(1)} %get-tuple-element.56), channel_id=1, source_target_pairs={{0,5},{1,4},{2,7},{3,6},{4,1},{5,0},{6,3},{7,2},{8,13},{9,12},{10,... | collective-permute-start | bytes 245768 | tf_op jit(solution)/shard_map/ppermute | solution.py:71
  122.5 7.0 %collective-permute-start.34 = (f32[2,40,256]{2,1,0:T(8,128)S(1)}, f32[2,40,256]{2,1,0:T(8,128)S(1)}, u32[]{:S(2)}, u32[]{:S(2)}) collective-permute-start(f32[2,40,256]{2,1,0:T(8,128)S(1)} %get-tuple-element.57), channel_id=1, source_target_pairs={{0,6},{1,7},{2,0},{3,1},{4,2},{5,3},{6,4},{7,5},{8,14},{9,15},{10,... | collective-permute-start | bytes 245768 | tf_op jit(solution)/shard_map/ppermute | solution.py:71
  125.1 5.8 %collective-permute-start.35 = (f32[2,40,256]{2,1,0:T(8,128)S(1)}, f32[2,40,256]{2,1,0:T(8,128)S(1)}, u32[]{:S(2)}, u32[]{:S(2)}) collective-permute-start(f32[2,40,256]{2,1,0:T(8,128)S(1)} %get-tuple-element.58), channel_id=1, source_target_pairs={{0,7},{1,6},{2,1},{3,0},{4,3},{5,2},{6,5},{7,4},{8,15},{9,14},{10,... | collective-permute-start | bytes 245768 | tf_op jit(solution)/shard_map/ppermute | solution.py:71
  (4 other events, 3.1 us)

commit v3 on v2

--- a/solution.py
+++ b/solution.py
@@ -87,8 +87,7 @@
 def unfolded(kept, last):
     row = lax.broadcasted_iota(jnp.int32, (H, K), 0)
     lane = lax.broadcasted_iota(jnp.int32, (H, K), 1)
-    turned = kept.T
-    wide = jnp.concatenate([turned, turned], axis=1)
+    wide = jnp.concatenate([kept, kept], axis=0).T
     head, tail = wide[:H], wide[H:]
     top = jnp.where(jnp.logical_and(lane < H, row > lane), head, kept)
     corner = pltpu.roll(jnp.where(row > lane, kept, head), H, 1)
@@ -346,7 +345,8 @@
 
 
 def final_kernel(where, hot_ref, *refs):
-    landed, out = refs[:8], refs[8]
+    landed, out, held, sems = refs[:8], *refs[8:]
+    stores = []
     for g in range(2):
         _, straight = straight_of(where, g)
         values = jnp.concatenate([ref[g] for ref in landed], axis=0)
@@ -358,11 +358,17 @@
 
         @pl.when(straight == 0)
         def _():
-            out[:, g * 256 : (g + 1) * 256] = picked
+            held[g] = picked
 
         @pl.when(straight > 0)
         def _():
-            out[:, g * 256 : (g + 1) * 256] = picked.T
+            held[g] = picked.T
+
+        store = pltpu.make_async_copy(held.at[g], out.at[:, pl.ds(g * 256, 256)], sems.at[g])
+        store.start()
+        stores.append(store)
+    for store in stores:
+        store.wait()
 
 
 def final_call(where, hot, landed):
@@ -370,7 +376,11 @@
         final_kernel,
         out_shape=jax.ShapeDtypeStruct((256, 512), jnp.float32),
         in_specs=[SMEM] + [VMEM] * 9,
-        out_specs=VMEM,
+        out_specs=HBM,
+        scratch_shapes=[
+            pltpu.VMEM((2, 256, 256), jnp.float32),
+            pltpu.SemaphoreType.DMA((2,)),
+        ],
         compiler_params=LIMIT,
         name="final",
     )(where, near(hot), *[near(v) for v in landed])

time: 134 us -> 133 us (level)
  no operation moved by 1% of the time
where the time goes in v3:
time: 133 us
  starting transfers between devices  56.7 us (43%)
  Pallas kernels  35 us (26%)
  waiting for transfers between devices  33.6 us (25%)
  local copies, waits for them, and re-layouts  6.92 us (5%)
    ppermute x21, starting transfers between devices, line_shift(): return lax.ppermute(x, LINE, pairs)  34.7 us
    ppermute x15, starting transfers between devices, plane_shift(): return lax.ppermute(x, PLANE, pairs)  22 us
    ppermute x21, waiting for transfers between devices, line_shift(): return lax.ppermute(x, LINE, pairs)  19.9 us
    pallas_call x4, Pallas kernels, reduce_call(): pl.pallas_call(functools.partial(reduce_kernel, plan, total is not None),...  19.6 us
    ppermute x15, waiting for transfers between devices, plane_shift(): return lax.ppermute(x, PLANE, pairs)  13.8 us
    pallas_call x3, Pallas kernels, contract_call(): pl.pallas_call(functools.partial(contract_kernel, n), out_shape=[made(UNI...  7.65 us
    unnamed x32, local copies, waits for them, and re-layouts  6.9 us
  transfers between devices with their start and end apart: 36, of which 11 were waited for; matrix products, arithmetic and copies ran while one was open for 0% of the time, Pallas kernels for 23%

profile of v3, /device:TPU:1, one launch (start us, length us, event | category | flops | bytes accessed | tf_op | source)
XLA Modules:
  0.0 132.8 jit_solution(913556239694916923)
XLA Ops:
  0.1 1.2 copy-done
  2.0 1.4 %fold.1 = (bf16[336,128]{1,0:T(8,128)(2,1)S(1)}, bf16[336,128]{1,0:T(8,128)(2,1)S(1)}, bf16[336,128]{1,0:T(8,128)(2,1)S(1)}, bf16[336,128]{1,0:T(8,128)(2,1)S(1)...) custom-call(s32[3]{0:T(128)S(1)} %pad_add_fusion.where, ...), custom_call_target="tpu_custom_call" | custom-call | tf_op jit(solution)/shard_map/fold/pallas_call | solution.py:131
  3.5 2.2 %collective-permute-start.18 = (bf16[2080,128]{1,0:T(8,128)(2,1)S(1)}, bf16[2080,128]{1,0:T(8,128)(2,1)S(1)}, u32[]{:S(2)}, u32[]{:S(2)}) collective-permute-start(bf16[2080,128]{1,0:T(8,128)(2,1)S(1)} %get-tuple-element.42), channel_id=1, source_target_pairs={{0,2},{1,3},{2,4},{3,5},{4,6},{5,7},{6,0},{7,1},{8,10},{9,11},{10,... | collective-permute-start | bytes 1597448 | tf_op jit(solution)/shard_map/ppermute | solution.py:71
  5.7 1.5 %collective-permute-start.16 = (bf16[2080,128]{1,0:T(8,128)(2,1)S(1)}, bf16[2080,128]{1,0:T(8,128)(2,1)S(1)}, u32[]{:S(2)}, u32[]{:S(2)}) collective-permute-start(bf16[2080,128]{1,0:T(8,128)(2,1)S(1)} %get-tuple-element.42), channel_id=1, source_target_pairs={{0,6},{1,7},{2,0},{3,1},{4,2},{5,3},{6,4},{7,5},{8,14},{9,15},{10,... | collective-permute-start | bytes 1597448 | tf_op jit(solution)/shard_map/ppermute | solution.py:71
  7.2 1.0 collective-permute-start
  8.4 1.5 %collective-permute-start.2 = (bf16[336,128]{1,0:T(8,128)(2,1)S(1)}, bf16[336,128]{1,0:T(8,128)(2,1)S(1)}, u32[]{:S(2)}, u32[]{:S(2)}) collective-permute-start(bf16[336,128]{1,0:T(8,128)(2,1)S(1)} %get-tuple-element.35), channel_id=1, source_target_pairs={{0,3},{1,2},{2,5},{3,4},{4,7},{5,6},{6,1},{7,0},{8,11},{9,10},{10,... | collective-permute-start | bytes 258056 | tf_op jit(solution)/shard_map/ppermute | solution.py:71
  9.8 2.4 %collective-permute-start.3 = (bf16[336,128]{1,0:T(8,128)(2,1)S(1)}, bf16[336,128]{1,0:T(8,128)(2,1)S(1)}, u32[]{:S(2)}, u32[]{:S(2)}) collective-permute-start(bf16[336,128]{1,0:T(8,128)(2,1)S(1)} %get-tuple-element.36), channel_id=1, source_target_pairs={{0,4},{1,5},{2,6},{3,7},{4,0},{5,1},{6,2},{7,3},{8,12},{9,13},{10,... | collective-permute-start | bytes 258056 | tf_op jit(solution)/shard_map/ppermute | solution.py:71
  12.2 8.4 %collective-permute-done.1.refs_2_ = bf16[336,128]{1,0:T(8,128)(2,1)S(1)} collective-permute-done((bf16[336,128]{1,0:T(8,128)(2,1)S(1)}, bf16[336,128]{1,0:T(8,128)(2,1)S(1)}, u32[]{:S(2)}, u32[]{:S(2)}) %collective-permute-start.1) | collective-permute-done | bytes 86048 | tf_op jit(solution)/shard_map/ppermute | solution.py:71
  20.6 4.1 %collective-permute-start.4 = (bf16[336,128]{1,0:T(8,128)(2,1)S(1)}, bf16[336,128]{1,0:T(8,128)(2,1)S(1)}, u32[]{:S(2)}, u32[]{:S(2)}) collective-permute-start(bf16[336,128]{1,0:T(8,128)(2,1)S(1)} %get-tuple-element.37), channel_id=1, source_target_pairs={{0,5},{1,4},{2,7},{3,6},{4,1},{5,0},{6,3},{7,2},{8,13},{9,12},{10,... | collective-permute-start | bytes 258056 | tf_op jit(solution)/shard_map/ppermute | solution.py:71
  25.7 2.1 %collective-permute-done.4.refs_5_ = bf16[336,128]{1,0:T(8,128)(2,1)S(1)} collective-permute-done((bf16[336,128]{1,0:T(8,128)(2,1)S(1)}, bf16[336,128]{1,0:T(8,128)(2,1)S(1)}, u32[]{:S(2)}, u32[]{:S(2)}) %collective-permute-start.4) | collective-permute-done | bytes 86048 | tf_op jit(solution)/shard_map/ppermute | solution.py:71
  27.8 0.8 collective-permute-done.5.refs_6_
  28.6 1.5 %collective-permute-done.6.refs_7_ = bf16[336,128]{1,0:T(8,128)(2,1)S(1)} collective-permute-done((bf16[336,128]{1,0:T(8,128)(2,1)S(1)}, bf16[336,128]{1,0:T(8,128)(2,1)S(1)}, u32[]{:S(2)}, u32[]{:S(2)}) %collective-permute-start.6) | collective-permute-done | bytes 86048 | tf_op jit(solution)/shard_map/ppermute | solution.py:71
  30.5 3.9 %collective-permute-start.9 = (bf16[40,8320]{1,0:T(8,128)(2,1)S(1)}, bf16[40,8320]{1,0:T(8,128)(2,1)}, u32[]{:S(2)}, u32[]{:S(2)}) collective-permute-start(bf16[40,8320]{1,0:T(8,128)(2,1)S(1)} %unit.1.refs_0_), channel_id=1, source_target_pairs={{0,104},{8,112},{16,120},{24,96},{32,8},{40,16},{48,24},{56,0},{64... | collective-permute-start | bytes 1996808 | tf_op jit(solution)/shard_map/ppermute | solution.py:63
  34.4 1.2 collective-permute-start.8
  35.6 1.6 %collective-permute-start.20 = (bf16[32,128,128]{2,1,0:T(8,128)(2,1)}, bf16[32,128,128]{2,1,0:T(8,128)(2,1)S(1)}, u32[]{:S(2)}, u32[]{:S(2)}) collective-permute-start(bf16[32,128,128]{2,1,0:T(8,128)(2,1)} %refs_0_.1), channel_id=1, source_target_pairs={{0,1},{1,0},{2,3},{3,2},{4,5},{5,4},{6,7},{7,6},{8,9},{9,8},{10,11... | collective-permute-start | bytes 3145736 | tf_op jit(solution)/shard_map/ppermute | solution.py:71
  37.2 2.0 %collective-permute-start.14 = (bf16[2080,128]{1,0:T(8,128)(2,1)S(1)}, bf16[2080,128]{1,0:T(8,128)(2,1)S(1)}, u32[]{:S(2)}, u32[]{:S(2)}) collective-permute-start(bf16[2080,128]{1,0:T(8,128)(2,1)S(1)} %get-tuple-element.42), channel_id=1, source_target_pairs={{0,4},{1,5},{2,6},{3,7},{4,0},{5,1},{6,2},{7,3},{8,12},{9,13},{10,... | collective-permute-start | bytes 1597448 | tf_op jit(solution)/shard_map/ppermute | solution.py:71
  39.2 10.5 %collective-permute-done.9.refs_3_ = bf16[40,8320]{1,0:T(8,128)(2,1)} collective-permute-done((bf16[40,8320]{1,0:T(8,128)(2,1)S(1)}, bf16[40,8320]{1,0:T(8,128)(2,1)}, u32[]{:S(2)}, u32[]{:S(2)}) %collective-permute-start.9) | collective-permute-done | bytes 665632 | tf_op jit(solution)/shard_map/ppermute | solution.py:63
  49.7 2.6 %collective-permute-done.14.refs_0_ = bf16[2080,128]{1,0:T(8,128)(2,1)S(1)} collective-permute-done((bf16[2080,128]{1,0:T(8,128)(2,1)S(1)}, bf16[2080,128]{1,0:T(8,128)(2,1)S(1)}, u32[]{:S(2)}, u32[]{:S(2)}) %collective-permute-start.14) | collective-permute-done | bytes 532512 | tf_op jit(solution)/shard_map/ppermute | solution.py:71
  52.2 0.9 collective-permute-start.19
  56.4 0.8 copy-done.8
  57.2 3.0 %collective-permute-start.11 = (bf16[40,8320]{1,0:T(8,128)(2,1)}, bf16[40,8320]{1,0:T(8,128)(2,1)}, u32[]{:S(2)}, u32[]{:S(2)}) collective-permute-start(bf16[40,8320]{1,0:T(8,128)(2,1)} %collective-permute-done.9.refs_3_), channel_id=1, source_target_pairs={{0,96},{8,104},{16,112},{24,120},{32,0},{40,8},{48,16},{56,24},{64... | collective-permute-start | bytes 1996808 | tf_op jit(solution)/shard_map/ppermute | solution.py:63
  60.2 0.8 copy-done.10
  61.9 2.3 %collective-permute-start.13 = (bf16[40,8320]{1,0:T(8,128)(2,1)}, bf16[40,8320]{1,0:T(8,128)(2,1)}, u32[]{:S(2)}, u32[]{:S(2)}) collective-permute-start(bf16[40,8320]{1,0:T(8,128)(2,1)} %collective-permute-done.8.refs_2_), channel_id=1, source_target_pairs={{0,24},{8,0},{16,8},{24,16},{32,56},{40,32},{48,40},{56,48},{64,88... | collective-permute-start | bytes 1996808 | tf_op jit(solution)/shard_map/ppermute | solution.py:63
  64.1 2.0 %collective-permute-done.10.refs_4_ = bf16[40,8320]{1,0:T(8,128)(2,1)} collective-permute-done((bf16[40,8320]{1,0:T(8,128)(2,1)}, bf16[40,8320]{1,0:T(8,128)(2,1)}, u32[]{:S(2)}, u32[]{:S(2)}) %collective-permute-start.10) | collective-permute-done | bytes 665632 | tf_op jit(solution)/shard_map/ppermute | solution.py:63
  66.2 2.0 %collective-permute-start.22 = (bf16[40,8320]{1,0:T(8,128)(2,1)}, bf16[40,8320]{1,0:T(8,128)(2,1)S(1)}, u32[]{:S(2)}, u32[]{:S(2)}) collective-permute-start(bf16[40,8320]{1,0:T(8,128)(2,1)} %collective-permute-done.10.refs_4_), channel_id=1, source_target_pairs={{0,96},{8,104},{16,112},{24,120},{32,0},{40,8},{48,16},{56,24},{64... | collective-permute-start | bytes 1996808 | tf_op jit(solution)/shard_map/ppermute | solution.py:63
  68.2 2.0 %prepare.1 = (bf16[8,128,256]{2,1,0:T(8,128)(2,1)S(1)}, bf16[8,128,256]{2,1,0:T(8,128)(2,1)S(1)}) custom-call(s32[3]{0:T(128)S(1)} %pad_add_fusion.where, bf16[1024,1024]{1,0:T(8,128)(2,1)} %primal.1, bf16[1024,1024]{1,0:T(8,128)(2,1)} %dual.1), custom_call_target="tpu_custom_call" | custom-call | tf_op jit(solution)/shard_map/prepare/pallas_call | solution.py:188
  70.3 3.2 %reduced.4.refs_2_ = bf16[256,8320]{1,0:T(8,128)(2,1)S(1)} custom-call(s32[3]{0:T(128)S(1)} %pad_add_fusion.where, s32[256]{0:T(256)S(1)} %bitcast.8, bf16[8,128,256]{2,1,0:T(8,128)(2,1)S(1)} %get-tuple-element.40.right, bf16[8,128,256]{2,1,0:T(8,128)(2,1)S(1)} %get-tuple-element.41.left, bf16[32,128,128]{2,1,0:T(8,128)(2,1)S(1)} %copy-done.1, ...), custom_call_target="tpu_custom_call" | custom-call | tf_op jit(solution)/shard_map/reduced/pallas_call | solution.py:242
  73.5 5.4 %reduced.5.refs_2_ = bf16[256,8320]{1,0:T(8,128)(2,1)S(1)} custom-call(s32[3]{0:T(128)S(1)} %pad_add_fusion.where, s32[256]{0:T(256)S(1)} %bitcast.9, bf16[8,128,256]{2,1,0:T(8,128)(2,1)S(1)} %get-tuple-element.40.right, bf16[8,128,256]{2,1,0:T(8,128)(2,1)S(1)} %get-tuple-element.41.left, ...), custom_call_target="tpu_custom_call", output_to_operand_aliasing={{}: (6, {})} | custom-call | tf_op jit(solution)/shard_map/reduced/pallas_call | solution.py:242
  78.9 5.4 %reduced.6.refs_2_ = bf16[256,8320]{1,0:T(8,128)(2,1)S(1)} custom-call(s32[3]{0:T(128)S(1)} %pad_add_fusion.where, s32[256]{0:T(256)S(1)} %bitcast.10, bf16[8,128,256]{2,1,0:T(8,128)(2,1)S(1)} %get-tuple-element.40.right, bf16[8,128,256]{2,1,0:T(8,128)(2,1)S(1)} %get-tuple-element.41.left, ...), custom_call_target="tpu_custom_call", output_to_operand_aliasing={{}: (6, {})} | custom-call | tf_op jit(solution)/shard_map/reduced/pallas_call | solution.py:242
  84.3 5.6 %reduced.7.refs_8_.refs_1_ = bf16[256,8320]{1,0:T(8,128)(2,1)S(1)} custom-call(s32[3]{0:T(128)S(1)} %pad_add_fusion.where, s32[256]{0:T(256)S(1)} %bitcast.11, bf16[8,128,256]{2,1,0:T(8,128)(2,1)S(1)} %get-tuple-element.40.right, bf16[8,128,256]{2,1,0:T(8,128)(2,1)S(1)} %get-tuple-element.41.left, ...), custom_call_target="tpu_custom_call", output_to_operand_aliasing={{}: (6, {})} | custom-call | tf_op jit(solution)/shard_map/reduced/pallas_call | solution.py:242
  90.0 2.4 %contract.4.refs_8_ = f32[40,256]{1,0:T(8,128)S(1)} custom-call(bf16[40,8320]{1,0:T(8,128)(2,1)} %collective-permute-done.21.refs_0_, bf16[256,8320]{1,0:T(8,128)(2,1)S(1)} %reduced.7.refs_8_.refs_1_), custom_call_target="tpu_custom_call" | custom-call | tf_op jit(solution)/shard_map/contract/pallas_call | solution.py:267
  92.4 1.1 collective-permute-start.28
  93.5 3.9 %contract.3 = (f32[40,256]{1,0:T(8,128)S(1)}, f32[40,256]{1,0:T(8,128)S(1)}, f32[40,256]{1,0:T(8,128)S(1)}, f32[40,256]{1,0:T(8,128)S(1)}, f32[40,256]{1,0:T(8,1...) custom-call(bf16[40,8320]{1,0:T(8,128)(2,1)S(1)} %unit.1.refs_0_, ...), custom_call_target="tpu_custom_call" | custom-call | tf_op jit(solution)/shard_map/contract/pallas_call | solution.py:267
  97.5 1.4 %collective-permute-start.24 = (f32[40,256]{1,0:T(8,128)S(1)}, f32[40,256]{1,0:T(8,128)S(1)}, u32[]{:S(2)}, u32[]{:S(2)}) collective-permute-start(f32[40,256]{1,0:T(8,128)S(1)} %get-tuple-element.45.refs_2_), channel_id=1, source_target_pairs={{0,8},{8,16},{16,24},{24,0},{32,40},{40,48},{48,56},{56,32},{64,72... | collective-permute-start | bytes 122888 | tf_op jit(solution)/shard_map/ppermute | solution.py:63
  98.9 2.5 %collective-permute-start.25 = (f32[40,256]{1,0:T(8,128)S(1)}, f32[40,256]{1,0:T(8,128)S(1)}, u32[]{:S(2)}, u32[]{:S(2)}) collective-permute-start(f32[40,256]{1,0:T(8,128)S(1)} %get-tuple-element.46.refs_3_), channel_id=1, source_target_pairs={{0,56},{8,32},{16,40},{24,48},{32,88},{40,64},{48,72},{56,80},{64,... | collective-permute-start | bytes 122888 | tf_op jit(solution)/shard_map/ppermute | solution.py:63
  101.8 4.0 %collective-permute-start.27 = (f32[40,256]{1,0:T(8,128)S(1)}, f32[40,256]{1,0:T(8,128)S(1)}, u32[]{:S(2)}, u32[]{:S(2)}) collective-permute-start(f32[40,256]{1,0:T(8,128)S(1)} %get-tuple-element.48.refs_5_), channel_id=1, source_target_pairs={{0,88},{8,64},{16,72},{24,80},{32,120},{40,96},{48,104},{56,112},{... | collective-permute-start | bytes 122888 | tf_op jit(solution)/shard_map/ppermute | solution.py:63
  105.8 1.3 %contract.5.refs_9_ = f32[40,256]{1,0:T(8,128)S(1)} custom-call(bf16[40,8320]{1,0:T(8,128)(2,1)S(1)} %collective-permute-done.22.refs_0_, bf16[256,8320]{1,0:T(8,128)(2,1)S(1)} %reduced.7.refs_8_.refs_1_), custom_call_target="tpu_custom_call" | custom-call | tf_op jit(solution)/shard_map/contract/pallas_call | solution.py:267
  107.2 1.2 collective-permute-done.26.refs_13_
  109.1 7.3 %collective-permute-start.29 = (f32[2,40,256]{2,1,0:T(8,128)S(1)}, f32[2,40,256]{2,1,0:T(8,128)S(1)}, u32[]{:S(2)}, u32[]{:S(2)}) collective-permute-start(f32[2,40,256]{2,1,0:T(8,128)S(1)} %get-tuple-element.52), channel_id=1, source_target_pairs={{0,1},{1,0},{2,3},{3,2},{4,5},{5,4},{6,7},{7,6},{8,9},{9,8},{10,11... | collective-permute-start | bytes 245768 | tf_op jit(solution)/shard_map/ppermute | solution.py:71
  116.4 1.9 %collective-permute-start.30 = (f32[2,40,256]{2,1,0:T(8,128)S(1)}, f32[2,40,256]{2,1,0:T(8,128)S(1)}, u32[]{:S(2)}, u32[]{:S(2)}) collective-permute-start(f32[2,40,256]{2,1,0:T(8,128)S(1)} %get-tuple-element.53), channel_id=1, source_target_pairs={{0,2},{1,3},{2,4},{3,5},{4,6},{5,7},{6,0},{7,1},{8,10},{9,11},{10,... | collective-permute-start | bytes 245768 | tf_op jit(solution)/shard_map/ppermute | solution.py:71
  118.4 2.6 %collective-permute-start.32 = (f32[2,40,256]{2,1,0:T(8,128)S(1)}, f32[2,40,256]{2,1,0:T(8,128)S(1)}, u32[]{:S(2)}, u32[]{:S(2)}) collective-permute-start(f32[2,40,256]{2,1,0:T(8,128)S(1)} %get-tuple-element.55), channel_id=1, source_target_pairs={{0,4},{1,5},{2,6},{3,7},{4,0},{5,1},{6,2},{7,3},{8,12},{9,13},{10,... | collective-permute-start | bytes 245768 | tf_op jit(solution)/shard_map/ppermute | solution.py:71
  120.9 0.9 collective-permute-start.33
  121.9 2.7 %collective-permute-start.34 = (f32[2,40,256]{2,1,0:T(8,128)S(1)}, f32[2,40,256]{2,1,0:T(8,128)S(1)}, u32[]{:S(2)}, u32[]{:S(2)}) collective-permute-start(f32[2,40,256]{2,1,0:T(8,128)S(1)} %get-tuple-element.57), channel_id=1, source_target_pairs={{0,6},{1,7},{2,0},{3,1},{4,2},{5,3},{6,4},{7,5},{8,14},{9,15},{10,... | collective-permute-start | bytes 245768 | tf_op jit(solution)/shard_map/ppermute | solution.py:71
  125.0 1.0 places.1.hot_ref
  126.0 0.9 collective-permute-done.32.refs_4_
  126.9 2.0 %collective-permute-done.33.refs_5_ = f32[2,40,256]{2,1,0:T(8,128)S(1)} collective-permute-done((f32[2,40,256]{2,1,0:T(8,128)S(1)}, f32[2,40,256]{2,1,0:T(8,128)S(1)}, u32[]{:S(2)}, u32[]{:S(2)}) %collective-permute-start.33) | collective-permute-done | bytes 81952 | tf_op jit(solution)/shard_map/ppermute | solution.py:71
  128.9 1.5 %collective-permute-done.35.refs_7_ = f32[2,40,256]{2,1,0:T(8,128)S(1)} collective-permute-done((f32[2,40,256]{2,1,0:T(8,128)S(1)}, f32[2,40,256]{2,1,0:T(8,128)S(1)}, u32[]{:S(2)}, u32[]{:S(2)}) %collective-permute-start.35) | collective-permute-done | bytes 81952 | tf_op jit(solution)/shard_map/ppermute | solution.py:71
  130.3 2.2 %final.1 = f32[256,512]{1,0:T(8,128)} custom-call(s32[3]{0:T(128)S(1)} %pad_add_fusion.where, bf16[2,256,320]{2,1,0:T(8,128)(2,1)S(1)} %places.1.hot_ref, f32[2,40,256]{2,1,0:T(8,128)S(1)} %get-tuple-element.51.refs_0_, f32[2,40,256]{2,1,0:T(8,128)S(1)} %collective-permute-done.29.refs_1_, f32[2,40,256]{2,1,0:T(8,128)S(1)} %collective-permute-done.30.refs_2_, ...), custom_call_target="tpu_custom_call" | custom-call | tf_op jit(solution)/shard_map/final/pallas_call | solution.py:375
  (71 shorter events, 8.0 us)
Async XLA Ops:
  0.0 70.2 %copy-start.15 = (s32[4096,1]{0,1:T(1,128)S(1)}, s32[4096,1]{0,1:T(1,128)}, u32[]{:S(2)}) copy-start(s32[4096,1]{0,1:T(1,128)} %param.5) | copy-start | bytes 49156
  0.1 1.2 copy-start
  2.0 68.2 %copy-start.1 = (bf16[32,128,128]{2,1,0:T(8,128)(2,1)S(1)}, bf16[32,128,128]{2,1,0:T(8,128)(2,1)}, u32[]{:S(2)}) copy-start(bf16[32,128,128]{2,1,0:T(8,128)(2,1)} %refs_0_.1) | copy-start | bytes 3145732
  3.5 32.1 %collective-permute-start.18 = (bf16[2080,128]{1,0:T(8,128)(2,1)S(1)}, bf16[2080,128]{1,0:T(8,128)(2,1)S(1)}, u32[]{:S(2)}, u32[]{:S(2)}) collective-permute-start(bf16[2080,128]{1,0:T(8,128)(2,1)S(1)} %get-tuple-element.42), channel_id=1, source_target_pairs={{0,2},{1,3},{2,4},{3,5},{4,6},{5,7},{6,0},{7,1},{8,10},{9,11},{10,... | collective-permute-start | bytes 1597448 | tf_op jit(solution)/shard_map/ppermute | solution.py:71
  5.7 31.5 %collective-permute-start.16 = (bf16[2080,128]{1,0:T(8,128)(2,1)S(1)}, bf16[2080,128]{1,0:T(8,128)(2,1)S(1)}, u32[]{:S(2)}, u32[]{:S(2)}) collective-permute-start(bf16[2080,128]{1,0:T(8,128)(2,1)S(1)} %get-tuple-element.42), channel_id=1, source_target_pairs={{0,6},{1,7},{2,0},{3,1},{4,2},{5,3},{6,4},{7,5},{8,14},{9,15},{10,... | collective-permute-start | bytes 1597448 | tf_op jit(solution)/shard_map/ppermute | solution.py:71
  7.2 2.6 %collective-permute-start = (bf16[336,128]{1,0:T(8,128)(2,1)S(1)}, bf16[336,128]{1,0:T(8,128)(2,1)S(1)}, u32[]{:S(2)}, u32[]{:S(2)}) collective-permute-start(bf16[336,128]{1,0:T(8,128)(2,1)S(1)} %get-tuple-element.33), channel_id=1, source_target_pairs={{0,1},{1,0},{2,3},{3,2},{4,5},{5,4},{6,7},{7,6},{8,9},{9,8},{10,11... | collective-permute-start | bytes 258056 | tf_op jit(solution)/shard_map/ppermute | solution.py:71
  8.2 12.5 %collective-permute-start.1 = (bf16[336,128]{1,0:T(8,128)(2,1)S(1)}, bf16[336,128]{1,0:T(8,128)(2,1)S(1)}, u32[]{:S(2)}, u32[]{:S(2)}) collective-permute-start(bf16[336,128]{1,0:T(8,128)(2,1)S(1)} %get-tuple-element.34), channel_id=1, source_target_pairs={{0,2},{1,3},{2,4},{3,5},{4,6},{5,7},{6,0},{7,1},{8,10},{9,11},{10,... | collective-permute-start | bytes 258056 | tf_op jit(solution)/shard_map/ppermute | solution.py:71
  8.4 16.4 %collective-permute-start.2 = (bf16[336,128]{1,0:T(8,128)(2,1)S(1)}, bf16[336,128]{1,0:T(8,128)(2,1)S(1)}, u32[]{:S(2)}, u32[]{:S(2)}) collective-permute-start(bf16[336,128]{1,0:T(8,128)(2,1)S(1)} %get-tuple-element.35), channel_id=1, source_target_pairs={{0,3},{1,2},{2,5},{3,4},{4,7},{5,6},{6,1},{7,0},{8,11},{9,10},{10,... | collective-permute-start | bytes 258056 | tf_op jit(solution)/shard_map/ppermute | solution.py:71
  9.8 15.7 %collective-permute-start.3 = (bf16[336,128]{1,0:T(8,128)(2,1)S(1)}, bf16[336,128]{1,0:T(8,128)(2,1)S(1)}, u32[]{:S(2)}, u32[]{:S(2)}) collective-permute-start(bf16[336,128]{1,0:T(8,128)(2,1)S(1)} %get-tuple-element.36), channel_id=1, source_target_pairs={{0,4},{1,5},{2,6},{3,7},{4,0},{5,1},{6,2},{7,3},{8,12},{9,13},{10,... | collective-permute-start | bytes 258056 | tf_op jit(solution)/shard_map/ppermute | solution.py:71
  20.6 7.1 %collective-permute-start.4 = (bf16[336,128]{1,0:T(8,128)(2,1)S(1)}, bf16[336,128]{1,0:T(8,128)(2,1)S(1)}, u32[]{:S(2)}, u32[]{:S(2)}) collective-permute-start(bf16[336,128]{1,0:T(8,128)(2,1)S(1)} %get-tuple-element.37), channel_id=1, source_target_pairs={{0,5},{1,4},{2,7},{3,6},{4,1},{5,0},{6,3},{7,2},{8,13},{9,12},{10,... | collective-permute-start | bytes 258056 | tf_op jit(solution)/shard_map/ppermute | solution.py:71
  24.8 3.8 %collective-permute-start.5 = (bf16[336,128]{1,0:T(8,128)(2,1)S(1)}, bf16[336,128]{1,0:T(8,128)(2,1)S(1)}, u32[]{:S(2)}, u32[]{:S(2)}) collective-permute-start(bf16[336,128]{1,0:T(8,128)(2,1)S(1)} %get-tuple-element.38), channel_id=1, source_target_pairs={{0,6},{1,7},{2,0},{3,1},{4,2},{5,3},{6,4},{7,5},{8,14},{9,15},{10,... | collective-permute-start | bytes 258056 | tf_op jit(solution)/shard_map/ppermute | solution.py:71
  25.5 4.6 %collective-permute-start.6 = (bf16[336,128]{1,0:T(8,128)(2,1)S(1)}, bf16[336,128]{1,0:T(8,128)(2,1)S(1)}, u32[]{:S(2)}, u32[]{:S(2)}) collective-permute-start(bf16[336,128]{1,0:T(8,128)(2,1)S(1)} %get-tuple-element.39), channel_id=1, source_target_pairs={{0,7},{1,6},{2,1},{3,0},{4,3},{5,2},{6,5},{7,4},{8,15},{9,14},{10,... | collective-permute-start | bytes 258056 | tf_op jit(solution)/shard_map/ppermute | solution.py:71
  30.5 19.2 %collective-permute-start.9 = (bf16[40,8320]{1,0:T(8,128)(2,1)S(1)}, bf16[40,8320]{1,0:T(8,128)(2,1)}, u32[]{:S(2)}, u32[]{:S(2)}) collective-permute-start(bf16[40,8320]{1,0:T(8,128)(2,1)S(1)} %unit.1.refs_0_), channel_id=1, source_target_pairs={{0,104},{8,112},{16,120},{24,96},{32,8},{40,16},{48,24},{56,0},{64... | collective-permute-start | bytes 1996808 | tf_op jit(solution)/shard_map/ppermute | solution.py:63
  34.4 19.6 %collective-permute-start.7 = (bf16[40,8320]{1,0:T(8,128)(2,1)S(1)}, bf16[40,8320]{1,0:T(8,128)(2,1)}, u32[]{:S(2)}, u32[]{:S(2)}) collective-permute-start(bf16[40,8320]{1,0:T(8,128)(2,1)S(1)} %unit.1.refs_0_), channel_id=1, source_target_pairs={{0,32},{8,40},{16,48},{24,56},{32,64},{40,72},{48,80},{56,88},{64,... | collective-permute-start | bytes 1996808 | tf_op jit(solution)/shard_map/ppermute | solution.py:63
  34.4 20.4 %collective-permute-start.8 = (bf16[40,8320]{1,0:T(8,128)(2,1)S(1)}, bf16[40,8320]{1,0:T(8,128)(2,1)}, u32[]{:S(2)}, u32[]{:S(2)}) collective-permute-start(bf16[40,8320]{1,0:T(8,128)(2,1)S(1)} %unit.1.refs_0_), channel_id=1, source_target_pairs={{0,24},{8,0},{16,8},{24,16},{32,56},{40,32},{48,40},{56,48},{64,88... | collective-permute-start | bytes 1996808 | tf_op jit(solution)/shard_map/ppermute | solution.py:63
  35.6 20.5 %collective-permute-start.20 = (bf16[32,128,128]{2,1,0:T(8,128)(2,1)}, bf16[32,128,128]{2,1,0:T(8,128)(2,1)S(1)}, u32[]{:S(2)}, u32[]{:S(2)}) collective-permute-start(bf16[32,128,128]{2,1,0:T(8,128)(2,1)} %refs_0_.1), channel_id=1, source_target_pairs={{0,1},{1,0},{2,3},{3,2},{4,5},{5,4},{6,7},{7,6},{8,9},{9,8},{10,11... | collective-permute-start | bytes 3145736 | tf_op jit(solution)/shard_map/ppermute | solution.py:71
  37.2 15.1 %collective-permute-start.14 = (bf16[2080,128]{1,0:T(8,128)(2,1)S(1)}, bf16[2080,128]{1,0:T(8,128)(2,1)S(1)}, u32[]{:S(2)}, u32[]{:S(2)}) collective-permute-start(bf16[2080,128]{1,0:T(8,128)(2,1)S(1)} %get-tuple-element.42), channel_id=1, source_target_pairs={{0,4},{1,5},{2,6},{3,7},{4,0},{5,1},{6,2},{7,3},{8,12},{9,13},{10,... | collective-permute-start | bytes 1597448 | tf_op jit(solution)/shard_map/ppermute | solution.py:71
  49.7 16.5 %collective-permute-start.10 = (bf16[40,8320]{1,0:T(8,128)(2,1)}, bf16[40,8320]{1,0:T(8,128)(2,1)}, u32[]{:S(2)}, u32[]{:S(2)}) collective-permute-start(bf16[40,8320]{1,0:T(8,128)(2,1)} %collective-permute-done.9.refs_3_), channel_id=1, source_target_pairs={{0,8},{8,16},{16,24},{24,0},{32,40},{40,48},{48,56},{56,32},{64,72... | collective-permute-start | bytes 1996808 | tf_op jit(solution)/shard_map/ppermute | solution.py:63
  52.2 4.1 %collective-permute-start.19 = (bf16[2080,128]{1,0:T(8,128)(2,1)S(1)}, bf16[2080,128]{1,0:T(8,128)(2,1)S(1)}, u32[]{:S(2)}, u32[]{:S(2)}) collective-permute-start(bf16[2080,128]{1,0:T(8,128)(2,1)S(1)} %collective-permute-done.18.refs_0_), channel_id=1, source_target_pairs={{0,1},{1,0},{2,3},{3,2},{4,5},{5,4},{6,7},{7,6},{8,9},{9,8},{10,11... | collective-permute-start | bytes 1597448 | tf_op jit(solution)/shard_map/ppermute | solution.py:71
  54.0 6.2 %collective-permute-start.17 = (bf16[2080,128]{1,0:T(8,128)(2,1)S(1)}, bf16[2080,128]{1,0:T(8,128)(2,1)S(1)}, u32[]{:S(2)}, u32[]{:S(2)}) collective-permute-start(bf16[2080,128]{1,0:T(8,128)(2,1)S(1)} %collective-permute-done.16.refs_0_), channel_id=1, source_target_pairs={{0,1},{1,0},{2,3},{3,2},{4,5},{5,4},{6,7},{7,6},{8,9},{9,8},{10,11... | collective-permute-start | bytes 1597448 | tf_op jit(solution)/shard_map/ppermute | solution.py:71
  54.8 6.2 %collective-permute-start.15 = (bf16[2080,128]{1,0:T(8,128)(2,1)S(1)}, bf16[2080,128]{1,0:T(8,128)(2,1)S(1)}, u32[]{:S(2)}, u32[]{:S(2)}) collective-permute-start(bf16[2080,128]{1,0:T(8,128)(2,1)S(1)} %collective-permute-done.14.refs_0_), channel_id=1, source_target_pairs={{0,1},{1,0},{2,3},{3,2},{4,5},{5,4},{6,7},{7,6},{8,9},{9,8},{10,11... | collective-permute-start | bytes 1597448 | tf_op jit(solution)/shard_map/ppermute | solution.py:71
  56.1 33.8 %collective-permute-start.21 = (bf16[40,8320]{1,0:T(8,128)(2,1)}, bf16[40,8320]{1,0:T(8,128)(2,1)}, u32[]{:S(2)}, u32[]{:S(2)}) collective-permute-start(bf16[40,8320]{1,0:T(8,128)(2,1)} %collective-permute-done.7.refs_1_), channel_id=1, source_target_pairs={{0,8},{8,16},{16,24},{24,0},{32,40},{40,48},{48,56},{56,32},{64,72... | collective-permute-start | bytes 1996808 | tf_op jit(solution)/shard_map/ppermute | solution.py:63
  56.4 0.8 copy-start.8
  57.2 36.3 %collective-permute-start.11 = (bf16[40,8320]{1,0:T(8,128)(2,1)}, bf16[40,8320]{1,0:T(8,128)(2,1)}, u32[]{:S(2)}, u32[]{:S(2)}) collective-permute-start(bf16[40,8320]{1,0:T(8,128)(2,1)} %collective-permute-done.9.refs_3_), channel_id=1, source_target_pairs={{0,96},{8,104},{16,112},{24,120},{32,0},{40,8},{48,16},{56,24},{64... | collective-permute-start | bytes 1996808 | tf_op jit(solution)/shard_map/ppermute | solution.py:63
  60.2 0.9 copy-start.10
  61.0 32.5 %collective-permute-start.12 = (bf16[40,8320]{1,0:T(8,128)(2,1)}, bf16[40,8320]{1,0:T(8,128)(2,1)}, u32[]{:S(2)}, u32[]{:S(2)}) collective-permute-start(bf16[40,8320]{1,0:T(8,128)(2,1)} %collective-permute-done.7.refs_1_), channel_id=1, source_target_pairs={{0,32},{8,40},{16,48},{24,56},{32,64},{40,72},{48,80},{56,88},{64,... | collective-permute-start | bytes 1996808 | tf_op jit(solution)/shard_map/ppermute | solution.py:63
  61.0 0.8 copy-start.12
  61.9 31.7 %collective-permute-start.13 = (bf16[40,8320]{1,0:T(8,128)(2,1)}, bf16[40,8320]{1,0:T(8,128)(2,1)}, u32[]{:S(2)}, u32[]{:S(2)}) collective-permute-start(bf16[40,8320]{1,0:T(8,128)(2,1)} %collective-permute-done.8.refs_2_), channel_id=1, source_target_pairs={{0,24},{8,0},{16,8},{24,16},{32,56},{40,32},{48,40},{56,48},{64,88... | collective-permute-start | bytes 1996808 | tf_op jit(solution)/shard_map/ppermute | solution.py:63
  66.2 35.6 %collective-permute-start.22 = (bf16[40,8320]{1,0:T(8,128)(2,1)}, bf16[40,8320]{1,0:T(8,128)(2,1)S(1)}, u32[]{:S(2)}, u32[]{:S(2)}) collective-permute-start(bf16[40,8320]{1,0:T(8,128)(2,1)} %collective-permute-done.10.refs_4_), channel_id=1, source_target_pairs={{0,96},{8,104},{16,112},{24,120},{32,0},{40,8},{48,16},{56,24},{64... | collective-permute-start | bytes 1996808 | tf_op jit(solution)/shard_map/ppermute | solution.py:63
  70.2 3.2 %copy-start.3 = (bf16[2080,128]{1,0:T(8,128)(2,1)S(1)}, bf16[2080,128]{1,0:T(8,128)(2,1)}, u32[]{:S(2)}) copy-start(bf16[2080,128]{1,0:T(8,128)(2,1)} %copy-done.2) | copy-start | bytes 1597444
  70.2 3.2 %copy-start.9 = (bf16[2080,128]{1,0:T(8,128)(2,1)S(1)}, bf16[2080,128]{1,0:T(8,128)(2,1)}, u32[]{:S(2)}) copy-start(bf16[2080,128]{1,0:T(8,128)(2,1)} %copy-done.8) | copy-start | bytes 1597444
  73.5 5.4 %copy-start.5 = (bf16[2080,128]{1,0:T(8,128)(2,1)S(1)}, bf16[2080,128]{1,0:T(8,128)(2,1)}, u32[]{:S(2)}) copy-start(bf16[2080,128]{1,0:T(8,128)(2,1)} %copy-done.4) | copy-start | bytes 1597444
  73.5 5.4 %copy-start.11 = (bf16[2080,128]{1,0:T(8,128)(2,1)S(1)}, bf16[2080,128]{1,0:T(8,128)(2,1)}, u32[]{:S(2)}) copy-start(bf16[2080,128]{1,0:T(8,128)(2,1)} %copy-done.10) | copy-start | bytes 1597444
  78.9 5.4 %copy-start.7 = (bf16[2080,128]{1,0:T(8,128)(2,1)S(1)}, bf16[2080,128]{1,0:T(8,128)(2,1)}, u32[]{:S(2)}) copy-start(bf16[2080,128]{1,0:T(8,128)(2,1)} %copy-done.6) | copy-start | bytes 1597444
  78.9 5.4 %copy-start.13 = (bf16[2080,128]{1,0:T(8,128)(2,1)S(1)}, bf16[2080,128]{1,0:T(8,128)(2,1)}, u32[]{:S(2)}) copy-start(bf16[2080,128]{1,0:T(8,128)(2,1)} %copy-done.12) | copy-start | bytes 1597444
  92.4 9.0 %collective-permute-start.28 = (f32[40,256]{1,0:T(8,128)S(1)}, f32[40,256]{1,0:T(8,128)S(1)}, u32[]{:S(2)}, u32[]{:S(2)}) collective-permute-start(f32[40,256]{1,0:T(8,128)S(1)} %contract.4.refs_8_), channel_id=1, source_target_pairs={{0,120},{8,96},{16,104},{24,112},{32,24},{40,0},{48,8},{56,16},{64... | collective-permute-start | bytes 122888 | tf_op jit(solution)/shard_map/ppermute | solution.py:63
  97.4 9.7 %collective-permute-start.23 = (f32[40,256]{1,0:T(8,128)S(1)}, f32[40,256]{1,0:T(8,128)S(1)}, u32[]{:S(2)}, u32[]{:S(2)}) collective-permute-start(f32[40,256]{1,0:T(8,128)S(1)} %get-tuple-element.44.refs_1_), channel_id=1, source_target_pairs={{0,96},{8,104},{16,112},{24,120},{32,0},{40,8},{48,16},{56,24},{64... | collective-permute-start | bytes 122888 | tf_op jit(solution)/shard_map/ppermute | solution.py:63
  97.5 9.6 %collective-permute-start.24 = (f32[40,256]{1,0:T(8,128)S(1)}, f32[40,256]{1,0:T(8,128)S(1)}, u32[]{:S(2)}, u32[]{:S(2)}) collective-permute-start(f32[40,256]{1,0:T(8,128)S(1)} %get-tuple-element.45.refs_2_), channel_id=1, source_target_pairs={{0,8},{8,16},{16,24},{24,0},{32,40},{40,48},{48,56},{56,32},{64,72... | collective-permute-start | bytes 122888 | tf_op jit(solution)/shard_map/ppermute | solution.py:63
  98.9 8.3 %collective-permute-start.25 = (f32[40,256]{1,0:T(8,128)S(1)}, f32[40,256]{1,0:T(8,128)S(1)}, u32[]{:S(2)}, u32[]{:S(2)}) collective-permute-start(f32[40,256]{1,0:T(8,128)S(1)} %get-tuple-element.46.refs_3_), channel_id=1, source_target_pairs={{0,56},{8,32},{16,40},{24,48},{32,88},{40,64},{48,72},{56,80},{64,... | collective-permute-start | bytes 122888 | tf_op jit(solution)/shard_map/ppermute | solution.py:63
  101.4 6.9 %collective-permute-start.26 = (f32[40,256]{1,0:T(8,128)S(1)}, f32[40,256]{1,0:T(8,128)S(1)}, u32[]{:S(2)}, u32[]{:S(2)}) collective-permute-start(f32[40,256]{1,0:T(8,128)S(1)} %get-tuple-element.47.refs_4_), channel_id=1, source_target_pairs={{0,48},{8,56},{16,32},{24,40},{32,80},{40,88},{48,64},{56,72},{64,... | collective-permute-start | bytes 122888 | tf_op jit(solution)/shard_map/ppermute | solution.py:63
  101.8 6.6 %collective-permute-start.27 = (f32[40,256]{1,0:T(8,128)S(1)}, f32[40,256]{1,0:T(8,128)S(1)}, u32[]{:S(2)}, u32[]{:S(2)}) collective-permute-start(f32[40,256]{1,0:T(8,128)S(1)} %get-tuple-element.48.refs_5_), channel_id=1, source_target_pairs={{0,88},{8,64},{16,72},{24,80},{32,120},{40,96},{48,104},{56,112},{... | collective-permute-start | bytes 122888 | tf_op jit(solution)/shard_map/ppermute | solution.py:63
  109.1 12.8 %collective-permute-start.29 = (f32[2,40,256]{2,1,0:T(8,128)S(1)}, f32[2,40,256]{2,1,0:T(8,128)S(1)}, u32[]{:S(2)}, u32[]{:S(2)}) collective-permute-start(f32[2,40,256]{2,1,0:T(8,128)S(1)} %get-tuple-element.52), channel_id=1, source_target_pairs={{0,1},{1,0},{2,3},{3,2},{4,5},{5,4},{6,7},{7,6},{8,9},{9,8},{10,11... | collective-permute-start | bytes 245768 | tf_op jit(solution)/shard_map/ppermute | solution.py:71
  116.4 8.2 %collective-permute-start.30 = (f32[2,40,256]{2,1,0:T(8,128)S(1)}, f32[2,40,256]{2,1,0:T(8,128)S(1)}, u32[]{:S(2)}, u32[]{:S(2)}) collective-permute-start(f32[2,40,256]{2,1,0:T(8,128)S(1)} %get-tuple-element.53), channel_id=1, source_target_pairs={{0,2},{1,3},{2,4},{3,5},{4,6},{5,7},{6,0},{7,1},{8,10},{9,11},{10,... | collective-permute-start | bytes 245768 | tf_op jit(solution)/shard_map/ppermute | solution.py:71
  118.3 7.6 %collective-permute-start.31 = (f32[2,40,256]{2,1,0:T(8,128)S(1)}, f32[2,40,256]{2,1,0:T(8,128)S(1)}, u32[]{:S(2)}, u32[]{:S(2)}) collective-permute-start(f32[2,40,256]{2,1,0:T(8,128)S(1)} %get-tuple-element.54), channel_id=1, source_target_pairs={{0,3},{1,2},{2,5},{3,4},{4,7},{5,6},{6,1},{7,0},{8,11},{9,10},{10,... | collective-permute-start | bytes 245768 | tf_op jit(solution)/shard_map/ppermute | solution.py:71
  118.4 8.5 %collective-permute-start.32 = (f32[2,40,256]{2,1,0:T(8,128)S(1)}, f32[2,40,256]{2,1,0:T(8,128)S(1)}, u32[]{:S(2)}, u32[]{:S(2)}) collective-permute-start(f32[2,40,256]{2,1,0:T(8,128)S(1)} %get-tuple-element.55), channel_id=1, source_target_pairs={{0,4},{1,5},{2,6},{3,7},{4,0},{5,1},{6,2},{7,3},{8,12},{9,13},{10,... | collective-permute-start | bytes 245768 | tf_op jit(solution)/shard_map/ppermute | solution.py:71
  120.9 7.9 %collective-permute-start.33 = (f32[2,40,256]{2,1,0:T(8,128)S(1)}, f32[2,40,256]{2,1,0:T(8,128)S(1)}, u32[]{:S(2)}, u32[]{:S(2)}) collective-permute-start(f32[2,40,256]{2,1,0:T(8,128)S(1)} %get-tuple-element.56), channel_id=1, source_target_pairs={{0,5},{1,4},{2,7},{3,6},{4,1},{5,0},{6,3},{7,2},{8,13},{9,12},{10,... | collective-permute-start | bytes 245768 | tf_op jit(solution)/shard_map/ppermute | solution.py:71
  121.9 7.0 %collective-permute-start.34 = (f32[2,40,256]{2,1,0:T(8,128)S(1)}, f32[2,40,256]{2,1,0:T(8,128)S(1)}, u32[]{:S(2)}, u32[]{:S(2)}) collective-permute-start(f32[2,40,256]{2,1,0:T(8,128)S(1)} %get-tuple-element.57), channel_id=1, source_target_pairs={{0,6},{1,7},{2,0},{3,1},{4,2},{5,3},{6,4},{7,5},{8,14},{9,15},{10,... | collective-permute-start | bytes 245768 | tf_op jit(solution)/shard_map/ppermute | solution.py:71
  124.5 5.8 %collective-permute-start.35 = (f32[2,40,256]{2,1,0:T(8,128)S(1)}, f32[2,40,256]{2,1,0:T(8,128)S(1)}, u32[]{:S(2)}, u32[]{:S(2)}) collective-permute-start(f32[2,40,256]{2,1,0:T(8,128)S(1)} %get-tuple-element.58), channel_id=1, source_target_pairs={{0,7},{1,6},{2,1},{3,0},{4,3},{5,2},{6,5},{7,4},{8,15},{9,14},{10,... | collective-permute-start | bytes 245768 | tf_op jit(solution)/shard_map/ppermute | solution.py:71
  (4 other events, 3.1 us)

commit v4 on v3

--- a/solution.py
+++ b/solution.py
@@ -96,7 +96,12 @@
 
 
 def fold_kernel(where, tiles, own_ref, *refs):
-    outs, plain, held, lasts, ends, counts = refs[:8], *refs[8:]
+    outs, plain, held, lasts, ends, counts, near_ref, sems = refs[:8], *refs[8:]
+    loads = []
+    for n in range(4):
+        rows = pl.ds(n * 8, 8)
+        loads.append(pltpu.make_async_copy(own_ref.at[rows], near_ref.at[rows], sems.at[n]))
+        loads[n].start()
     held[...] = jnp.zeros(held.shape, held.dtype)
     lasts[...] = jnp.zeros(lasts.shape, lasts.dtype)
     for k in range(8):
@@ -104,23 +109,21 @@
     y, core = where[1], where[2]
     mine = where[0] * 256 + y * 64 + core * 32
 
-    def four(n, carry):
+    for n in range(4):
+        loads[n].wait()
         for m in range(8):
             i = n * 8 + m
             t = tiles[mine + i]
             order = counts[t]
             counts[t] = order + 1
             goal = lax.rem(t // 2 - y + 4, 4) * 2 + lax.rem(t + core, 2)
-            kept, last = folded(own_ref[i].astype(jnp.float32), False)
+            kept, last = folded(near_ref[i].astype(jnp.float32), False)
             row = pl.multiple_of(goal * PIECE + order * H, 16)
             kept = kept.astype(held.dtype)
             held[pl.ds(row, H), :] = kept
-            plain[pl.ds(pl.multiple_of(i * H, H), H), :] = kept
-            ends[pl.ds(i, 1), :] = last
+            plain[i * H : (i + 1) * H, :] = kept
+            ends[i : i + 1, :] = last
             lasts[pl.ds(goal * 16 + order, 1), :] = last
-        return carry
-
-    lax.fori_loop(0, 4, four, 0)
     plain[32 * H :, :] = ends[...].astype(plain.dtype)
     for k in range(8):
         outs[k][: MOST * H, :] = held[k * PIECE : k * PIECE + MOST * H, :]
@@ -131,17 +134,19 @@
     return pl.pallas_call(
         fold_kernel,
         out_shape=[made(PIECE, K)] * 8 + [made(32 * H + 32, K)],
-        in_specs=[SMEM, SMEM, VMEM],
+        in_specs=[SMEM, SMEM, HBM],
         out_specs=[VMEM] * 9,
         scratch_shapes=[
             pltpu.VMEM((8 * PIECE, K), jnp.bfloat16),
             pltpu.VMEM((8 * 16, K), jnp.float32),
             pltpu.VMEM((32, K), jnp.float32),
             pltpu.SMEM((8,), jnp.int32),
+            pltpu.VMEM((32, K, K), jnp.bfloat16),
+            pltpu.SemaphoreType.DMA((4,)),
         ],
         compiler_params=LIMIT,
         name="fold",
-    )(where, tiles, own)
+    )(where, far(tiles), far(own))
 
 
 def unit_kernel(*refs):

time: 133 us -> 133 us (level)
  local copies, waits for them, and re-layouts: 6.92 us -> 4.98 us
  Pallas kernels: 35 us -> 36.4 us
    unnamed x32 -> x28, local copies, waits for them, and re-layouts: 6.9 us -> 4.97 us
where the time goes in v4:
time: 133 us; the launch traced here: 132 us
  starting transfers between devices  56.8 us (43%)
  Pallas kernels  36.4 us (27%)
  waiting for transfers between devices  33.6 us (25%)
  local copies, waits for them, and re-layouts  4.98 us (4%)
    ppermute x21, starting transfers between devices, line_shift(): return lax.ppermute(x, LINE, pairs)  34.7 us
    ppermute x15, starting transfers between devices, plane_shift(): return lax.ppermute(x, PLANE, pairs)  22 us
    pallas_call x4, Pallas kernels, reduce_call(): pl.pallas_call(functools.partial(reduce_kernel, plan, total is not None),...  19.9 us
    ppermute x21, waiting for transfers between devices, line_shift(): return lax.ppermute(x, LINE, pairs)  19.8 us
    ppermute x15, waiting for transfers between devices, plane_shift(): return lax.ppermute(x, PLANE, pairs)  13.7 us
    pallas_call x3, Pallas kernels, contract_call(): pl.pallas_call(functools.partial(contract_kernel, n), out_shape=[made(UNI...  7.65 us
    unnamed x28, local copies, waits for them, and re-layouts  4.97 us
  transfers between devices with their start and end apart: 36, of which 11 were waited for; matrix products, arithmetic and copies ran while one was open for 0% of the time, Pallas kernels for 23%

profile of v4, /device:TPU:1, one launch (start us, length us, event | category | flops | bytes accessed | tf_op | source)
XLA Modules:
  0.0 132.2 jit_solution(16874764346738573234)
XLA Ops:
  0.1 2.5 %fold.1 = (bf16[336,128]{1,0:T(8,128)(2,1)S(1)}, bf16[336,128]{1,0:T(8,128)(2,1)S(1)}, bf16[336,128]{1,0:T(8,128)(2,1)S(1)}, bf16[336,128]{1,0:T(8,128)(2,1)S(1)...) custom-call(s32[3]{0:T(128)S(1)} %pad_add_fusion.where, ...), custom_call_target="tpu_custom_call" | custom-call | tf_op jit(solution)/shard_map/fold/pallas_call | solution.py:134
  2.6 2.2 %collective-permute-start.18 = (bf16[2080,128]{1,0:T(8,128)(2,1)S(1)}, bf16[2080,128]{1,0:T(8,128)(2,1)S(1)}, u32[]{:S(2)}, u32[]{:S(2)}) collective-permute-start(bf16[2080,128]{1,0:T(8,128)(2,1)S(1)} %get-tuple-element.42), channel_id=1, source_target_pairs={{0,2},{1,3},{2,4},{3,5},{4,6},{5,7},{6,0},{7,1},{8,10},{9,11},{10,... | collective-permute-start | bytes 1597448 | tf_op jit(solution)/shard_map/ppermute | solution.py:71
  4.8 1.5 %collective-permute-start.16 = (bf16[2080,128]{1,0:T(8,128)(2,1)S(1)}, bf16[2080,128]{1,0:T(8,128)(2,1)S(1)}, u32[]{:S(2)}, u32[]{:S(2)}) collective-permute-start(bf16[2080,128]{1,0:T(8,128)(2,1)S(1)} %get-tuple-element.42), channel_id=1, source_target_pairs={{0,6},{1,7},{2,0},{3,1},{4,2},{5,3},{6,4},{7,5},{8,14},{9,15},{10,... | collective-permute-start | bytes 1597448 | tf_op jit(solution)/shard_map/ppermute | solution.py:71
  6.3 1.0 collective-permute-start
  7.5 1.5 %collective-permute-start.2 = (bf16[336,128]{1,0:T(8,128)(2,1)S(1)}, bf16[336,128]{1,0:T(8,128)(2,1)S(1)}, u32[]{:S(2)}, u32[]{:S(2)}) collective-permute-start(bf16[336,128]{1,0:T(8,128)(2,1)S(1)} %get-tuple-element.35), channel_id=1, source_target_pairs={{0,3},{1,2},{2,5},{3,4},{4,7},{5,6},{6,1},{7,0},{8,11},{9,10},{10,... | collective-permute-start | bytes 258056 | tf_op jit(solution)/shard_map/ppermute | solution.py:71
  9.0 2.4 %collective-permute-start.3 = (bf16[336,128]{1,0:T(8,128)(2,1)S(1)}, bf16[336,128]{1,0:T(8,128)(2,1)S(1)}, u32[]{:S(2)}, u32[]{:S(2)}) collective-permute-start(bf16[336,128]{1,0:T(8,128)(2,1)S(1)} %get-tuple-element.36), channel_id=1, source_target_pairs={{0,4},{1,5},{2,6},{3,7},{4,0},{5,1},{6,2},{7,3},{8,12},{9,13},{10,... | collective-permute-start | bytes 258056 | tf_op jit(solution)/shard_map/ppermute | solution.py:71
  11.3 8.4 %collective-permute-done.1.refs_2_ = bf16[336,128]{1,0:T(8,128)(2,1)S(1)} collective-permute-done((bf16[336,128]{1,0:T(8,128)(2,1)S(1)}, bf16[336,128]{1,0:T(8,128)(2,1)S(1)}, u32[]{:S(2)}, u32[]{:S(2)}) %collective-permute-start.1) | collective-permute-done | bytes 86048 | tf_op jit(solution)/shard_map/ppermute | solution.py:71
  19.8 4.1 %collective-permute-start.4 = (bf16[336,128]{1,0:T(8,128)(2,1)S(1)}, bf16[336,128]{1,0:T(8,128)(2,1)S(1)}, u32[]{:S(2)}, u32[]{:S(2)}) collective-permute-start(bf16[336,128]{1,0:T(8,128)(2,1)S(1)} %get-tuple-element.37), channel_id=1, source_target_pairs={{0,5},{1,4},{2,7},{3,6},{4,1},{5,0},{6,3},{7,2},{8,13},{9,12},{10,... | collective-permute-start | bytes 258056 | tf_op jit(solution)/shard_map/ppermute | solution.py:71
  24.8 2.1 %collective-permute-done.4.refs_5_ = bf16[336,128]{1,0:T(8,128)(2,1)S(1)} collective-permute-done((bf16[336,128]{1,0:T(8,128)(2,1)S(1)}, bf16[336,128]{1,0:T(8,128)(2,1)S(1)}, u32[]{:S(2)}, u32[]{:S(2)}) %collective-permute-start.4) | collective-permute-done | bytes 86048 | tf_op jit(solution)/shard_map/ppermute | solution.py:71
  26.9 0.8 collective-permute-done.5.refs_6_
  27.8 1.5 %collective-permute-done.6.refs_7_ = bf16[336,128]{1,0:T(8,128)(2,1)S(1)} collective-permute-done((bf16[336,128]{1,0:T(8,128)(2,1)S(1)}, bf16[336,128]{1,0:T(8,128)(2,1)S(1)}, u32[]{:S(2)}, u32[]{:S(2)}) %collective-permute-start.6) | collective-permute-done | bytes 86048 | tf_op jit(solution)/shard_map/ppermute | solution.py:71
  29.6 3.9 %collective-permute-start.9 = (bf16[40,8320]{1,0:T(8,128)(2,1)S(1)}, bf16[40,8320]{1,0:T(8,128)(2,1)}, u32[]{:S(2)}, u32[]{:S(2)}) collective-permute-start(bf16[40,8320]{1,0:T(8,128)(2,1)S(1)} %unit.1.refs_0_), channel_id=1, source_target_pairs={{0,104},{8,112},{16,120},{24,96},{32,8},{40,16},{48,24},{56,0},{64... | collective-permute-start | bytes 1996808 | tf_op jit(solution)/shard_map/ppermute | solution.py:63
  33.5 1.2 collective-permute-start.8
  34.8 1.6 %collective-permute-start.20 = (bf16[32,128,128]{2,1,0:T(8,128)(2,1)}, bf16[32,128,128]{2,1,0:T(8,128)(2,1)S(1)}, u32[]{:S(2)}, u32[]{:S(2)}) collective-permute-start(bf16[32,128,128]{2,1,0:T(8,128)(2,1)} %refs_0_.1), channel_id=1, source_target_pairs={{0,1},{1,0},{2,3},{3,2},{4,5},{5,4},{6,7},{7,6},{8,9},{9,8},{10,11... | collective-permute-start | bytes 3145736 | tf_op jit(solution)/shard_map/ppermute | solution.py:71
  36.3 2.0 %collective-permute-start.14 = (bf16[2080,128]{1,0:T(8,128)(2,1)S(1)}, bf16[2080,128]{1,0:T(8,128)(2,1)S(1)}, u32[]{:S(2)}, u32[]{:S(2)}) collective-permute-start(bf16[2080,128]{1,0:T(8,128)(2,1)S(1)} %get-tuple-element.42), channel_id=1, source_target_pairs={{0,4},{1,5},{2,6},{3,7},{4,0},{5,1},{6,2},{7,3},{8,12},{9,13},{10,... | collective-permute-start | bytes 1597448 | tf_op jit(solution)/shard_map/ppermute | solution.py:71
  38.3 10.5 %collective-permute-done.9.refs_3_ = bf16[40,8320]{1,0:T(8,128)(2,1)} collective-permute-done((bf16[40,8320]{1,0:T(8,128)(2,1)S(1)}, bf16[40,8320]{1,0:T(8,128)(2,1)}, u32[]{:S(2)}, u32[]{:S(2)}) %collective-permute-start.9) | collective-permute-done | bytes 665632 | tf_op jit(solution)/shard_map/ppermute | solution.py:63
  48.8 2.6 %collective-permute-done.14.refs_0_ = bf16[2080,128]{1,0:T(8,128)(2,1)S(1)} collective-permute-done((bf16[2080,128]{1,0:T(8,128)(2,1)S(1)}, bf16[2080,128]{1,0:T(8,128)(2,1)S(1)}, u32[]{:S(2)}, u32[]{:S(2)}) %collective-permute-start.14) | collective-permute-done | bytes 532512 | tf_op jit(solution)/shard_map/ppermute | solution.py:71
  51.4 0.9 collective-permute-start.19
  53.1 0.8 copy-done.3
  55.5 0.8 copy-done.7
  56.4 3.0 %collective-permute-start.11 = (bf16[40,8320]{1,0:T(8,128)(2,1)}, bf16[40,8320]{1,0:T(8,128)(2,1)}, u32[]{:S(2)}, u32[]{:S(2)}) collective-permute-start(bf16[40,8320]{1,0:T(8,128)(2,1)} %collective-permute-done.9.refs_3_), channel_id=1, source_target_pairs={{0,96},{8,104},{16,112},{24,120},{32,0},{40,8},{48,16},{56,24},{64... | collective-permute-start | bytes 1996808 | tf_op jit(solution)/shard_map/ppermute | solution.py:63
  59.3 0.8 copy-done.9
  61.0 2.3 %collective-permute-start.13 = (bf16[40,8320]{1,0:T(8,128)(2,1)}, bf16[40,8320]{1,0:T(8,128)(2,1)}, u32[]{:S(2)}, u32[]{:S(2)}) collective-permute-start(bf16[40,8320]{1,0:T(8,128)(2,1)} %collective-permute-done.8.refs_2_), channel_id=1, source_target_pairs={{0,24},{8,0},{16,8},{24,16},{32,56},{40,32},{48,40},{56,48},{64,88... | collective-permute-start | bytes 1996808 | tf_op jit(solution)/shard_map/ppermute | solution.py:63
  63.3 2.0 %collective-permute-done.10.refs_4_ = bf16[40,8320]{1,0:T(8,128)(2,1)} collective-permute-done((bf16[40,8320]{1,0:T(8,128)(2,1)}, bf16[40,8320]{1,0:T(8,128)(2,1)}, u32[]{:S(2)}, u32[]{:S(2)}) %collective-permute-start.10) | collective-permute-done | bytes 665632 | tf_op jit(solution)/shard_map/ppermute | solution.py:63
  65.3 2.0 %collective-permute-start.22 = (bf16[40,8320]{1,0:T(8,128)(2,1)}, bf16[40,8320]{1,0:T(8,128)(2,1)S(1)}, u32[]{:S(2)}, u32[]{:S(2)}) collective-permute-start(bf16[40,8320]{1,0:T(8,128)(2,1)} %collective-permute-done.10.refs_4_), channel_id=1, source_target_pairs={{0,96},{8,104},{16,112},{24,120},{32,0},{40,8},{48,16},{56,24},{64... | collective-permute-start | bytes 1996808 | tf_op jit(solution)/shard_map/ppermute | solution.py:63
  67.3 2.0 %prepare.1 = (bf16[8,128,256]{2,1,0:T(8,128)(2,1)S(1)}, bf16[8,128,256]{2,1,0:T(8,128)(2,1)S(1)}) custom-call(s32[3]{0:T(128)S(1)} %pad_add_fusion.where, bf16[1024,1024]{1,0:T(8,128)(2,1)} %primal.1, bf16[1024,1024]{1,0:T(8,128)(2,1)} %dual.1), custom_call_target="tpu_custom_call" | custom-call | tf_op jit(solution)/shard_map/prepare/pallas_call | solution.py:193
  69.4 3.2 %reduced.4.refs_2_ = bf16[256,8320]{1,0:T(8,128)(2,1)S(1)} custom-call(s32[3]{0:T(128)S(1)} %pad_add_fusion.where, s32[256]{0:T(256)S(1)} %bitcast.8, bf16[8,128,256]{2,1,0:T(8,128)(2,1)S(1)} %get-tuple-element.40.right, bf16[8,128,256]{2,1,0:T(8,128)(2,1)S(1)} %get-tuple-element.41.left, bf16[32,128,128]{2,1,0:T(8,128)(2,1)S(1)} %copy-done, ...), custom_call_target="tpu_custom_call" | custom-call | tf_op jit(solution)/shard_map/reduced/pallas_call | solution.py:247
  72.7 5.5 %reduced.5.refs_2_ = bf16[256,8320]{1,0:T(8,128)(2,1)S(1)} custom-call(s32[3]{0:T(128)S(1)} %pad_add_fusion.where, s32[256]{0:T(256)S(1)} %bitcast.9, bf16[8,128,256]{2,1,0:T(8,128)(2,1)S(1)} %get-tuple-element.40.right, bf16[8,128,256]{2,1,0:T(8,128)(2,1)S(1)} %get-tuple-element.41.left, ...), custom_call_target="tpu_custom_call", output_to_operand_aliasing={{}: (6, {})} | custom-call | tf_op jit(solution)/shard_map/reduced/pallas_call | solution.py:247
  78.2 5.5 %reduced.6.refs_2_ = bf16[256,8320]{1,0:T(8,128)(2,1)S(1)} custom-call(s32[3]{0:T(128)S(1)} %pad_add_fusion.where, s32[256]{0:T(256)S(1)} %bitcast.10, bf16[8,128,256]{2,1,0:T(8,128)(2,1)S(1)} %get-tuple-element.40.right, bf16[8,128,256]{2,1,0:T(8,128)(2,1)S(1)} %get-tuple-element.41.left, ...), custom_call_target="tpu_custom_call", output_to_operand_aliasing={{}: (6, {})} | custom-call | tf_op jit(solution)/shard_map/reduced/pallas_call | solution.py:247
  83.7 5.7 %reduced.7.refs_8_.refs_1_ = bf16[256,8320]{1,0:T(8,128)(2,1)S(1)} custom-call(s32[3]{0:T(128)S(1)} %pad_add_fusion.where, s32[256]{0:T(256)S(1)} %bitcast.11, bf16[8,128,256]{2,1,0:T(8,128)(2,1)S(1)} %get-tuple-element.40.right, bf16[8,128,256]{2,1,0:T(8,128)(2,1)S(1)} %get-tuple-element.41.left, ...), custom_call_target="tpu_custom_call", output_to_operand_aliasing={{}: (6, {})} | custom-call | tf_op jit(solution)/shard_map/reduced/pallas_call | solution.py:247
  89.4 2.4 %contract.4.refs_8_ = f32[40,256]{1,0:T(8,128)S(1)} custom-call(bf16[40,8320]{1,0:T(8,128)(2,1)} %collective-permute-done.21.refs_0_, bf16[256,8320]{1,0:T(8,128)(2,1)S(1)} %reduced.7.refs_8_.refs_1_), custom_call_target="tpu_custom_call" | custom-call | tf_op jit(solution)/shard_map/contract/pallas_call | solution.py:272
  91.9 1.1 collective-permute-start.28
  93.0 3.9 %contract.3 = (f32[40,256]{1,0:T(8,128)S(1)}, f32[40,256]{1,0:T(8,128)S(1)}, f32[40,256]{1,0:T(8,128)S(1)}, f32[40,256]{1,0:T(8,128)S(1)}, f32[40,256]{1,0:T(8,1...) custom-call(bf16[40,8320]{1,0:T(8,128)(2,1)S(1)} %unit.1.refs_0_, ...), custom_call_target="tpu_custom_call" | custom-call | tf_op jit(solution)/shard_map/contract/pallas_call | solution.py:272
  97.0 1.4 %collective-permute-start.24 = (f32[40,256]{1,0:T(8,128)S(1)}, f32[40,256]{1,0:T(8,128)S(1)}, u32[]{:S(2)}, u32[]{:S(2)}) collective-permute-start(f32[40,256]{1,0:T(8,128)S(1)} %get-tuple-element.45.refs_2_), channel_id=1, source_target_pairs={{0,8},{8,16},{16,24},{24,0},{32,40},{40,48},{48,56},{56,32},{64,72... | collective-permute-start | bytes 122888 | tf_op jit(solution)/shard_map/ppermute | solution.py:63
  98.4 2.5 %collective-permute-start.25 = (f32[40,256]{1,0:T(8,128)S(1)}, f32[40,256]{1,0:T(8,128)S(1)}, u32[]{:S(2)}, u32[]{:S(2)}) collective-permute-start(f32[40,256]{1,0:T(8,128)S(1)} %get-tuple-element.46.refs_3_), channel_id=1, source_target_pairs={{0,56},{8,32},{16,40},{24,48},{32,88},{40,64},{48,72},{56,80},{64,... | collective-permute-start | bytes 122888 | tf_op jit(solution)/shard_map/ppermute | solution.py:63
  101.3 4.0 %collective-permute-start.27 = (f32[40,256]{1,0:T(8,128)S(1)}, f32[40,256]{1,0:T(8,128)S(1)}, u32[]{:S(2)}, u32[]{:S(2)}) collective-permute-start(f32[40,256]{1,0:T(8,128)S(1)} %get-tuple-element.48.refs_5_), channel_id=1, source_target_pairs={{0,88},{8,64},{16,72},{24,80},{32,120},{40,96},{48,104},{56,112},{... | collective-permute-start | bytes 122888 | tf_op jit(solution)/shard_map/ppermute | solution.py:63
  105.2 1.3 %contract.5.refs_9_ = f32[40,256]{1,0:T(8,128)S(1)} custom-call(bf16[40,8320]{1,0:T(8,128)(2,1)S(1)} %collective-permute-done.22.refs_0_, bf16[256,8320]{1,0:T(8,128)(2,1)S(1)} %reduced.7.refs_8_.refs_1_), custom_call_target="tpu_custom_call" | custom-call | tf_op jit(solution)/shard_map/contract/pallas_call | solution.py:272
  106.6 1.2 collective-permute-done.26.refs_13_
  108.5 7.4 %collective-permute-start.29 = (f32[2,40,256]{2,1,0:T(8,128)S(1)}, f32[2,40,256]{2,1,0:T(8,128)S(1)}, u32[]{:S(2)}, u32[]{:S(2)}) collective-permute-start(f32[2,40,256]{2,1,0:T(8,128)S(1)} %get-tuple-element.52), channel_id=1, source_target_pairs={{0,1},{1,0},{2,3},{3,2},{4,5},{5,4},{6,7},{7,6},{8,9},{9,8},{10,11... | collective-permute-start | bytes 245768 | tf_op jit(solution)/shard_map/ppermute | solution.py:71
  115.8 2.0 %collective-permute-start.30 = (f32[2,40,256]{2,1,0:T(8,128)S(1)}, f32[2,40,256]{2,1,0:T(8,128)S(1)}, u32[]{:S(2)}, u32[]{:S(2)}) collective-permute-start(f32[2,40,256]{2,1,0:T(8,128)S(1)} %get-tuple-element.53), channel_id=1, source_target_pairs={{0,2},{1,3},{2,4},{3,5},{4,6},{5,7},{6,0},{7,1},{8,10},{9,11},{10,... | collective-permute-start | bytes 245768 | tf_op jit(solution)/shard_map/ppermute | solution.py:71
  117.9 2.6 %collective-permute-start.32 = (f32[2,40,256]{2,1,0:T(8,128)S(1)}, f32[2,40,256]{2,1,0:T(8,128)S(1)}, u32[]{:S(2)}, u32[]{:S(2)}) collective-permute-start(f32[2,40,256]{2,1,0:T(8,128)S(1)} %get-tuple-element.55), channel_id=1, source_target_pairs={{0,4},{1,5},{2,6},{3,7},{4,0},{5,1},{6,2},{7,3},{8,12},{9,13},{10,... | collective-permute-start | bytes 245768 | tf_op jit(solution)/shard_map/ppermute | solution.py:71
  120.4 0.9 collective-permute-start.33
  121.4 2.7 %collective-permute-start.34 = (f32[2,40,256]{2,1,0:T(8,128)S(1)}, f32[2,40,256]{2,1,0:T(8,128)S(1)}, u32[]{:S(2)}, u32[]{:S(2)}) collective-permute-start(f32[2,40,256]{2,1,0:T(8,128)S(1)} %get-tuple-element.57), channel_id=1, source_target_pairs={{0,6},{1,7},{2,0},{3,1},{4,2},{5,3},{6,4},{7,5},{8,14},{9,15},{10,... | collective-permute-start | bytes 245768 | tf_op jit(solution)/shard_map/ppermute | solution.py:71
  124.5 1.0 places.1.hot_ref
  125.5 0.9 collective-permute-done.32.refs_4_
  126.3 2.0 %collective-permute-done.33.refs_5_ = f32[2,40,256]{2,1,0:T(8,128)S(1)} collective-permute-done((f32[2,40,256]{2,1,0:T(8,128)S(1)}, f32[2,40,256]{2,1,0:T(8,128)S(1)}, u32[]{:S(2)}, u32[]{:S(2)}) %collective-permute-start.33) | collective-permute-done | bytes 81952 | tf_op jit(solution)/shard_map/ppermute | solution.py:71
  128.3 1.5 %collective-permute-done.35.refs_7_ = f32[2,40,256]{2,1,0:T(8,128)S(1)} collective-permute-done((f32[2,40,256]{2,1,0:T(8,128)S(1)}, f32[2,40,256]{2,1,0:T(8,128)S(1)}, u32[]{:S(2)}, u32[]{:S(2)}) %collective-permute-start.35) | collective-permute-done | bytes 81952 | tf_op jit(solution)/shard_map/ppermute | solution.py:71
  129.8 2.2 %final.1 = f32[256,512]{1,0:T(8,128)} custom-call(s32[3]{0:T(128)S(1)} %pad_add_fusion.where, bf16[2,256,320]{2,1,0:T(8,128)(2,1)S(1)} %places.1.hot_ref, f32[2,40,256]{2,1,0:T(8,128)S(1)} %get-tuple-element.51.refs_0_, f32[2,40,256]{2,1,0:T(8,128)S(1)} %collective-permute-done.29.refs_1_, f32[2,40,256]{2,1,0:T(8,128)S(1)} %collective-permute-done.30.refs_2_, ...), custom_call_target="tpu_custom_call" | custom-call | tf_op jit(solution)/shard_map/final/pallas_call | solution.py:380
  (67 shorter events, 6.5 us)
Async XLA Ops:
  0.0 69.4 %copy-start = (bf16[32,128,128]{2,1,0:T(8,128)(2,1)S(1)}, bf16[32,128,128]{2,1,0:T(8,128)(2,1)}, u32[]{:S(2)}) copy-start(bf16[32,128,128]{2,1,0:T(8,128)(2,1)} %refs_0_.1) | copy-start | bytes 3145732
  0.0 69.3 %copy-start.13 = (s32[4096,1]{0,1:T(1,128)S(1)}, s32[4096,1]{0,1:T(1,128)}, u32[]{:S(2)}) copy-start(s32[4096,1]{0,1:T(1,128)} %param.5) | copy-start | bytes 49156
  2.6 32.1 %collective-permute-start.18 = (bf16[2080,128]{1,0:T(8,128)(2,1)S(1)}, bf16[2080,128]{1,0:T(8,128)(2,1)S(1)}, u32[]{:S(2)}, u32[]{:S(2)}) collective-permute-start(bf16[2080,128]{1,0:T(8,128)(2,1)S(1)} %get-tuple-element.42), channel_id=1, source_target_pairs={{0,2},{1,3},{2,4},{3,5},{4,6},{5,7},{6,0},{7,1},{8,10},{9,11},{10,... | collective-permute-start | bytes 1597448 | tf_op jit(solution)/shard_map/ppermute | solution.py:71
  4.8 31.5 %collective-permute-start.16 = (bf16[2080,128]{1,0:T(8,128)(2,1)S(1)}, bf16[2080,128]{1,0:T(8,128)(2,1)S(1)}, u32[]{:S(2)}, u32[]{:S(2)}) collective-permute-start(bf16[2080,128]{1,0:T(8,128)(2,1)S(1)} %get-tuple-element.42), channel_id=1, source_target_pairs={{0,6},{1,7},{2,0},{3,1},{4,2},{5,3},{6,4},{7,5},{8,14},{9,15},{10,... | collective-permute-start | bytes 1597448 | tf_op jit(solution)/shard_map/ppermute | solution.py:71
  6.3 2.6 %collective-permute-start = (bf16[336,128]{1,0:T(8,128)(2,1)S(1)}, bf16[336,128]{1,0:T(8,128)(2,1)S(1)}, u32[]{:S(2)}, u32[]{:S(2)}) collective-permute-start(bf16[336,128]{1,0:T(8,128)(2,1)S(1)} %get-tuple-element.33), channel_id=1, source_target_pairs={{0,1},{1,0},{2,3},{3,2},{4,5},{5,4},{6,7},{7,6},{8,9},{9,8},{10,11... | collective-permute-start | bytes 258056 | tf_op jit(solution)/shard_map/ppermute | solution.py:71
  7.3 12.5 %collective-permute-start.1 = (bf16[336,128]{1,0:T(8,128)(2,1)S(1)}, bf16[336,128]{1,0:T(8,128)(2,1)S(1)}, u32[]{:S(2)}, u32[]{:S(2)}) collective-permute-start(bf16[336,128]{1,0:T(8,128)(2,1)S(1)} %get-tuple-element.34), channel_id=1, source_target_pairs={{0,2},{1,3},{2,4},{3,5},{4,6},{5,7},{6,0},{7,1},{8,10},{9,11},{10,... | collective-permute-start | bytes 258056 | tf_op jit(solution)/shard_map/ppermute | solution.py:71
  7.5 16.4 %collective-permute-start.2 = (bf16[336,128]{1,0:T(8,128)(2,1)S(1)}, bf16[336,128]{1,0:T(8,128)(2,1)S(1)}, u32[]{:S(2)}, u32[]{:S(2)}) collective-permute-start(bf16[336,128]{1,0:T(8,128)(2,1)S(1)} %get-tuple-element.35), channel_id=1, source_target_pairs={{0,3},{1,2},{2,5},{3,4},{4,7},{5,6},{6,1},{7,0},{8,11},{9,10},{10,... | collective-permute-start | bytes 258056 | tf_op jit(solution)/shard_map/ppermute | solution.py:71
  9.0 15.7 %collective-permute-start.3 = (bf16[336,128]{1,0:T(8,128)(2,1)S(1)}, bf16[336,128]{1,0:T(8,128)(2,1)S(1)}, u32[]{:S(2)}, u32[]{:S(2)}) collective-permute-start(bf16[336,128]{1,0:T(8,128)(2,1)S(1)} %get-tuple-element.36), channel_id=1, source_target_pairs={{0,4},{1,5},{2,6},{3,7},{4,0},{5,1},{6,2},{7,3},{8,12},{9,13},{10,... | collective-permute-start | bytes 258056 | tf_op jit(solution)/shard_map/ppermute | solution.py:71
  19.8 7.1 %collective-permute-start.4 = (bf16[336,128]{1,0:T(8,128)(2,1)S(1)}, bf16[336,128]{1,0:T(8,128)(2,1)S(1)}, u32[]{:S(2)}, u32[]{:S(2)}) collective-permute-start(bf16[336,128]{1,0:T(8,128)(2,1)S(1)} %get-tuple-element.37), channel_id=1, source_target_pairs={{0,5},{1,4},{2,7},{3,6},{4,1},{5,0},{6,3},{7,2},{8,13},{9,12},{10,... | collective-permute-start | bytes 258056 | tf_op jit(solution)/shard_map/ppermute | solution.py:71
  23.9 3.8 %collective-permute-start.5 = (bf16[336,128]{1,0:T(8,128)(2,1)S(1)}, bf16[336,128]{1,0:T(8,128)(2,1)S(1)}, u32[]{:S(2)}, u32[]{:S(2)}) collective-permute-start(bf16[336,128]{1,0:T(8,128)(2,1)S(1)} %get-tuple-element.38), channel_id=1, source_target_pairs={{0,6},{1,7},{2,0},{3,1},{4,2},{5,3},{6,4},{7,5},{8,14},{9,15},{10,... | collective-permute-start | bytes 258056 | tf_op jit(solution)/shard_map/ppermute | solution.py:71
  24.7 4.6 %collective-permute-start.6 = (bf16[336,128]{1,0:T(8,128)(2,1)S(1)}, bf16[336,128]{1,0:T(8,128)(2,1)S(1)}, u32[]{:S(2)}, u32[]{:S(2)}) collective-permute-start(bf16[336,128]{1,0:T(8,128)(2,1)S(1)} %get-tuple-element.39), channel_id=1, source_target_pairs={{0,7},{1,6},{2,1},{3,0},{4,3},{5,2},{6,5},{7,4},{8,15},{9,14},{10,... | collective-permute-start | bytes 258056 | tf_op jit(solution)/shard_map/ppermute | solution.py:71
  29.6 19.2 %collective-permute-start.9 = (bf16[40,8320]{1,0:T(8,128)(2,1)S(1)}, bf16[40,8320]{1,0:T(8,128)(2,1)}, u32[]{:S(2)}, u32[]{:S(2)}) collective-permute-start(bf16[40,8320]{1,0:T(8,128)(2,1)S(1)} %unit.1.refs_0_), channel_id=1, source_target_pairs={{0,104},{8,112},{16,120},{24,96},{32,8},{40,16},{48,24},{56,0},{64... | collective-permute-start | bytes 1996808 | tf_op jit(solution)/shard_map/ppermute | solution.py:63
  33.5 19.6 %collective-permute-start.7 = (bf16[40,8320]{1,0:T(8,128)(2,1)S(1)}, bf16[40,8320]{1,0:T(8,128)(2,1)}, u32[]{:S(2)}, u32[]{:S(2)}) collective-permute-start(bf16[40,8320]{1,0:T(8,128)(2,1)S(1)} %unit.1.refs_0_), channel_id=1, source_target_pairs={{0,32},{8,40},{16,48},{24,56},{32,64},{40,72},{48,80},{56,88},{64,... | collective-permute-start | bytes 1996808 | tf_op jit(solution)/shard_map/ppermute | solution.py:63
  33.5 20.4 %collective-permute-start.8 = (bf16[40,8320]{1,0:T(8,128)(2,1)S(1)}, bf16[40,8320]{1,0:T(8,128)(2,1)}, u32[]{:S(2)}, u32[]{:S(2)}) collective-permute-start(bf16[40,8320]{1,0:T(8,128)(2,1)S(1)} %unit.1.refs_0_), channel_id=1, source_target_pairs={{0,24},{8,0},{16,8},{24,16},{32,56},{40,32},{48,40},{56,48},{64,88... | collective-permute-start | bytes 1996808 | tf_op jit(solution)/shard_map/ppermute | solution.py:63
  34.8 20.5 %collective-permute-start.20 = (bf16[32,128,128]{2,1,0:T(8,128)(2,1)}, bf16[32,128,128]{2,1,0:T(8,128)(2,1)S(1)}, u32[]{:S(2)}, u32[]{:S(2)}) collective-permute-start(bf16[32,128,128]{2,1,0:T(8,128)(2,1)} %refs_0_.1), channel_id=1, source_target_pairs={{0,1},{1,0},{2,3},{3,2},{4,5},{5,4},{6,7},{7,6},{8,9},{9,8},{10,11... | collective-permute-start | bytes 3145736 | tf_op jit(solution)/shard_map/ppermute | solution.py:71
  36.3 15.1 %collective-permute-start.14 = (bf16[2080,128]{1,0:T(8,128)(2,1)S(1)}, bf16[2080,128]{1,0:T(8,128)(2,1)S(1)}, u32[]{:S(2)}, u32[]{:S(2)}) collective-permute-start(bf16[2080,128]{1,0:T(8,128)(2,1)S(1)} %get-tuple-element.42), channel_id=1, source_target_pairs={{0,4},{1,5},{2,6},{3,7},{4,0},{5,1},{6,2},{7,3},{8,12},{9,13},{10,... | collective-permute-start | bytes 1597448 | tf_op jit(solution)/shard_map/ppermute | solution.py:71
  48.8 16.5 %collective-permute-start.10 = (bf16[40,8320]{1,0:T(8,128)(2,1)}, bf16[40,8320]{1,0:T(8,128)(2,1)}, u32[]{:S(2)}, u32[]{:S(2)}) collective-permute-start(bf16[40,8320]{1,0:T(8,128)(2,1)} %collective-permute-done.9.refs_3_), channel_id=1, source_target_pairs={{0,8},{8,16},{16,24},{24,0},{32,40},{40,48},{48,56},{56,32},{64,72... | collective-permute-start | bytes 1996808 | tf_op jit(solution)/shard_map/ppermute | solution.py:63
  51.4 4.1 %collective-permute-start.19 = (bf16[2080,128]{1,0:T(8,128)(2,1)S(1)}, bf16[2080,128]{1,0:T(8,128)(2,1)S(1)}, u32[]{:S(2)}, u32[]{:S(2)}) collective-permute-start(bf16[2080,128]{1,0:T(8,128)(2,1)S(1)} %collective-permute-done.18.refs_0_), channel_id=1, source_target_pairs={{0,1},{1,0},{2,3},{3,2},{4,5},{5,4},{6,7},{7,6},{8,9},{9,8},{10,11... | collective-permute-start | bytes 1597448 | tf_op jit(solution)/shard_map/ppermute | solution.py:71
  53.1 6.2 %collective-permute-start.17 = (bf16[2080,128]{1,0:T(8,128)(2,1)S(1)}, bf16[2080,128]{1,0:T(8,128)(2,1)S(1)}, u32[]{:S(2)}, u32[]{:S(2)}) collective-permute-start(bf16[2080,128]{1,0:T(8,128)(2,1)S(1)} %collective-permute-done.16.refs_0_), channel_id=1, source_target_pairs={{0,1},{1,0},{2,3},{3,2},{4,5},{5,4},{6,7},{7,6},{8,9},{9,8},{10,11... | collective-permute-start | bytes 1597448 | tf_op jit(solution)/shard_map/ppermute | solution.py:71
  53.1 0.8 copy-start.3
  54.0 6.2 %collective-permute-start.15 = (bf16[2080,128]{1,0:T(8,128)(2,1)S(1)}, bf16[2080,128]{1,0:T(8,128)(2,1)S(1)}, u32[]{:S(2)}, u32[]{:S(2)}) collective-permute-start(bf16[2080,128]{1,0:T(8,128)(2,1)S(1)} %collective-permute-done.14.refs_0_), channel_id=1, source_target_pairs={{0,1},{1,0},{2,3},{3,2},{4,5},{5,4},{6,7},{7,6},{8,9},{9,8},{10,11... | collective-permute-start | bytes 1597448 | tf_op jit(solution)/shard_map/ppermute | solution.py:71
  55.3 34.1 %collective-permute-start.21 = (bf16[40,8320]{1,0:T(8,128)(2,1)}, bf16[40,8320]{1,0:T(8,128)(2,1)}, u32[]{:S(2)}, u32[]{:S(2)}) collective-permute-start(bf16[40,8320]{1,0:T(8,128)(2,1)} %collective-permute-done.7.refs_1_), channel_id=1, source_target_pairs={{0,8},{8,16},{16,24},{24,0},{32,40},{40,48},{48,56},{56,32},{64,72... | collective-permute-start | bytes 1996808 | tf_op jit(solution)/shard_map/ppermute | solution.py:63
  55.5 0.8 copy-start.7
  56.4 36.6 %collective-permute-start.11 = (bf16[40,8320]{1,0:T(8,128)(2,1)}, bf16[40,8320]{1,0:T(8,128)(2,1)}, u32[]{:S(2)}, u32[]{:S(2)}) collective-permute-start(bf16[40,8320]{1,0:T(8,128)(2,1)} %collective-permute-done.9.refs_3_), channel_id=1, source_target_pairs={{0,96},{8,104},{16,112},{24,120},{32,0},{40,8},{48,16},{56,24},{64... | collective-permute-start | bytes 1996808 | tf_op jit(solution)/shard_map/ppermute | solution.py:63
  59.3 0.9 copy-start.9
  60.2 32.8 %collective-permute-start.12 = (bf16[40,8320]{1,0:T(8,128)(2,1)}, bf16[40,8320]{1,0:T(8,128)(2,1)}, u32[]{:S(2)}, u32[]{:S(2)}) collective-permute-start(bf16[40,8320]{1,0:T(8,128)(2,1)} %collective-permute-done.7.refs_1_), channel_id=1, source_target_pairs={{0,32},{8,40},{16,48},{24,56},{32,64},{40,72},{48,80},{56,88},{64,... | collective-permute-start | bytes 1996808 | tf_op jit(solution)/shard_map/ppermute | solution.py:63
  60.2 0.8 copy-start.11
  61.0 32.0 %collective-permute-start.13 = (bf16[40,8320]{1,0:T(8,128)(2,1)}, bf16[40,8320]{1,0:T(8,128)(2,1)}, u32[]{:S(2)}, u32[]{:S(2)}) collective-permute-start(bf16[40,8320]{1,0:T(8,128)(2,1)} %collective-permute-done.8.refs_2_), channel_id=1, source_target_pairs={{0,24},{8,0},{16,8},{24,16},{32,56},{40,32},{48,40},{56,48},{64,88... | collective-permute-start | bytes 1996808 | tf_op jit(solution)/shard_map/ppermute | solution.py:63
  65.3 35.9 %collective-permute-start.22 = (bf16[40,8320]{1,0:T(8,128)(2,1)}, bf16[40,8320]{1,0:T(8,128)(2,1)S(1)}, u32[]{:S(2)}, u32[]{:S(2)}) collective-permute-start(bf16[40,8320]{1,0:T(8,128)(2,1)} %collective-permute-done.10.refs_4_), channel_id=1, source_target_pairs={{0,96},{8,104},{16,112},{24,120},{32,0},{40,8},{48,16},{56,24},{64... | collective-permute-start | bytes 1996808 | tf_op jit(solution)/shard_map/ppermute | solution.py:63
  69.4 3.3 %copy-start.2 = (bf16[2080,128]{1,0:T(8,128)(2,1)S(1)}, bf16[2080,128]{1,0:T(8,128)(2,1)}, u32[]{:S(2)}) copy-start(bf16[2080,128]{1,0:T(8,128)(2,1)} %copy-done.1) | copy-start | bytes 1597444
  69.4 3.3 %copy-start.8 = (bf16[2080,128]{1,0:T(8,128)(2,1)S(1)}, bf16[2080,128]{1,0:T(8,128)(2,1)}, u32[]{:S(2)}) copy-start(bf16[2080,128]{1,0:T(8,128)(2,1)} %copy-done.7) | copy-start | bytes 1597444
  72.7 5.5 %copy-start.4 = (bf16[2080,128]{1,0:T(8,128)(2,1)S(1)}, bf16[2080,128]{1,0:T(8,128)(2,1)}, u32[]{:S(2)}) copy-start(bf16[2080,128]{1,0:T(8,128)(2,1)} %copy-done.3) | copy-start | bytes 1597444
  72.7 5.5 %copy-start.10 = (bf16[2080,128]{1,0:T(8,128)(2,1)S(1)}, bf16[2080,128]{1,0:T(8,128)(2,1)}, u32[]{:S(2)}) copy-start(bf16[2080,128]{1,0:T(8,128)(2,1)} %copy-done.9) | copy-start | bytes 1597444
  78.2 5.5 %copy-start.6 = (bf16[2080,128]{1,0:T(8,128)(2,1)S(1)}, bf16[2080,128]{1,0:T(8,128)(2,1)}, u32[]{:S(2)}) copy-start(bf16[2080,128]{1,0:T(8,128)(2,1)} %copy-done.5) | copy-start | bytes 1597444
  78.2 5.5 %copy-start.12 = (bf16[2080,128]{1,0:T(8,128)(2,1)S(1)}, bf16[2080,128]{1,0:T(8,128)(2,1)}, u32[]{:S(2)}) copy-start(bf16[2080,128]{1,0:T(8,128)(2,1)} %copy-done.11) | copy-start | bytes 1597444
  91.9 9.0 %collective-permute-start.28 = (f32[40,256]{1,0:T(8,128)S(1)}, f32[40,256]{1,0:T(8,128)S(1)}, u32[]{:S(2)}, u32[]{:S(2)}) collective-permute-start(f32[40,256]{1,0:T(8,128)S(1)} %contract.4.refs_8_), channel_id=1, source_target_pairs={{0,120},{8,96},{16,104},{24,112},{32,24},{40,0},{48,8},{56,16},{64... | collective-permute-start | bytes 122888 | tf_op jit(solution)/shard_map/ppermute | solution.py:63
  96.9 9.7 %collective-permute-start.23 = (f32[40,256]{1,0:T(8,128)S(1)}, f32[40,256]{1,0:T(8,128)S(1)}, u32[]{:S(2)}, u32[]{:S(2)}) collective-permute-start(f32[40,256]{1,0:T(8,128)S(1)} %get-tuple-element.44.refs_1_), channel_id=1, source_target_pairs={{0,96},{8,104},{16,112},{24,120},{32,0},{40,8},{48,16},{56,24},{64... | collective-permute-start | bytes 122888 | tf_op jit(solution)/shard_map/ppermute | solution.py:63
  97.0 9.7 %collective-permute-start.24 = (f32[40,256]{1,0:T(8,128)S(1)}, f32[40,256]{1,0:T(8,128)S(1)}, u32[]{:S(2)}, u32[]{:S(2)}) collective-permute-start(f32[40,256]{1,0:T(8,128)S(1)} %get-tuple-element.45.refs_2_), channel_id=1, source_target_pairs={{0,8},{8,16},{16,24},{24,0},{32,40},{40,48},{48,56},{56,32},{64,72... | collective-permute-start | bytes 122888 | tf_op jit(solution)/shard_map/ppermute | solution.py:63
  98.4 8.3 %collective-permute-start.25 = (f32[40,256]{1,0:T(8,128)S(1)}, f32[40,256]{1,0:T(8,128)S(1)}, u32[]{:S(2)}, u32[]{:S(2)}) collective-permute-start(f32[40,256]{1,0:T(8,128)S(1)} %get-tuple-element.46.refs_3_), channel_id=1, source_target_pairs={{0,56},{8,32},{16,40},{24,48},{32,88},{40,64},{48,72},{56,80},{64,... | collective-permute-start | bytes 122888 | tf_op jit(solution)/shard_map/ppermute | solution.py:63
  100.9 6.9 %collective-permute-start.26 = (f32[40,256]{1,0:T(8,128)S(1)}, f32[40,256]{1,0:T(8,128)S(1)}, u32[]{:S(2)}, u32[]{:S(2)}) collective-permute-start(f32[40,256]{1,0:T(8,128)S(1)} %get-tuple-element.47.refs_4_), channel_id=1, source_target_pairs={{0,48},{8,56},{16,32},{24,40},{32,80},{40,88},{48,64},{56,72},{64,... | collective-permute-start | bytes 122888 | tf_op jit(solution)/shard_map/ppermute | solution.py:63
  101.3 6.5 %collective-permute-start.27 = (f32[40,256]{1,0:T(8,128)S(1)}, f32[40,256]{1,0:T(8,128)S(1)}, u32[]{:S(2)}, u32[]{:S(2)}) collective-permute-start(f32[40,256]{1,0:T(8,128)S(1)} %get-tuple-element.48.refs_5_), channel_id=1, source_target_pairs={{0,88},{8,64},{16,72},{24,80},{32,120},{40,96},{48,104},{56,112},{... | collective-permute-start | bytes 122888 | tf_op jit(solution)/shard_map/ppermute | solution.py:63
  108.5 12.9 %collective-permute-start.29 = (f32[2,40,256]{2,1,0:T(8,128)S(1)}, f32[2,40,256]{2,1,0:T(8,128)S(1)}, u32[]{:S(2)}, u32[]{:S(2)}) collective-permute-start(f32[2,40,256]{2,1,0:T(8,128)S(1)} %get-tuple-element.52), channel_id=1, source_target_pairs={{0,1},{1,0},{2,3},{3,2},{4,5},{5,4},{6,7},{7,6},{8,9},{9,8},{10,11... | collective-permute-start | bytes 245768 | tf_op jit(solution)/shard_map/ppermute | solution.py:71
  115.8 8.2 %collective-permute-start.30 = (f32[2,40,256]{2,1,0:T(8,128)S(1)}, f32[2,40,256]{2,1,0:T(8,128)S(1)}, u32[]{:S(2)}, u32[]{:S(2)}) collective-permute-start(f32[2,40,256]{2,1,0:T(8,128)S(1)} %get-tuple-element.53), channel_id=1, source_target_pairs={{0,2},{1,3},{2,4},{3,5},{4,6},{5,7},{6,0},{7,1},{8,10},{9,11},{10,... | collective-permute-start | bytes 245768 | tf_op jit(solution)/shard_map/ppermute | solution.py:71
  117.8 7.6 %collective-permute-start.31 = (f32[2,40,256]{2,1,0:T(8,128)S(1)}, f32[2,40,256]{2,1,0:T(8,128)S(1)}, u32[]{:S(2)}, u32[]{:S(2)}) collective-permute-start(f32[2,40,256]{2,1,0:T(8,128)S(1)} %get-tuple-element.54), channel_id=1, source_target_pairs={{0,3},{1,2},{2,5},{3,4},{4,7},{5,6},{6,1},{7,0},{8,11},{9,10},{10,... | collective-permute-start | bytes 245768 | tf_op jit(solution)/shard_map/ppermute | solution.py:71
  117.9 8.5 %collective-permute-start.32 = (f32[2,40,256]{2,1,0:T(8,128)S(1)}, f32[2,40,256]{2,1,0:T(8,128)S(1)}, u32[]{:S(2)}, u32[]{:S(2)}) collective-permute-start(f32[2,40,256]{2,1,0:T(8,128)S(1)} %get-tuple-element.55), channel_id=1, source_target_pairs={{0,4},{1,5},{2,6},{3,7},{4,0},{5,1},{6,2},{7,3},{8,12},{9,13},{10,... | collective-permute-start | bytes 245768 | tf_op jit(solution)/shard_map/ppermute | solution.py:71
  120.4 7.9 %collective-permute-start.33 = (f32[2,40,256]{2,1,0:T(8,128)S(1)}, f32[2,40,256]{2,1,0:T(8,128)S(1)}, u32[]{:S(2)}, u32[]{:S(2)}) collective-permute-start(f32[2,40,256]{2,1,0:T(8,128)S(1)} %get-tuple-element.56), channel_id=1, source_target_pairs={{0,5},{1,4},{2,7},{3,6},{4,1},{5,0},{6,3},{7,2},{8,13},{9,12},{10,... | collective-permute-start | bytes 245768 | tf_op jit(solution)/shard_map/ppermute | solution.py:71
  121.4 7.0 %collective-permute-start.34 = (f32[2,40,256]{2,1,0:T(8,128)S(1)}, f32[2,40,256]{2,1,0:T(8,128)S(1)}, u32[]{:S(2)}, u32[]{:S(2)}) collective-permute-start(f32[2,40,256]{2,1,0:T(8,128)S(1)} %get-tuple-element.57), channel_id=1, source_target_pairs={{0,6},{1,7},{2,0},{3,1},{4,2},{5,3},{6,4},{7,5},{8,14},{9,15},{10,... | collective-permute-start | bytes 245768 | tf_op jit(solution)/shard_map/ppermute | solution.py:71
  124.0 5.8 %collective-permute-start.35 = (f32[2,40,256]{2,1,0:T(8,128)S(1)}, f32[2,40,256]{2,1,0:T(8,128)S(1)}, u32[]{:S(2)}, u32[]{:S(2)}) collective-permute-start(f32[2,40,256]{2,1,0:T(8,128)S(1)} %get-tuple-element.58), channel_id=1, source_target_pairs={{0,7},{1,6},{2,1},{3,0},{4,3},{5,2},{6,5},{7,4},{8,15},{9,14},{10,... | collective-permute-start | bytes 245768 | tf_op jit(solution)/shard_map/ppermute | solution.py:71
  (2 other events, 1.6 us)

commit v5 on v4

--- a/solution.py
+++ b/solution.py
@@ -42,8 +42,8 @@
 FIRST = (((1, 0), (0, 0)), ((0, 3), (0, 0)), ((3, 1), (0, 0)))
 SECOND = (((3, 2), (3, 1)), ((2, 1), (3, 1)), ((2, 0), (1, 0)), ((0, 2), (0, 3)))
 THIRD = (((1, 1), (1, 0)), ((2, 2), (3, 2)))
-EARLY = ((0, 0),) + tuple(d for d, _ in FIRST + SECOND)
-MIDDLE = ((1, 1),)
+EARLY = ((0, 0), (1, 0), (0, 3), (3, 1), (3, 2), (2, 1))
+MIDDLE = ((2, 0), (0, 2), (1, 1))
 LATE = ((2, 2),)
 FORMED = EARLY + MIDDLE + LATE
 
@@ -430,7 +430,7 @@
     for part in (EARLY, MIDDLE, LATE):
         values = contract_call([units[d] for d in part], total)
         known.update(zip(part, values))
-    for d in EARLY + MIDDLE:
+    for d in EARLY + MIDDLE[2:]:
         if negated(d) in TURNED:
             known[negated(d)] = plane_shift(known[d], negated(d))
     ordered = gather_call(where, known)

time: 133 us -> 132 us (level)
    ppermute x21, waiting for transfers between devices: 19.8 us -> 17.3 us  [line_shift(): return lax.ppermute(x, LINE, pairs)]
    ppermute x15, waiting for transfers between devices: 13.7 us -> 15.2 us  [plane_shift(): return lax.ppermute(x, PLANE, pairs)]
    ppermute x21, starting transfers between devices: 34.7 us -> 36.1 us  [line_shift(): return lax.ppermute(x, LINE, pairs)]
  transfers between devices with their start and end apart: 36 -> 36, of which waited for: 11 -> 10; matrix products, arithmetic and copies ran while one was open for 0% -> 0% of each run, Pallas kernels for 23% -> 23%
where the time goes in v5:
time: 132 us
  starting transfers between devices  57.9 us (44%)
  Pallas kernels  36.3 us (27%)
  waiting for transfers between devices  32.5 us (25%)
  local copies, waits for them, and re-layouts  4.98 us (4%)
    ppermute x21, starting transfers between devices, line_shift(): return lax.ppermute(x, LINE, pairs)  36.1 us
    ppermute x15, starting transfers between devices, plane_shift(): return lax.ppermute(x, PLANE, pairs)  21.7 us
    pallas_call x4, Pallas kernels, reduce_call(): pl.pallas_call(functools.partial(reduce_kernel, plan, total is not None),...  19.9 us
    ppermute x21, waiting for transfers between devices, line_shift(): return lax.ppermute(x, LINE, pairs)  17.3 us
    ppermute x15, waiting for transfers between devices, plane_shift(): return lax.ppermute(x, PLANE, pairs)  15.2 us
    pallas_call x3, Pallas kernels, contract_call(): pl.pallas_call(functools.partial(contract_kernel, n), out_shape=[made(UNI...  7.55 us
    unnamed x28, local copies, waits for them, and re-layouts  4.97 us
  transfers between devices with their start and end apart: 36, of which 10 were waited for; matrix products, arithmetic and copies ran while one was open for 0% of the time, Pallas kernels for 23%

profile of v5, /device:TPU:1, one launch (start us, length us, event | category | flops | bytes accessed | tf_op | source)
XLA Modules:
  0.0 132.2 jit_solution(5356549988368680627)
XLA Ops:
  0.1 2.5 %fold.1 = (bf16[336,128]{1,0:T(8,128)(2,1)S(1)}, bf16[336,128]{1,0:T(8,128)(2,1)S(1)}, bf16[336,128]{1,0:T(8,128)(2,1)S(1)}, bf16[336,128]{1,0:T(8,128)(2,1)S(1)...) custom-call(s32[3]{0:T(128)S(1)} %pad_add_fusion.where, ...), custom_call_target="tpu_custom_call" | custom-call | tf_op jit(solution)/shard_map/fold/pallas_call | solution.py:134
  2.6 2.2 %collective-permute-start.16 = (bf16[2080,128]{1,0:T(8,128)(2,1)S(1)}, bf16[2080,128]{1,0:T(8,128)(2,1)S(1)}, u32[]{:S(2)}, u32[]{:S(2)}) collective-permute-start(bf16[2080,128]{1,0:T(8,128)(2,1)S(1)} %get-tuple-element.43), channel_id=1, source_target_pairs={{0,2},{1,3},{2,4},{3,5},{4,6},{5,7},{6,0},{7,1},{8,10},{9,11},{10,... | collective-permute-start | bytes 1597448 | tf_op jit(solution)/shard_map/ppermute | solution.py:71
  4.8 1.5 %collective-permute-start.14 = (bf16[2080,128]{1,0:T(8,128)(2,1)S(1)}, bf16[2080,128]{1,0:T(8,128)(2,1)S(1)}, u32[]{:S(2)}, u32[]{:S(2)}) collective-permute-start(bf16[2080,128]{1,0:T(8,128)(2,1)S(1)} %get-tuple-element.43), channel_id=1, source_target_pairs={{0,6},{1,7},{2,0},{3,1},{4,2},{5,3},{6,4},{7,5},{8,14},{9,15},{10,... | collective-permute-start | bytes 1597448 | tf_op jit(solution)/shard_map/ppermute | solution.py:71
  6.3 1.0 collective-permute-start
  7.5 1.5 %collective-permute-start.2 = (bf16[336,128]{1,0:T(8,128)(2,1)S(1)}, bf16[336,128]{1,0:T(8,128)(2,1)S(1)}, u32[]{:S(2)}, u32[]{:S(2)}) collective-permute-start(bf16[336,128]{1,0:T(8,128)(2,1)S(1)} %get-tuple-element.36), channel_id=1, source_target_pairs={{0,3},{1,2},{2,5},{3,4},{4,7},{5,6},{6,1},{7,0},{8,11},{9,10},{10,... | collective-permute-start | bytes 258056 | tf_op jit(solution)/shard_map/ppermute | solution.py:71
  9.0 2.4 %collective-permute-start.3 = (bf16[336,128]{1,0:T(8,128)(2,1)S(1)}, bf16[336,128]{1,0:T(8,128)(2,1)S(1)}, u32[]{:S(2)}, u32[]{:S(2)}) collective-permute-start(bf16[336,128]{1,0:T(8,128)(2,1)S(1)} %get-tuple-element.37), channel_id=1, source_target_pairs={{0,4},{1,5},{2,6},{3,7},{4,0},{5,1},{6,2},{7,3},{8,12},{9,13},{10,... | collective-permute-start | bytes 258056 | tf_op jit(solution)/shard_map/ppermute | solution.py:71
  11.3 8.4 %collective-permute-done.1.refs_2_ = bf16[336,128]{1,0:T(8,128)(2,1)S(1)} collective-permute-done((bf16[336,128]{1,0:T(8,128)(2,1)S(1)}, bf16[336,128]{1,0:T(8,128)(2,1)S(1)}, u32[]{:S(2)}, u32[]{:S(2)}) %collective-permute-start.1) | collective-permute-done | bytes 86048 | tf_op jit(solution)/shard_map/ppermute | solution.py:71
  19.8 4.1 %collective-permute-start.4 = (bf16[336,128]{1,0:T(8,128)(2,1)S(1)}, bf16[336,128]{1,0:T(8,128)(2,1)S(1)}, u32[]{:S(2)}, u32[]{:S(2)}) collective-permute-start(bf16[336,128]{1,0:T(8,128)(2,1)S(1)} %get-tuple-element.38), channel_id=1, source_target_pairs={{0,5},{1,4},{2,7},{3,6},{4,1},{5,0},{6,3},{7,2},{8,13},{9,12},{10,... | collective-permute-start | bytes 258056 | tf_op jit(solution)/shard_map/ppermute | solution.py:71
  24.8 2.1 %collective-permute-done.4.refs_5_ = bf16[336,128]{1,0:T(8,128)(2,1)S(1)} collective-permute-done((bf16[336,128]{1,0:T(8,128)(2,1)S(1)}, bf16[336,128]{1,0:T(8,128)(2,1)S(1)}, u32[]{:S(2)}, u32[]{:S(2)}) %collective-permute-start.4) | collective-permute-done | bytes 86048 | tf_op jit(solution)/shard_map/ppermute | solution.py:71
  26.9 0.8 collective-permute-done.5.refs_6_
  27.8 1.5 %collective-permute-done.6.refs_7_ = bf16[336,128]{1,0:T(8,128)(2,1)S(1)} collective-permute-done((bf16[336,128]{1,0:T(8,128)(2,1)S(1)}, bf16[336,128]{1,0:T(8,128)(2,1)S(1)}, u32[]{:S(2)}, u32[]{:S(2)}) %collective-permute-start.6) | collective-permute-done | bytes 86048 | tf_op jit(solution)/shard_map/ppermute | solution.py:71
  29.6 3.9 %collective-permute-start.9 = (bf16[40,8320]{1,0:T(8,128)(2,1)S(1)}, bf16[40,8320]{1,0:T(8,128)(2,1)}, u32[]{:S(2)}, u32[]{:S(2)}) collective-permute-start(bf16[40,8320]{1,0:T(8,128)(2,1)S(1)} %unit.1.refs_0_), channel_id=1, source_target_pairs={{0,104},{8,112},{16,120},{24,96},{32,8},{40,16},{48,24},{56,0},{64... | collective-permute-start | bytes 1996808 | tf_op jit(solution)/shard_map/ppermute | solution.py:63
  33.5 1.2 collective-permute-start.8
  34.8 2.0 %collective-permute-start.12 = (bf16[2080,128]{1,0:T(8,128)(2,1)S(1)}, bf16[2080,128]{1,0:T(8,128)(2,1)S(1)}, u32[]{:S(2)}, u32[]{:S(2)}) collective-permute-start(bf16[2080,128]{1,0:T(8,128)(2,1)S(1)} %get-tuple-element.43), channel_id=1, source_target_pairs={{0,4},{1,5},{2,6},{3,7},{4,0},{5,1},{6,2},{7,3},{8,12},{9,13},{10,... | collective-permute-start | bytes 1597448 | tf_op jit(solution)/shard_map/ppermute | solution.py:71
  36.7 1.9 %collective-permute-start.18 = (bf16[32,128,128]{2,1,0:T(8,128)(2,1)}, bf16[32,128,128]{2,1,0:T(8,128)(2,1)S(1)}, u32[]{:S(2)}, u32[]{:S(2)}) collective-permute-start(bf16[32,128,128]{2,1,0:T(8,128)(2,1)} %refs_0_.1), channel_id=1, source_target_pairs={{0,1},{1,0},{2,3},{3,2},{4,5},{5,4},{6,7},{7,6},{8,9},{9,8},{10,11... | collective-permute-start | bytes 3145736 | tf_op jit(solution)/shard_map/ppermute | solution.py:71
  38.6 10.2 %collective-permute-done.9.refs_3_ = bf16[40,8320]{1,0:T(8,128)(2,1)} collective-permute-done((bf16[40,8320]{1,0:T(8,128)(2,1)S(1)}, bf16[40,8320]{1,0:T(8,128)(2,1)}, u32[]{:S(2)}, u32[]{:S(2)}) %collective-permute-start.9) | collective-permute-done | bytes 665632 | tf_op jit(solution)/shard_map/ppermute | solution.py:63
  48.8 1.9 %collective-permute-start.17 = (bf16[2080,128]{1,0:T(8,128)(2,1)S(1)}, bf16[2080,128]{1,0:T(8,128)(2,1)S(1)}, u32[]{:S(2)}, u32[]{:S(2)}) collective-permute-start(bf16[2080,128]{1,0:T(8,128)(2,1)S(1)} %collective-permute-done.16.refs_0_), channel_id=1, source_target_pairs={{0,1},{1,0},{2,3},{3,2},{4,5},{5,4},{6,7},{7,6},{8,9},{9,8},{10,11... | collective-permute-start | bytes 1597448 | tf_op jit(solution)/shard_map/ppermute | solution.py:71
  53.9 1.1 collective-permute-start.19
  54.9 0.8 copy-done.7
  55.8 2.6 %collective-permute-start.20 = (bf16[40,8320]{1,0:T(8,128)(2,1)}, bf16[40,8320]{1,0:T(8,128)(2,1)}, u32[]{:S(2)}, u32[]{:S(2)}) collective-permute-start(bf16[40,8320]{1,0:T(8,128)(2,1)} %collective-permute-done.8.refs_2_), channel_id=1, source_target_pairs={{0,24},{8,0},{16,8},{24,16},{32,56},{40,32},{48,40},{56,48},{64,88... | collective-permute-start | bytes 1996808 | tf_op jit(solution)/shard_map/ppermute | solution.py:63
  58.4 0.8 copy-done.9
  59.2 0.8 copy-done.11
  60.1 1.5 %collective-permute-start.11 = (bf16[40,8320]{1,0:T(8,128)(2,1)}, bf16[40,8320]{1,0:T(8,128)(2,1)}, u32[]{:S(2)}, u32[]{:S(2)}) collective-permute-start(bf16[40,8320]{1,0:T(8,128)(2,1)} %collective-permute-done.9.refs_3_), channel_id=1, source_target_pairs={{0,96},{8,104},{16,112},{24,120},{32,0},{40,8},{48,16},{56,24},{64... | collective-permute-start | bytes 1996808 | tf_op jit(solution)/shard_map/ppermute | solution.py:63
  61.5 3.8 %collective-permute-done.10.refs_4_ = bf16[40,8320]{1,0:T(8,128)(2,1)} collective-permute-done((bf16[40,8320]{1,0:T(8,128)(2,1)}, bf16[40,8320]{1,0:T(8,128)(2,1)}, u32[]{:S(2)}, u32[]{:S(2)}) %collective-permute-start.10) | collective-permute-done | bytes 665632 | tf_op jit(solution)/shard_map/ppermute | solution.py:63
  65.3 2.0 %collective-permute-start.22 = (bf16[40,8320]{1,0:T(8,128)(2,1)}, bf16[40,8320]{1,0:T(8,128)(2,1)S(1)}, u32[]{:S(2)}, u32[]{:S(2)}) collective-permute-start(bf16[40,8320]{1,0:T(8,128)(2,1)} %collective-permute-done.10.refs_4_), channel_id=1, source_target_pairs={{0,96},{8,104},{16,112},{24,120},{32,0},{40,8},{48,16},{56,24},{64... | collective-permute-start | bytes 1996808 | tf_op jit(solution)/shard_map/ppermute | solution.py:63
  67.3 2.0 %prepare.1 = (bf16[8,128,256]{2,1,0:T(8,128)(2,1)S(1)}, bf16[8,128,256]{2,1,0:T(8,128)(2,1)S(1)}) custom-call(s32[3]{0:T(128)S(1)} %pad_add_fusion.where, bf16[1024,1024]{1,0:T(8,128)(2,1)} %primal.1, bf16[1024,1024]{1,0:T(8,128)(2,1)} %dual.1), custom_call_target="tpu_custom_call" | custom-call | tf_op jit(solution)/shard_map/prepare/pallas_call | solution.py:193
  69.4 3.2 %reduced.4.refs_2_ = bf16[256,8320]{1,0:T(8,128)(2,1)S(1)} custom-call(s32[3]{0:T(128)S(1)} %pad_add_fusion.where, s32[256]{0:T(256)S(1)} %bitcast.8, bf16[8,128,256]{2,1,0:T(8,128)(2,1)S(1)} %get-tuple-element.41.right, bf16[8,128,256]{2,1,0:T(8,128)(2,1)S(1)} %get-tuple-element.42.left, bf16[32,128,128]{2,1,0:T(8,128)(2,1)S(1)} %copy-done, ...), custom_call_target="tpu_custom_call" | custom-call | tf_op jit(solution)/shard_map/reduced/pallas_call | solution.py:247
  72.7 5.5 %reduced.5.refs_2_ = bf16[256,8320]{1,0:T(8,128)(2,1)S(1)} custom-call(s32[3]{0:T(128)S(1)} %pad_add_fusion.where, s32[256]{0:T(256)S(1)} %bitcast.9, bf16[8,128,256]{2,1,0:T(8,128)(2,1)S(1)} %get-tuple-element.41.right, bf16[8,128,256]{2,1,0:T(8,128)(2,1)S(1)} %get-tuple-element.42.left, ...), custom_call_target="tpu_custom_call", output_to_operand_aliasing={{}: (6, {})} | custom-call | tf_op jit(solution)/shard_map/reduced/pallas_call | solution.py:247
  78.2 5.5 %reduced.6.refs_2_ = bf16[256,8320]{1,0:T(8,128)(2,1)S(1)} custom-call(s32[3]{0:T(128)S(1)} %pad_add_fusion.where, s32[256]{0:T(256)S(1)} %bitcast.10, bf16[8,128,256]{2,1,0:T(8,128)(2,1)S(1)} %get-tuple-element.41.right, bf16[8,128,256]{2,1,0:T(8,128)(2,1)S(1)} %get-tuple-element.42.left, ...), custom_call_target="tpu_custom_call", output_to_operand_aliasing={{}: (6, {})} | custom-call | tf_op jit(solution)/shard_map/reduced/pallas_call | solution.py:247
  83.7 5.7 %reduced.7.refs_6_.refs_3_.refs_1_ = bf16[256,8320]{1,0:T(8,128)(2,1)S(1)} custom-call(s32[3]{0:T(128)S(1)} %pad_add_fusion.where, s32[256]{0:T(256)S(1)} %bitcast.11, bf16[8,128,256]{2,1,0:T(8,128)(2,1)S(1)} %get-tuple-element.41.right, bf16[8,128,256]{2,1,0:T(8,128)(2,1)S(1)} %get-tuple-element.42.left, ...), custom_call_target="tpu_custom_call", output_to_operand_aliasing={{}: (6, {})} | custom-call | tf_op jit(solution)/shard_map/reduced/pallas_call | solution.py:247
  89.4 3.0 %contract.4 = (f32[40,256]{1,0:T(8,128)S(1)}, f32[40,256]{1,0:T(8,128)S(1)}, f32[40,256]{1,0:T(8,128)S(1)}) custom-call(bf16[40,8320]{1,0:T(8,128)(2,1)} %collective-permute-done.19.refs_0_, bf16[40,8320]{1,0:T(8,128)(2,1)} %collective-permute-done.20.refs_1_, bf16[40,8320]{1,0:T(8,128)(2,1)} %collective-permute-done.21.refs_2_, ...), custom_call_target="tpu_custom_call" | custom-call | tf_op jit(solution)/shard_map/contract/pallas_call | solution.py:272
  92.5 1.1 collective-permute-start.28
  93.6 3.2 %contract.3 = (f32[40,256]{1,0:T(8,128)S(1)}, f32[40,256]{1,0:T(8,128)S(1)}, f32[40,256]{1,0:T(8,128)S(1)}, f32[40,256]{1,0:T(8,128)S(1)}, f32[40,256]{1,0:T(8,128)S(1)}, /*index=5*/f32[40,256]{1,0:T(8,128)S(1)}) custom-call(bf16[40,8320]{1,0:T(8,128)(2,1)S(1)} %unit.1.refs_0_, bf16[40,8320]{1,0:T(8,128)(2,1)} %collective-permute-done.7.refs_1_, ...), custom_call_target="tpu_custom_call" | custom-call | tf_op jit(solution)/shard_map/contract/pallas_call | solution.py:272
  96.9 1.4 %collective-permute-start.24 = (f32[40,256]{1,0:T(8,128)S(1)}, f32[40,256]{1,0:T(8,128)S(1)}, u32[]{:S(2)}, u32[]{:S(2)}) collective-permute-start(f32[40,256]{1,0:T(8,128)S(1)} %get-tuple-element.46.refs_2_), channel_id=1, source_target_pairs={{0,8},{8,16},{16,24},{24,0},{32,40},{40,48},{48,56},{56,32},{64,72... | collective-permute-start | bytes 122888 | tf_op jit(solution)/shard_map/ppermute | solution.py:63
  98.3 2.5 %collective-permute-start.25 = (f32[40,256]{1,0:T(8,128)S(1)}, f32[40,256]{1,0:T(8,128)S(1)}, u32[]{:S(2)}, u32[]{:S(2)}) collective-permute-start(f32[40,256]{1,0:T(8,128)S(1)} %get-tuple-element.47.refs_3_), channel_id=1, source_target_pairs={{0,56},{8,32},{16,40},{24,48},{32,88},{40,64},{48,72},{56,80},{64,... | collective-permute-start | bytes 122888 | tf_op jit(solution)/shard_map/ppermute | solution.py:63
  101.2 4.0 %collective-permute-start.27 = (f32[40,256]{1,0:T(8,128)S(1)}, f32[40,256]{1,0:T(8,128)S(1)}, u32[]{:S(2)}, u32[]{:S(2)}) collective-permute-start(f32[40,256]{1,0:T(8,128)S(1)} %get-tuple-element.49.refs_5_), channel_id=1, source_target_pairs={{0,88},{8,64},{16,72},{24,80},{32,120},{40,96},{48,104},{56,112},{... | collective-permute-start | bytes 122888 | tf_op jit(solution)/shard_map/ppermute | solution.py:63
  105.2 1.3 %contract.5.refs_9_ = f32[40,256]{1,0:T(8,128)S(1)} custom-call(bf16[40,8320]{1,0:T(8,128)(2,1)S(1)} %collective-permute-done.22.refs_0_, bf16[256,8320]{1,0:T(8,128)(2,1)S(1)} %reduced.7.refs_6_.refs_3_.refs_1_), custom_call_target="tpu_custom_call" | custom-call | tf_op jit(solution)/shard_map/contract/pallas_call | solution.py:272
  106.5 1.2 collective-permute-done.26.refs_13_
  108.4 7.4 %collective-permute-start.29 = (f32[2,40,256]{2,1,0:T(8,128)S(1)}, f32[2,40,256]{2,1,0:T(8,128)S(1)}, u32[]{:S(2)}, u32[]{:S(2)}) collective-permute-start(f32[2,40,256]{2,1,0:T(8,128)S(1)} %get-tuple-element.54), channel_id=1, source_target_pairs={{0,1},{1,0},{2,3},{3,2},{4,5},{5,4},{6,7},{7,6},{8,9},{9,8},{10,11... | collective-permute-start | bytes 245768 | tf_op jit(solution)/shard_map/ppermute | solution.py:71
  115.8 2.0 %collective-permute-start.30 = (f32[2,40,256]{2,1,0:T(8,128)S(1)}, f32[2,40,256]{2,1,0:T(8,128)S(1)}, u32[]{:S(2)}, u32[]{:S(2)}) collective-permute-start(f32[2,40,256]{2,1,0:T(8,128)S(1)} %get-tuple-element.55), channel_id=1, source_target_pairs={{0,2},{1,3},{2,4},{3,5},{4,6},{5,7},{6,0},{7,1},{8,10},{9,11},{10,... | collective-permute-start | bytes 245768 | tf_op jit(solution)/shard_map/ppermute | solution.py:71
  117.8 2.6 %collective-permute-start.32 = (f32[2,40,256]{2,1,0:T(8,128)S(1)}, f32[2,40,256]{2,1,0:T(8,128)S(1)}, u32[]{:S(2)}, u32[]{:S(2)}) collective-permute-start(f32[2,40,256]{2,1,0:T(8,128)S(1)} %get-tuple-element.57), channel_id=1, source_target_pairs={{0,4},{1,5},{2,6},{3,7},{4,0},{5,1},{6,2},{7,3},{8,12},{9,13},{10,... | collective-permute-start | bytes 245768 | tf_op jit(solution)/shard_map/ppermute | solution.py:71
  120.3 0.9 collective-permute-start.33
  121.3 2.7 %collective-permute-start.34 = (f32[2,40,256]{2,1,0:T(8,128)S(1)}, f32[2,40,256]{2,1,0:T(8,128)S(1)}, u32[]{:S(2)}, u32[]{:S(2)}) collective-permute-start(f32[2,40,256]{2,1,0:T(8,128)S(1)} %get-tuple-element.59), channel_id=1, source_target_pairs={{0,6},{1,7},{2,0},{3,1},{4,2},{5,3},{6,4},{7,5},{8,14},{9,15},{10,... | collective-permute-start | bytes 245768 | tf_op jit(solution)/shard_map/ppermute | solution.py:71
  124.4 1.0 places.1.hot_ref
  125.4 0.9 collective-permute-done.32.refs_4_
  126.3 2.0 %collective-permute-done.33.refs_5_ = f32[2,40,256]{2,1,0:T(8,128)S(1)} collective-permute-done((f32[2,40,256]{2,1,0:T(8,128)S(1)}, f32[2,40,256]{2,1,0:T(8,128)S(1)}, u32[]{:S(2)}, u32[]{:S(2)}) %collective-permute-start.33) | collective-permute-done | bytes 81952 | tf_op jit(solution)/shard_map/ppermute | solution.py:71
  128.3 1.5 %collective-permute-done.35.refs_7_ = f32[2,40,256]{2,1,0:T(8,128)S(1)} collective-permute-done((f32[2,40,256]{2,1,0:T(8,128)S(1)}, f32[2,40,256]{2,1,0:T(8,128)S(1)}, u32[]{:S(2)}, u32[]{:S(2)}) %collective-permute-start.35) | collective-permute-done | bytes 81952 | tf_op jit(solution)/shard_map/ppermute | solution.py:71
  129.8 2.2 %final.1 = f32[256,512]{1,0:T(8,128)} custom-call(s32[3]{0:T(128)S(1)} %pad_add_fusion.where, bf16[2,256,320]{2,1,0:T(8,128)(2,1)S(1)} %places.1.hot_ref, f32[2,40,256]{2,1,0:T(8,128)S(1)} %get-tuple-element.53.refs_0_, f32[2,40,256]{2,1,0:T(8,128)S(1)} %collective-permute-done.29.refs_1_, f32[2,40,256]{2,1,0:T(8,128)S(1)} %collective-permute-done.30.refs_2_, ...), custom_call_target="tpu_custom_call" | custom-call | tf_op jit(solution)/shard_map/final/pallas_call | solution.py:380
  (67 shorter events, 6.4 us)
Async XLA Ops:
  0.0 69.4 %copy-start = (bf16[32,128,128]{2,1,0:T(8,128)(2,1)S(1)}, bf16[32,128,128]{2,1,0:T(8,128)(2,1)}, u32[]{:S(2)}) copy-start(bf16[32,128,128]{2,1,0:T(8,128)(2,1)} %refs_0_.1) | copy-start | bytes 3145732
  0.0 69.3 %copy-start.13 = (s32[4096,1]{0,1:T(1,128)S(1)}, s32[4096,1]{0,1:T(1,128)}, u32[]{:S(2)}) copy-start(s32[4096,1]{0,1:T(1,128)} %param.5) | copy-start | bytes 49156
  2.6 32.1 %collective-permute-start.16 = (bf16[2080,128]{1,0:T(8,128)(2,1)S(1)}, bf16[2080,128]{1,0:T(8,128)(2,1)S(1)}, u32[]{:S(2)}, u32[]{:S(2)}) collective-permute-start(bf16[2080,128]{1,0:T(8,128)(2,1)S(1)} %get-tuple-element.43), channel_id=1, source_target_pairs={{0,2},{1,3},{2,4},{3,5},{4,6},{5,7},{6,0},{7,1},{8,10},{9,11},{10,... | collective-permute-start | bytes 1597448 | tf_op jit(solution)/shard_map/ppermute | solution.py:71
  4.8 31.9 %collective-permute-start.14 = (bf16[2080,128]{1,0:T(8,128)(2,1)S(1)}, bf16[2080,128]{1,0:T(8,128)(2,1)S(1)}, u32[]{:S(2)}, u32[]{:S(2)}) collective-permute-start(bf16[2080,128]{1,0:T(8,128)(2,1)S(1)} %get-tuple-element.43), channel_id=1, source_target_pairs={{0,6},{1,7},{2,0},{3,1},{4,2},{5,3},{6,4},{7,5},{8,14},{9,15},{10,... | collective-permute-start | bytes 1597448 | tf_op jit(solution)/shard_map/ppermute | solution.py:71
  6.3 2.6 %collective-permute-start = (bf16[336,128]{1,0:T(8,128)(2,1)S(1)}, bf16[336,128]{1,0:T(8,128)(2,1)S(1)}, u32[]{:S(2)}, u32[]{:S(2)}) collective-permute-start(bf16[336,128]{1,0:T(8,128)(2,1)S(1)} %get-tuple-element.34), channel_id=1, source_target_pairs={{0,1},{1,0},{2,3},{3,2},{4,5},{5,4},{6,7},{7,6},{8,9},{9,8},{10,11... | collective-permute-start | bytes 258056 | tf_op jit(solution)/shard_map/ppermute | solution.py:71
  7.3 12.5 %collective-permute-start.1 = (bf16[336,128]{1,0:T(8,128)(2,1)S(1)}, bf16[336,128]{1,0:T(8,128)(2,1)S(1)}, u32[]{:S(2)}, u32[]{:S(2)}) collective-permute-start(bf16[336,128]{1,0:T(8,128)(2,1)S(1)} %get-tuple-element.35), channel_id=1, source_target_pairs={{0,2},{1,3},{2,4},{3,5},{4,6},{5,7},{6,0},{7,1},{8,10},{9,11},{10,... | collective-permute-start | bytes 258056 | tf_op jit(solution)/shard_map/ppermute | solution.py:71
  7.5 16.4 %collective-permute-start.2 = (bf16[336,128]{1,0:T(8,128)(2,1)S(1)}, bf16[336,128]{1,0:T(8,128)(2,1)S(1)}, u32[]{:S(2)}, u32[]{:S(2)}) collective-permute-start(bf16[336,128]{1,0:T(8,128)(2,1)S(1)} %get-tuple-element.36), channel_id=1, source_target_pairs={{0,3},{1,2},{2,5},{3,4},{4,7},{5,6},{6,1},{7,0},{8,11},{9,10},{10,... | collective-permute-start | bytes 258056 | tf_op jit(solution)/shard_map/ppermute | solution.py:71
  9.0 15.7 %collective-permute-start.3 = (bf16[336,128]{1,0:T(8,128)(2,1)S(1)}, bf16[336,128]{1,0:T(8,128)(2,1)S(1)}, u32[]{:S(2)}, u32[]{:S(2)}) collective-permute-start(bf16[336,128]{1,0:T(8,128)(2,1)S(1)} %get-tuple-element.37), channel_id=1, source_target_pairs={{0,4},{1,5},{2,6},{3,7},{4,0},{5,1},{6,2},{7,3},{8,12},{9,13},{10,... | collective-permute-start | bytes 258056 | tf_op jit(solution)/shard_map/ppermute | solution.py:71
  19.8 7.1 %collective-permute-start.4 = (bf16[336,128]{1,0:T(8,128)(2,1)S(1)}, bf16[336,128]{1,0:T(8,128)(2,1)S(1)}, u32[]{:S(2)}, u32[]{:S(2)}) collective-permute-start(bf16[336,128]{1,0:T(8,128)(2,1)S(1)} %get-tuple-element.38), channel_id=1, source_target_pairs={{0,5},{1,4},{2,7},{3,6},{4,1},{5,0},{6,3},{7,2},{8,13},{9,12},{10,... | collective-permute-start | bytes 258056 | tf_op jit(solution)/shard_map/ppermute | solution.py:71
  23.9 3.8 %collective-permute-start.5 = (bf16[336,128]{1,0:T(8,128)(2,1)S(1)}, bf16[336,128]{1,0:T(8,128)(2,1)S(1)}, u32[]{:S(2)}, u32[]{:S(2)}) collective-permute-start(bf16[336,128]{1,0:T(8,128)(2,1)S(1)} %get-tuple-element.39), channel_id=1, source_target_pairs={{0,6},{1,7},{2,0},{3,1},{4,2},{5,3},{6,4},{7,5},{8,14},{9,15},{10,... | collective-permute-start | bytes 258056 | tf_op jit(solution)/shard_map/ppermute | solution.py:71
  24.7 4.6 %collective-permute-start.6 = (bf16[336,128]{1,0:T(8,128)(2,1)S(1)}, bf16[336,128]{1,0:T(8,128)(2,1)S(1)}, u32[]{:S(2)}, u32[]{:S(2)}) collective-permute-start(bf16[336,128]{1,0:T(8,128)(2,1)S(1)} %get-tuple-element.40), channel_id=1, source_target_pairs={{0,7},{1,6},{2,1},{3,0},{4,3},{5,2},{6,5},{7,4},{8,15},{9,14},{10,... | collective-permute-start | bytes 258056 | tf_op jit(solution)/shard_map/ppermute | solution.py:71
  29.6 19.2 %collective-permute-start.9 = (bf16[40,8320]{1,0:T(8,128)(2,1)S(1)}, bf16[40,8320]{1,0:T(8,128)(2,1)}, u32[]{:S(2)}, u32[]{:S(2)}) collective-permute-start(bf16[40,8320]{1,0:T(8,128)(2,1)S(1)} %unit.1.refs_0_), channel_id=1, source_target_pairs={{0,104},{8,112},{16,120},{24,96},{32,8},{40,16},{48,24},{56,0},{64... | collective-permute-start | bytes 1996808 | tf_op jit(solution)/shard_map/ppermute | solution.py:63
  33.5 18.0 %collective-permute-start.7 = (bf16[40,8320]{1,0:T(8,128)(2,1)S(1)}, bf16[40,8320]{1,0:T(8,128)(2,1)}, u32[]{:S(2)}, u32[]{:S(2)}) collective-permute-start(bf16[40,8320]{1,0:T(8,128)(2,1)S(1)} %unit.1.refs_0_), channel_id=1, source_target_pairs={{0,32},{8,40},{16,48},{24,56},{32,64},{40,72},{48,80},{56,88},{64,... | collective-permute-start | bytes 1996808 | tf_op jit(solution)/shard_map/ppermute | solution.py:63
  33.5 19.5 %collective-permute-start.8 = (bf16[40,8320]{1,0:T(8,128)(2,1)S(1)}, bf16[40,8320]{1,0:T(8,128)(2,1)}, u32[]{:S(2)}, u32[]{:S(2)}) collective-permute-start(bf16[40,8320]{1,0:T(8,128)(2,1)S(1)} %unit.1.refs_0_), channel_id=1, source_target_pairs={{0,24},{8,0},{16,8},{24,16},{32,56},{40,32},{48,40},{56,48},{64,88... | collective-permute-start | bytes 1996808 | tf_op jit(solution)/shard_map/ppermute | solution.py:63
  34.8 14.1 %collective-permute-start.12 = (bf16[2080,128]{1,0:T(8,128)(2,1)S(1)}, bf16[2080,128]{1,0:T(8,128)(2,1)S(1)}, u32[]{:S(2)}, u32[]{:S(2)}) collective-permute-start(bf16[2080,128]{1,0:T(8,128)(2,1)S(1)} %get-tuple-element.43), channel_id=1, source_target_pairs={{0,4},{1,5},{2,6},{3,7},{4,0},{5,1},{6,2},{7,3},{8,12},{9,13},{10,... | collective-permute-start | bytes 1597448 | tf_op jit(solution)/shard_map/ppermute | solution.py:71
  36.7 17.1 %collective-permute-start.18 = (bf16[32,128,128]{2,1,0:T(8,128)(2,1)}, bf16[32,128,128]{2,1,0:T(8,128)(2,1)S(1)}, u32[]{:S(2)}, u32[]{:S(2)}) collective-permute-start(bf16[32,128,128]{2,1,0:T(8,128)(2,1)} %refs_0_.1), channel_id=1, source_target_pairs={{0,1},{1,0},{2,3},{3,2},{4,5},{5,4},{6,7},{7,6},{8,9},{9,8},{10,11... | collective-permute-start | bytes 3145736 | tf_op jit(solution)/shard_map/ppermute | solution.py:71
  48.8 16.5 %collective-permute-start.10 = (bf16[40,8320]{1,0:T(8,128)(2,1)}, bf16[40,8320]{1,0:T(8,128)(2,1)}, u32[]{:S(2)}, u32[]{:S(2)}) collective-permute-start(bf16[40,8320]{1,0:T(8,128)(2,1)} %collective-permute-done.9.refs_3_), channel_id=1, source_target_pairs={{0,8},{8,16},{16,24},{24,0},{32,40},{40,48},{48,56},{56,32},{64,72... | collective-permute-start | bytes 1996808 | tf_op jit(solution)/shard_map/ppermute | solution.py:63
  48.8 6.1 %collective-permute-start.17 = (bf16[2080,128]{1,0:T(8,128)(2,1)S(1)}, bf16[2080,128]{1,0:T(8,128)(2,1)S(1)}, u32[]{:S(2)}, u32[]{:S(2)}) collective-permute-start(bf16[2080,128]{1,0:T(8,128)(2,1)S(1)} %collective-permute-done.16.refs_0_), channel_id=1, source_target_pairs={{0,1},{1,0},{2,3},{3,2},{4,5},{5,4},{6,7},{7,6},{8,9},{9,8},{10,11... | collective-permute-start | bytes 1597448 | tf_op jit(solution)/shard_map/ppermute | solution.py:71
  51.6 6.8 %collective-permute-start.15 = (bf16[2080,128]{1,0:T(8,128)(2,1)S(1)}, bf16[2080,128]{1,0:T(8,128)(2,1)S(1)}, u32[]{:S(2)}, u32[]{:S(2)}) collective-permute-start(bf16[2080,128]{1,0:T(8,128)(2,1)S(1)} %collective-permute-done.14.refs_0_), channel_id=1, source_target_pairs={{0,1},{1,0},{2,3},{3,2},{4,5},{5,4},{6,7},{7,6},{8,9},{9,8},{10,11... | collective-permute-start | bytes 1597448 | tf_op jit(solution)/shard_map/ppermute | solution.py:71
  52.2 0.8 copy-start.3
  53.0 6.2 %collective-permute-start.13 = (bf16[2080,128]{1,0:T(8,128)(2,1)S(1)}, bf16[2080,128]{1,0:T(8,128)(2,1)S(1)}, u32[]{:S(2)}, u32[]{:S(2)}) collective-permute-start(bf16[2080,128]{1,0:T(8,128)(2,1)S(1)} %collective-permute-done.12.refs_0_), channel_id=1, source_target_pairs={{0,1},{1,0},{2,3},{3,2},{4,5},{5,4},{6,7},{7,6},{8,9},{9,8},{10,11... | collective-permute-start | bytes 1597448 | tf_op jit(solution)/shard_map/ppermute | solution.py:71
  53.9 35.6 %collective-permute-start.19 = (bf16[40,8320]{1,0:T(8,128)(2,1)}, bf16[40,8320]{1,0:T(8,128)(2,1)}, u32[]{:S(2)}, u32[]{:S(2)}) collective-permute-start(bf16[40,8320]{1,0:T(8,128)(2,1)} %collective-permute-done.7.refs_1_), channel_id=1, source_target_pairs={{0,32},{8,40},{16,48},{24,56},{32,64},{40,72},{48,80},{56,88},{64,... | collective-permute-start | bytes 1996808 | tf_op jit(solution)/shard_map/ppermute | solution.py:63
  54.9 0.8 copy-start.7
  55.8 33.6 %collective-permute-start.20 = (bf16[40,8320]{1,0:T(8,128)(2,1)}, bf16[40,8320]{1,0:T(8,128)(2,1)}, u32[]{:S(2)}, u32[]{:S(2)}) collective-permute-start(bf16[40,8320]{1,0:T(8,128)(2,1)} %collective-permute-done.8.refs_2_), channel_id=1, source_target_pairs={{0,24},{8,0},{16,8},{24,16},{32,56},{40,32},{48,40},{56,48},{64,88... | collective-permute-start | bytes 1996808 | tf_op jit(solution)/shard_map/ppermute | solution.py:63
  58.4 0.8 copy-start.9
  59.2 30.2 %collective-permute-start.21 = (bf16[40,8320]{1,0:T(8,128)(2,1)}, bf16[40,8320]{1,0:T(8,128)(2,1)}, u32[]{:S(2)}, u32[]{:S(2)}) collective-permute-start(bf16[40,8320]{1,0:T(8,128)(2,1)} %collective-permute-done.7.refs_1_), channel_id=1, source_target_pairs={{0,8},{8,16},{16,24},{24,0},{32,40},{40,48},{48,56},{56,32},{64,72... | collective-permute-start | bytes 1996808 | tf_op jit(solution)/shard_map/ppermute | solution.py:63
  59.2 0.8 copy-start.11
  60.1 33.5 %collective-permute-start.11 = (bf16[40,8320]{1,0:T(8,128)(2,1)}, bf16[40,8320]{1,0:T(8,128)(2,1)}, u32[]{:S(2)}, u32[]{:S(2)}) collective-permute-start(bf16[40,8320]{1,0:T(8,128)(2,1)} %collective-permute-done.9.refs_3_), channel_id=1, source_target_pairs={{0,96},{8,104},{16,112},{24,120},{32,0},{40,8},{48,16},{56,24},{64... | collective-permute-start | bytes 1996808 | tf_op jit(solution)/shard_map/ppermute | solution.py:63
  65.3 35.9 %collective-permute-start.22 = (bf16[40,8320]{1,0:T(8,128)(2,1)}, bf16[40,8320]{1,0:T(8,128)(2,1)S(1)}, u32[]{:S(2)}, u32[]{:S(2)}) collective-permute-start(bf16[40,8320]{1,0:T(8,128)(2,1)} %collective-permute-done.10.refs_4_), channel_id=1, source_target_pairs={{0,96},{8,104},{16,112},{24,120},{32,0},{40,8},{48,16},{56,24},{64... | collective-permute-start | bytes 1996808 | tf_op jit(solution)/shard_map/ppermute | solution.py:63
  69.4 3.3 %copy-start.2 = (bf16[2080,128]{1,0:T(8,128)(2,1)S(1)}, bf16[2080,128]{1,0:T(8,128)(2,1)}, u32[]{:S(2)}) copy-start(bf16[2080,128]{1,0:T(8,128)(2,1)} %copy-done.1) | copy-start | bytes 1597444
  69.4 3.3 %copy-start.8 = (bf16[2080,128]{1,0:T(8,128)(2,1)S(1)}, bf16[2080,128]{1,0:T(8,128)(2,1)}, u32[]{:S(2)}) copy-start(bf16[2080,128]{1,0:T(8,128)(2,1)} %copy-done.7) | copy-start | bytes 1597444
  72.7 5.5 %copy-start.4 = (bf16[2080,128]{1,0:T(8,128)(2,1)S(1)}, bf16[2080,128]{1,0:T(8,128)(2,1)}, u32[]{:S(2)}) copy-start(bf16[2080,128]{1,0:T(8,128)(2,1)} %copy-done.3) | copy-start | bytes 1597444
  72.7 5.5 %copy-start.10 = (bf16[2080,128]{1,0:T(8,128)(2,1)S(1)}, bf16[2080,128]{1,0:T(8,128)(2,1)}, u32[]{:S(2)}) copy-start(bf16[2080,128]{1,0:T(8,128)(2,1)} %copy-done.9) | copy-start | bytes 1597444
  78.2 5.5 %copy-start.6 = (bf16[2080,128]{1,0:T(8,128)(2,1)S(1)}, bf16[2080,128]{1,0:T(8,128)(2,1)}, u32[]{:S(2)}) copy-start(bf16[2080,128]{1,0:T(8,128)(2,1)} %copy-done.5) | copy-start | bytes 1597444
  78.2 5.5 %copy-start.12 = (bf16[2080,128]{1,0:T(8,128)(2,1)S(1)}, bf16[2080,128]{1,0:T(8,128)(2,1)}, u32[]{:S(2)}) copy-start(bf16[2080,128]{1,0:T(8,128)(2,1)} %copy-done.11) | copy-start | bytes 1597444
  92.5 8.3 %collective-permute-start.28 = (f32[40,256]{1,0:T(8,128)S(1)}, f32[40,256]{1,0:T(8,128)S(1)}, u32[]{:S(2)}, u32[]{:S(2)}) collective-permute-start(f32[40,256]{1,0:T(8,128)S(1)} %get-tuple-element.52.refs_8_), channel_id=1, source_target_pairs={{0,120},{8,96},{16,104},{24,112},{32,24},{40,0},{48,8},{56,16},{64... | collective-permute-start | bytes 122888 | tf_op jit(solution)/shard_map/ppermute | solution.py:63
  96.8 9.7 %collective-permute-start.23 = (f32[40,256]{1,0:T(8,128)S(1)}, f32[40,256]{1,0:T(8,128)S(1)}, u32[]{:S(2)}, u32[]{:S(2)}) collective-permute-start(f32[40,256]{1,0:T(8,128)S(1)} %get-tuple-element.45.refs_1_), channel_id=1, source_target_pairs={{0,96},{8,104},{16,112},{24,120},{32,0},{40,8},{48,16},{56,24},{64... | collective-permute-start | bytes 122888 | tf_op jit(solution)/shard_map/ppermute | solution.py:63
  96.9 9.7 %collective-permute-start.24 = (f32[40,256]{1,0:T(8,128)S(1)}, f32[40,256]{1,0:T(8,128)S(1)}, u32[]{:S(2)}, u32[]{:S(2)}) collective-permute-start(f32[40,256]{1,0:T(8,128)S(1)} %get-tuple-element.46.refs_2_), channel_id=1, source_target_pairs={{0,8},{8,16},{16,24},{24,0},{32,40},{40,48},{48,56},{56,32},{64,72... | collective-permute-start | bytes 122888 | tf_op jit(solution)/shard_map/ppermute | solution.py:63
  98.3 8.3 %collective-permute-start.25 = (f32[40,256]{1,0:T(8,128)S(1)}, f32[40,256]{1,0:T(8,128)S(1)}, u32[]{:S(2)}, u32[]{:S(2)}) collective-permute-start(f32[40,256]{1,0:T(8,128)S(1)} %get-tuple-element.47.refs_3_), channel_id=1, source_target_pairs={{0,56},{8,32},{16,40},{24,48},{32,88},{40,64},{48,72},{56,80},{64,... | collective-permute-start | bytes 122888 | tf_op jit(solution)/shard_map/ppermute | solution.py:63
  100.8 6.9 %collective-permute-start.26 = (f32[40,256]{1,0:T(8,128)S(1)}, f32[40,256]{1,0:T(8,128)S(1)}, u32[]{:S(2)}, u32[]{:S(2)}) collective-permute-start(f32[40,256]{1,0:T(8,128)S(1)} %get-tuple-element.48.refs_4_), channel_id=1, source_target_pairs={{0,48},{8,56},{16,32},{24,40},{32,80},{40,88},{48,64},{56,72},{64,... | collective-permute-start | bytes 122888 | tf_op jit(solution)/shard_map/ppermute | solution.py:63
  101.2 6.5 %collective-permute-start.27 = (f32[40,256]{1,0:T(8,128)S(1)}, f32[40,256]{1,0:T(8,128)S(1)}, u32[]{:S(2)}, u32[]{:S(2)}) collective-permute-start(f32[40,256]{1,0:T(8,128)S(1)} %get-tuple-element.49.refs_5_), channel_id=1, source_target_pairs={{0,88},{8,64},{16,72},{24,80},{32,120},{40,96},{48,104},{56,112},{... | collective-permute-start | bytes 122888 | tf_op jit(solution)/shard_map/ppermute | solution.py:63
  108.4 12.9 %collective-permute-start.29 = (f32[2,40,256]{2,1,0:T(8,128)S(1)}, f32[2,40,256]{2,1,0:T(8,128)S(1)}, u32[]{:S(2)}, u32[]{:S(2)}) collective-permute-start(f32[2,40,256]{2,1,0:T(8,128)S(1)} %get-tuple-element.54), channel_id=1, source_target_pairs={{0,1},{1,0},{2,3},{3,2},{4,5},{5,4},{6,7},{7,6},{8,9},{9,8},{10,11... | collective-permute-start | bytes 245768 | tf_op jit(solution)/shard_map/ppermute | solution.py:71
  115.8 8.2 %collective-permute-start.30 = (f32[2,40,256]{2,1,0:T(8,128)S(1)}, f32[2,40,256]{2,1,0:T(8,128)S(1)}, u32[]{:S(2)}, u32[]{:S(2)}) collective-permute-start(f32[2,40,256]{2,1,0:T(8,128)S(1)} %get-tuple-element.55), channel_id=1, source_target_pairs={{0,2},{1,3},{2,4},{3,5},{4,6},{5,7},{6,0},{7,1},{8,10},{9,11},{10,... | collective-permute-start | bytes 245768 | tf_op jit(solution)/shard_map/ppermute | solution.py:71
  117.7 7.6 %collective-permute-start.31 = (f32[2,40,256]{2,1,0:T(8,128)S(1)}, f32[2,40,256]{2,1,0:T(8,128)S(1)}, u32[]{:S(2)}, u32[]{:S(2)}) collective-permute-start(f32[2,40,256]{2,1,0:T(8,128)S(1)} %get-tuple-element.56), channel_id=1, source_target_pairs={{0,3},{1,2},{2,5},{3,4},{4,7},{5,6},{6,1},{7,0},{8,11},{9,10},{10,... | collective-permute-start | bytes 245768 | tf_op jit(solution)/shard_map/ppermute | solution.py:71
  117.8 8.5 %collective-permute-start.32 = (f32[2,40,256]{2,1,0:T(8,128)S(1)}, f32[2,40,256]{2,1,0:T(8,128)S(1)}, u32[]{:S(2)}, u32[]{:S(2)}) collective-permute-start(f32[2,40,256]{2,1,0:T(8,128)S(1)} %get-tuple-element.57), channel_id=1, source_target_pairs={{0,4},{1,5},{2,6},{3,7},{4,0},{5,1},{6,2},{7,3},{8,12},{9,13},{10,... | collective-permute-start | bytes 245768 | tf_op jit(solution)/shard_map/ppermute | solution.py:71
  120.3 7.9 %collective-permute-start.33 = (f32[2,40,256]{2,1,0:T(8,128)S(1)}, f32[2,40,256]{2,1,0:T(8,128)S(1)}, u32[]{:S(2)}, u32[]{:S(2)}) collective-permute-start(f32[2,40,256]{2,1,0:T(8,128)S(1)} %get-tuple-element.58), channel_id=1, source_target_pairs={{0,5},{1,4},{2,7},{3,6},{4,1},{5,0},{6,3},{7,2},{8,13},{9,12},{10,... | collective-permute-start | bytes 245768 | tf_op jit(solution)/shard_map/ppermute | solution.py:71
  121.3 7.0 %collective-permute-start.34 = (f32[2,40,256]{2,1,0:T(8,128)S(1)}, f32[2,40,256]{2,1,0:T(8,128)S(1)}, u32[]{:S(2)}, u32[]{:S(2)}) collective-permute-start(f32[2,40,256]{2,1,0:T(8,128)S(1)} %get-tuple-element.59), channel_id=1, source_target_pairs={{0,6},{1,7},{2,0},{3,1},{4,2},{5,3},{6,4},{7,5},{8,14},{9,15},{10,... | collective-permute-start | bytes 245768 | tf_op jit(solution)/shard_map/ppermute | solution.py:71
  124.0 5.8 %collective-permute-start.35 = (f32[2,40,256]{2,1,0:T(8,128)S(1)}, f32[2,40,256]{2,1,0:T(8,128)S(1)}, u32[]{:S(2)}, u32[]{:S(2)}) collective-permute-start(f32[2,40,256]{2,1,0:T(8,128)S(1)} %get-tuple-element.60), channel_id=1, source_target_pairs={{0,7},{1,6},{2,1},{3,0},{4,3},{5,2},{6,5},{7,4},{8,15},{9,14},{10,... | collective-permute-start | bytes 245768 | tf_op jit(solution)/shard_map/ppermute | solution.py:71
  (2 other events, 1.6 us)
